TPU v7x, 8 devices: a whole 2x2x1 slice. The times are simulated.
8 devices in a mesh: dp: 1 (over z), ty: 2 (over y), tx: 4 (over x, core).
Axes of the slice: x: 2, y: 2, z: 1, core: 2. Of those that a mesh axis runs over, the one named last changes fastest.
Arguments:
- x_in: bfloat16 [1, 256, 2048], P('dp', None, 'tx')
- positions: int32 [1, 256], P('dp')
- d_y: bfloat16 [1, 256, 2048], P('dp', None, 'tx')
- ln_gamma: float32 [2048], P('tx')
- w_q: bfloat16 [2048, 2048], P('tx', 'ty')
- w_g: bfloat16 [2048, 8192], P('tx', 'ty')
- w_u: bfloat16 [2048, 8192], P('tx', 'ty')
- w_k: bfloat16 [2048, 256], P('tx')
- w_v: bfloat16 [2048, 256], P('tx')
- w_o: bfloat16 [2048, 2048], P('ty', 'tx')
- w_d: bfloat16 [8192, 2048], P('ty', 'tx')
Outputs:
- output 1: bfloat16 [1, 256, 2048], P('dp', None, 'tx')
- output 2: bfloat16 [1, 256, 2048], P('dp', None, 'tx')
- output 3: float32 [2048], P(('dp', 'tx'))
- output 4: float32 [2048, 2048], P(('dp', 'tx'), 'ty')
- output 5: float32 [2048, 8192], P(('dp', 'tx'), 'ty')
- output 6: float32 [2048, 8192], P(('dp', 'tx'), 'ty')
- output 7: float32 [2048, 256], P(('dp', 'tx'))
- output 8: float32 [2048, 256], P(('dp', 'tx'))
- output 9: float32 [2048, 2048], P(('dp', 'ty'), 'tx')
- output 10: float32 [8192, 2048], P(('dp', 'ty'), 'tx')
All inputs are finite; a program needn't handle non-finite values.
Results may differ from a plain program's by a relative error of at most 0.02.
Values are sent between devices in bfloat16 or wider.
A program may use at most 1 GiB of HBM per device.

v0:
```python
import jax
import jax.numpy as jnp
from jax import lax
from jax.sharding import PartitionSpec as P

EPS = 1e-6
ROPE_BASE = 10000.0


def rope_tables(positions, head_dim):
    half_dim = head_dim // 2
    inv_freq = ROPE_BASE ** (-2.0 * jnp.arange(half_dim, dtype=jnp.float32) / head_dim)
    angles = positions.astype(jnp.float32)[:, None] * inv_freq[None, :]
    return jnp.cos(angles), jnp.sin(angles)


def apply_rope(values, cos_t, sin_t):
    half_dim = values.shape[-1] // 2
    first = values[..., :half_dim]
    second = values[..., half_dim:]
    return jnp.concatenate([first * cos_t - second * sin_t, second * cos_t + first * sin_t], axis=-1)


def rope_grad(grad_out, cos_t, sin_t):
    half_dim = grad_out.shape[-1] // 2
    first = grad_out[..., :half_dim]
    second = grad_out[..., half_dim:]
    return jnp.concatenate([first * cos_t + second * sin_t, second * cos_t - first * sin_t], axis=-1)


def attend(q_rot, k_rot, v_val):
    seq_len = k_rot.shape[1]
    score_scale = k_rot.shape[2] ** -0.5
    scores = jnp.einsum('bihe,bje->bihj', q_rot, k_rot, preferred_element_type=jnp.float32) * score_scale
    seq_idx = jnp.arange(seq_len)
    causal = seq_idx[:, None, None] >= seq_idx[None, None, :]
    prob_mat = jax.nn.softmax(jnp.where(causal, scores, -1e30), axis=-1).astype(jnp.bfloat16)
    return jnp.einsum('bihj,bje->bihe', prob_mat, v_val, preferred_element_type=jnp.float32).astype(jnp.bfloat16)


def solution(mesh):
    tx_size = mesh.shape['tx']
    tok_spec = P('dp', None, 'tx')
    in_specs = (tok_spec, P('dp', None), tok_spec, P('tx'), P('tx', 'ty'), P('tx', 'ty'), P('tx', 'ty'),
                P('tx', None), P('tx', None), P('ty', 'tx'), P('ty', 'tx'))
    out_specs = (tok_spec, tok_spec, P(('dp', 'tx')), P(('dp', 'tx'), 'ty'), P(('dp', 'tx'), 'ty'), P(('dp', 'tx'), 'ty'),
                 P(('dp', 'tx'), None), P(('dp', 'tx'), None), P(('dp', 'ty'), 'tx'), P(('dp', 'ty'), 'tx'))

    def local_layer(x_in, positions, d_y, ln_gamma, w_q, w_g, w_u, w_k, w_v, w_o, w_d):
        n_seqs, seq_len, d_local = x_in.shape
        n_tok = n_seqs * seq_len
        d_model = d_local * tx_size
        head_dim = w_k.shape[1]
        heads_local = w_q.shape[1] // head_dim
        x_f = x_in.reshape(n_tok, d_local).astype(jnp.float32)
        tok_stats = lax.psum(jnp.stack([jnp.sum(x_f, axis=1), jnp.sum(x_f * x_f, axis=1)], axis=1), 'tx')
        tok_mean = tok_stats[:, 0:1] / d_model
        tok_var = tok_stats[:, 1:2] / d_model - tok_mean * tok_mean
        inv_std = lax.rsqrt(tok_var + EPS)
        x_hat = (x_f - tok_mean) * inv_std
        normed = (x_hat * ln_gamma).astype(jnp.bfloat16)
        partials = tuple(jnp.dot(normed, weight, preferred_element_type=jnp.float32).astype(jnp.bfloat16) for weight in (w_q, w_g, w_u, w_k, w_v))
        q_lin, gate_proj, up_proj, k_lin, v_val = lax.psum(partials, 'tx')
        cos_t, sin_t = rope_tables(positions.reshape(n_tok), head_dim)
        q_rot = apply_rope(q_lin.astype(jnp.float32).reshape(n_tok, heads_local, head_dim), cos_t[:, None, :], sin_t[:, None, :]).astype(jnp.bfloat16)
        k_rot = apply_rope(k_lin.astype(jnp.float32), cos_t, sin_t).astype(jnp.bfloat16)
        attn_out, attn_pullback = jax.vjp(attend, q_rot.reshape(n_seqs, seq_len, heads_local, head_dim), k_rot.reshape(n_seqs, seq_len, head_dim), v_val.reshape(n_seqs, seq_len, head_dim))
        attn_flat = attn_out.reshape(n_tok, heads_local * head_dim)
        gate_f = gate_proj.astype(jnp.float32)
        up_f = up_proj.astype(jnp.float32)
        sig_gate = jax.nn.sigmoid(gate_f)
        silu_gate = gate_f * sig_gate
        hidden_act = (silu_gate * up_f).astype(jnp.bfloat16)
        branch_part = jnp.dot(attn_flat, w_o, preferred_element_type=jnp.float32) + jnp.dot(hidden_act, w_d, preferred_element_type=jnp.float32)
        branch = lax.psum(branch_part.astype(jnp.bfloat16), 'ty')
        y_out = (x_f + branch.astype(jnp.float32)).astype(jnp.bfloat16)
        dy_flat = d_y.reshape(n_tok, d_local)
        d_attn_part = jnp.einsum('td,hd->th', dy_flat, w_o, preferred_element_type=jnp.float32).astype(jnp.bfloat16)
        d_act_part = jnp.einsum('td,fd->tf', dy_flat, w_d, preferred_element_type=jnp.float32).astype(jnp.bfloat16)
        d_attn, d_act = lax.psum((d_attn_part, d_act_part), 'tx')
        d_wo = jnp.einsum('th,td->hd', attn_flat, dy_flat, preferred_element_type=jnp.float32)
        d_wd = jnp.einsum('tf,td->fd', hidden_act, dy_flat, preferred_element_type=jnp.float32)
        d_act_f = d_act.astype(jnp.float32)
        d_up = (d_act_f * silu_gate).astype(jnp.bfloat16)
        d_gate = (d_act_f * up_f * sig_gate * (1.0 + gate_f * (1.0 - sig_gate))).astype(jnp.bfloat16)
        d_qrot, d_krot_part, d_v_part = attn_pullback(d_attn.reshape(n_seqs, seq_len, heads_local, head_dim))
        d_krot, d_v = lax.psum((d_krot_part.reshape(n_tok, head_dim), d_v_part.reshape(n_tok, head_dim)), 'ty')
        d_q = rope_grad(d_qrot.astype(jnp.float32).reshape(n_tok, heads_local, head_dim), cos_t[:, None, :], sin_t[:, None, :]).astype(jnp.bfloat16).reshape(n_tok, heads_local * head_dim)
        d_k = rope_grad(d_krot.astype(jnp.float32), cos_t, sin_t).astype(jnp.bfloat16)
        d_wq, d_wg, d_wu, d_wk, d_wv = (jnp.einsum('td,tc->dc', normed, grad_col, preferred_element_type=jnp.float32) for grad_col in (d_q, d_gate, d_up, d_k, d_v))
        dh_part = (jnp.einsum('tc,dc->td', d_q, w_q, preferred_element_type=jnp.float32)
                   + jnp.einsum('tc,dc->td', d_gate, w_g, preferred_element_type=jnp.float32)
                   + jnp.einsum('tc,dc->td', d_up, w_u, preferred_element_type=jnp.float32))
        d_normed = (lax.psum(dh_part.astype(jnp.bfloat16), 'ty').astype(jnp.float32)
                    + jnp.einsum('tc,dc->td', d_k, w_k, preferred_element_type=jnp.float32)
                    + jnp.einsum('tc,dc->td', d_v, w_v, preferred_element_type=jnp.float32))
        value_a6 = d_normed * ln_gamma
        d_gamma = jnp.sum(d_normed * x_hat, axis=0)
        back_stats = lax.psum(jnp.stack([jnp.sum(value_a6, axis=1), jnp.sum(value_a6 * x_hat, axis=1)], axis=1), 'tx')
        d_x = dy_flat.astype(jnp.float32) + inv_std * (value_a6 - back_stats[:, 0:1] / d_model - x_hat * back_stats[:, 1:2] / d_model)
        return (y_out.reshape(x_in.shape), d_x.astype(jnp.bfloat16).reshape(x_in.shape), d_gamma,
                d_wq, d_wg, d_wu, d_wk, d_wv, d_wo, d_wd)

    return jax.shard_map(local_layer, mesh=mesh, in_specs=in_specs, out_specs=out_specs, check_vma=False)
```

profile of v0, /device:TPU:0, one launch (start us, length us, event | category | flops | bytes accessed | tf_op | source)
XLA Modules:
  0.0 261.4 jit_solution(1098948466531557531)
XLA Ops:
  9.5 8.8 %psum.91 = f32[256,2]{0,1:T(2,128)S(1)} all-reduce(f32[256,2]{0,1:T(2,128)S(1)} %pad_maximum_fusion.10), channel_id=1, replica_groups=mesh['dp'=1,'ty'=2,'tx'=4] {'tx'}, use_global_device_ids=true, to_apply=%region_2.0 | all-reduce | flops 512 | bytes 4096 | tf_op jit(solution)/shard_map/psum | solution.py:56
  18.2 1.5 convolution_convert_fusion.7
  19.8 5.1 %convolution_convert_fusion.2 = bf16[256,4096]{1,0:T(8,128)(2,1)} fusion(bf16[512,4096]{1,0:T(8,128)(2,1)} %param.16, bf16[1,256,512]{2,1,0:T(8,128)(2,1)} %param.11, f32[512]{0:T(512)} %param.14, f32[256]{0:T(256)S(1)} %bitcast.169, f32[256]{0:T(256)S(1)} %bitcast.157), kind=kOutput, calls=%fused_computation.9 | convolution fusion | flops 1075445760 | bytes 6557696 | tf_op jit(solution)/shard_map/dot_general | solution.py:62
  24.9 2.7 %convolution_convert_fusion.1 = bf16[256,4096]{1,0:T(8,128)(2,1)} fusion(bf16[512,4096]{1,0:T(8,128)(2,1)S(1)} %copy-done.35, bf16[1,256,512]{2,1,0:T(8,128)(2,1)S(1)} %copy-done.1, f32[512]{0:T(512)S(1)} %copy-done.19, f32[256]{0:T(256)S(1)} %bitcast.170, f32[256]{0:T(256)S(1)} %bitcast.158), kind=kOutput, calls=%fused_computation.8 | convolution fusion | flops 1075445760 | bytes 6557696 | tf_op jit(solution)/shard_map/dot_general | solution.py:62
  29.9 2.6 convolution_convert_fusion
  35.4 133.6 %all-reduce.5.cloned.1.call-done = (bf16[256,4096]{1,0:T(8,128)(2,1)}, bf16[256,4096]{1,0:T(8,128)(2,1)}, bf16[256,256]{1,0:T(8,128)(2,1)}, bf16[256,4,256]{2,0,...) async-done(((bf16[256,4096]{1,0:T(8,128)(2,1)}, bf16[256,4096]{1,0:T(8,128)(2,1)}, bf16[256,256]{1,0:T(8,128)(2,1)}, ...) | async-done | bytes 7602192 | tf_op jit(solution)/shard_map/psum | solution.py:63
  173.2 1.6 fusion.105
  175.9 1.3 fusion.25
  177.3 2.1 fusion.17
  182.4 2.9 %fusion.4 = (bf16[256,4096]{1,0:T(8,128)(2,1)S(1)}, bf16[256,4096]{1,0:T(8,128)(2,1)S(1)}, bf16[256,4096]{1,0:T(8,128)(2,1)S(1)}) fusion(bf16[256,4096]{1,0:T(8,128)(2,1)S(1)} %copy-done.10, bf16[256,4096]{1,0:T(8,128)(2,1)S(1)} %copy-done.12, bf16[256,4096]{1,0:T(8,128)(2,1)S(1)} %copy-done.11), kind=kLoop, calls=%fused_computation.13 | loop fusion | flops 18874368 | bytes 12582912 | tf_op jit(solution)/shard_map/convert_element_type | solution.py:85
  185.4 2.1 fusion.108
  187.4 4.8 %fusion.96 = f32[512,4096]{1,0:T(8,128)} fusion(bf16[256,4096]{1,0:T(8,128)(2,1)S(1)} %get-tuple-element.25, bf16[1,256,512]{2,1,0:T(8,128)(2,1)S(1)} %copy-done.1, f32[512]{0:T(512)S(1)} %copy-done.19, f32[256]{0:T(256)S(1)} %bitcast.173, f32[256]{0:T(256)S(1)} %bitcast.161), kind=kOutput, calls=%fused_computation.141 | convolution fusion | flops 1074397184 | bytes 10752000 | tf_op jit(solution)/shard_map/td,tc->dc/dot_general | solution.py:90
  192.3 2.0 fusion.106
  194.3 4.7 %fusion.51 = f32[4096,512]{1,0:T(8,128)} fusion(bf16[256,4096]{1,0:T(8,128)(2,1)S(1)} %get-tuple-element.26, bf16[1,256,512]{2,1,0:T(8,128)(2,1)S(1)} %copy-done.3), kind=kOutput, calls=%fused_computation.88 | convolution fusion | flops 1073741824 | bytes 10747904 | tf_op jit(solution)/shard_map/tf,td->fd/dot_general | solution.py:82
  200.0 2.0 copy.37
  202.1 3.6 %fusion.107 = f32[256,512]{1,0:T(8,128)S(1)} fusion(bf16[256,4096]{1,0:T(8,128)(2,1)S(1)} %get-tuple-element.24, bf16[512,4096]{1,0:T(8,128)(2,1)} %param.16), kind=kOutput, calls=%fused_computation.145 | convolution fusion | flops 1073741824 | bytes 6815744 | tf_op jit(solution)/shard_map/tc,dc->td/dot_general | solution.py:92
  205.7 1.9 fusion.48
  210.0 2.9 %fusion.53 = f32[1024,512]{1,0:T(8,128)} fusion(bf16[256,1024]{0,1:T(8,128)(2,1)} %bitcast.153, bf16[1,256,512]{2,1,0:T(8,128)(2,1)} %param.13), kind=kOutput, calls=%fused_computation.90 | convolution fusion | flops 268435456 | bytes 2883584 | tf_op jit(solution)/shard_map/th,td->hd/dot_general | solution.py:81
  212.9 4.8 %fusion.98 = f32[512,4096]{1,0:T(8,128)} fusion(bf16[256,4096]{1,0:T(8,128)(2,1)S(1)} %get-tuple-element.24, bf16[1,256,512]{2,1,0:T(8,128)(2,1)S(1)} %copy-done.1, f32[512]{0:T(512)S(1)} %copy-done.19, f32[256]{0:T(256)S(1)} %bitcast.175, f32[256]{0:T(256)S(1)} %bitcast.163), kind=kOutput, calls=%fused_computation.142 | convolution fusion | flops 1074397184 | bytes 10752000 | tf_op jit(solution)/shard_map/td,tc->dc/dot_general | solution.py:90
  217.7 21.3 %all-reduce.7.cloned.1.call-done = (bf16[256,512]{1,0:T(8,128)(2,1)}, bf16[256,512]{1,0:T(8,128)(2,1)}, bf16[256,256]{1,0:T(8,128)(2,1)}, bf16[256,256]{0,1:T(8,128)(2,1)}) async-done(((bf16[256,512]{1,0:T(8,128)(2,1)}, bf16[256,512]{1,0:T(8,128)(2,1)}, bf16[256,256]{1,0:T(8,128)(2,1)}, bf16[256,256]{0,1:T(8,128)(2,1)}), (bf16[256,512]{1,0:T(8,128)(2,1)}, bf16[256,512]{1,0:T(8,128)(2,1)}, ...) | async-done | bytes 786448 | tf_op jit(solution)/shard_map/psum | solution.py:75
  241.8 1.3 convolution_add_fusion.3
  243.1 2.1 fusion.93
  245.2 2.1 fusion.42
  247.2 6.3 %psum.103 = f32[256,2]{0,1:T(2,128)S(1)} all-reduce(f32[256,2]{0,1:T(2,128)S(1)} %pad_maximum_fusion.11), channel_id=1, replica_groups=mesh['dp'=1,'ty'=2,'tx'=4] {'tx'}, use_global_device_ids=true, to_apply=%region_19.20 | all-reduce | flops 512 | bytes 4096 | tf_op jit(solution)/shard_map/psum | solution.py:99
  (108 shorter events, 23.1 us)
Async XLA Ops:
  7.2 11.1 %copy-start = (bf16[512,1024]{1,0:T(8,128)(2,1)S(1)}, bf16[512,1024]{1,0:T(8,128)(2,1)}, u32[]{:S(2)}) copy-start(bf16[512,1024]{1,0:T(8,128)(2,1)} %param.15) | copy-start | bytes 3145732
  7.2 161.8 %all-reduce.5.cloned.1.call-start = ((), (), s32[]{:S(2)}) async-start(), calls=%async_computation | async-start | bytes 15204352 | tf_op jit(solution)/shard_map/psum | solution.py:63
  19.7 5.1 %copy-start.1 = (bf16[1,256,512]{2,1,0:T(8,128)(2,1)S(1)}, bf16[1,256,512]{2,1,0:T(8,128)(2,1)}, u32[]{:S(2)}) copy-start(bf16[1,256,512]{2,1,0:T(8,128)(2,1)} %param.11) | copy-start | bytes 786436
  19.7 5.1 %copy-start.19 = (f32[512]{0:T(512)S(1)}, f32[512]{0:T(512)}, u32[]{:S(2)}) copy-start(f32[512]{0:T(512)} %param.14) | copy-start | bytes 6148
  19.7 5.1 %copy-start.35 = (bf16[512,4096]{1,0:T(8,128)(2,1)S(1)}, bf16[512,4096]{1,0:T(8,128)(2,1)}, u32[]{:S(2)}) copy-start(bf16[512,4096]{1,0:T(8,128)(2,1)} %param.17) | copy-start | bytes 12582916
  24.8 3.7 %copy-start.22 = (bf16[512,256]{1,0:T(8,128)(2,1)S(1)}, bf16[512,256]{1,0:T(8,128)(2,1)}, u32[]{:S(2)}) copy-start(bf16[512,256]{1,0:T(8,128)(2,1)} %param.18) | copy-start | bytes 786436
  24.9 4.6 %copy-start.2 = (bf16[1,256,512]{2,1,0:T(8,128)(2,1)S(1)}, bf16[1,256,512]{2,1,0:T(8,128)(2,1)}, u32[]{:S(2)}) copy-start(bf16[1,256,512]{2,1,0:T(8,128)(2,1)} %param.13) | copy-start | bytes 786436
  24.9 4.6 %copy-start.6 = (bf16[1024,512]{1,0:T(8,128)(2,1)S(1)}, bf16[1024,512]{1,0:T(8,128)(2,1)}, u32[]{:S(2)}) copy-start(bf16[1024,512]{1,0:T(8,128)(2,1)} %param.20) | copy-start | bytes 3145732
  24.9 5.1 %copy-start.8 = (bf16[4096,512]{1,0:T(8,128)(2,1)S(1)}, bf16[4096,512]{1,0:T(8,128)(2,1)}, u32[]{:S(2)}) copy-start(bf16[4096,512]{1,0:T(8,128)(2,1)} %param.21) | copy-start | bytes 12582916
  33.6 205.4 %all-reduce.7.cloned.1.call-start = ((), (), s32[]{:S(2)}) async-start(), calls=%async_computation.1 | async-start | bytes 1572864 | tf_op jit(solution)/shard_map/psum | solution.py:75
  169.0 5.9 %copy-start.16 = (bf16[256,4,256]{2,0,1:T(8,128)(2,1)S(1)}, bf16[256,4,256]{2,0,1:T(8,128)(2,1)}, u32[]{:S(2)}) copy-start(bf16[256,4,256]{2,0,1:T(8,128)(2,1)} %get-tuple-element.19) | copy-start | bytes 1572868
  172.4 3.5 %copy-start.26 = (bf16[256,128]{1,0:T(8,128)(2,1)}, bf16[256,128]{1,0:T(8,128)(2,1)S(1)}, u32[]{:S(2)}) copy-start(bf16[256,128]{1,0:T(8,128)(2,1)S(1)} %get-tuple-element.33) | copy-start | bytes 196612
  172.4 3.5 %copy-start.28 = (bf16[256,128]{1,0:T(8,128)(2,1)}, bf16[256,128]{1,0:T(8,128)(2,1)S(1)}, u32[]{:S(2)}) copy-start(bf16[256,128]{1,0:T(8,128)(2,1)S(1)} %get-tuple-element.34) | copy-start | bytes 196612
  175.9 3.5 %copy-start.27 = (bf16[256,128]{1,0:T(8,128)(2,1)S(1)}, bf16[256,128]{1,0:T(8,128)(2,1)}, u32[]{:S(2)}) copy-start(bf16[256,128]{1,0:T(8,128)(2,1)} %copy-done.26) | copy-start | bytes 196612
  175.9 3.4 %copy-start.29 = (bf16[256,128]{1,0:T(8,128)(2,1)S(1)}, bf16[256,128]{1,0:T(8,128)(2,1)}, u32[]{:S(2)}) copy-start(bf16[256,128]{1,0:T(8,128)(2,1)} %copy-done.28) | copy-start | bytes 196612
  175.9 3.4 %copy-start.32 = (f32[256,4]{0,1:T(4,128)S(1)}, f32[256,4]{0,1:T(4,128)}, u32[]{:S(2)}) copy-start(f32[256,4]{0,1:T(4,128)} %copy-done.31) | copy-start | bytes 12292
  187.4 4.8 %copy-start.9 = (bf16[4096,512]{1,0:T(8,128)(2,1)S(1)}, bf16[4096,512]{1,0:T(8,128)(2,1)}, u32[]{:S(2)}) copy-start(bf16[4096,512]{1,0:T(8,128)(2,1)} %param.21) | copy-start | bytes 12582916
  194.3 4.7 %copy-start.15 = (f32[256,128]{1,0:T(8,128)S(1)}, f32[256,128]{1,0:T(8,128)}, u32[]{:S(2)}) copy-start(f32[256,128]{1,0:T(8,128)} %copy-done.14) | copy-start | bytes 393220
  202.0 3.6 %copy-start.5 = (bf16[256,4,256]{0,2,1:T(8,128)(2,1)S(1)}, bf16[256,4,256]{0,2,1:T(8,128)(2,1)}, u32[]{:S(2)}) copy-start(bf16[256,4,256]{0,2,1:T(8,128)(2,1)} %copy.37) | copy-start | bytes 1572868
  202.0 5.6 %copy-start.18 = (f32[256,512]{1,0:T(8,128)S(1)}, f32[256,512]{1,0:T(8,128)}, u32[]{:S(2)}) copy-start(f32[256,512]{1,0:T(8,128)} %fusion.108) | copy-start | bytes 1572868
  205.6 3.2 %copy-start.7 = (bf16[1024,512]{1,0:T(8,128)(2,1)S(1)}, bf16[1024,512]{1,0:T(8,128)(2,1)}, u32[]{:S(2)}) copy-start(bf16[1024,512]{1,0:T(8,128)(2,1)} %param.20) | copy-start | bytes 3145732
  212.9 27.1 %copy-start.33 = (f32[128]{0:T(128)S(1)}, f32[128]{0:T(128)}, u32[]{:S(2)}) copy-start(f32[128]{0:T(128)} %multiply_power_fusion) | copy-start | bytes 1540
  217.7 35.8 %copy-start.4 = (bf16[1,256,512]{2,1,0:T(8,128)(2,1)S(1)}, bf16[1,256,512]{2,1,0:T(8,128)(2,1)}, u32[]{:S(2)}) copy-start(bf16[1,256,512]{2,1,0:T(8,128)(2,1)} %param.13) | copy-start | bytes 786436
  239.1 14.5 %copy-start.24 = (bf16[256,512]{1,0:T(8,128)(2,1)S(1)}, bf16[256,512]{1,0:T(8,128)(2,1)}, u32[]{:S(2)}) copy-start(bf16[256,512]{1,0:T(8,128)(2,1)} %get-tuple-element.20) | copy-start | bytes 786436
  (15 other events, 34.0 us)
Sparse Core Ops, SparseCore 0:
  33.7 135.2 all-reduce.4
  210.1 28.8 all-reduce.6
where the time goes:
time: 262 us; the launch traced here: 261 us
  waiting for transfers between devices  155 us (59%)
  matrix products  57.6 us (22%)
  blocking collectives  15 us (6%)
  between operations  14.5 us (6%)
  other arithmetic  14.1 us (5%)
  local copies, waits for them, and re-layouts  5.19 us (2%)
    psum x1, waiting for transfers between devices, local_layer(): q_lin, gate_proj, up_proj, k_lin, v_val = lax.psum(partials, 'tx')  134 us
    psum x1, waiting for transfers between devices, local_layer(): branch = lax.psum(branch_part.astype(jnp.bfloat16), 'ty')  21.3 us
    dot_general x5, matrix products, local_layer(): jnp.einsum('td,tc->dc', normed, grad_col, preferred_element_type=jnp.floa...  14.9 us
    dot_general x5, matrix products, local_layer(): jnp.dot(normed, weight, preferred_element_type=jnp.float32)  11.1 us
    psum x1, blocking collectives, local_layer(): lax.psum(jnp.stack([jnp.sum(x_f, axis=1), jnp.sum(x_f * x_f, axis=1)], ax...  8.75 us
    psum x1, blocking collectives, local_layer(): lax.psum(jnp.stack([jnp.sum(value_a6, axis=1), jnp.sum(value_a6 * x_hat,...  6.29 us
  transfers between devices with their start and end apart: 2, of which 2 were waited for; matrix products, arithmetic and copies ran while one was open for 3% of the time, Pallas kernels for 0%

commit v1 on v0

v1 whole, which is shorter than its diff:
```python
import functools

import jax
import jax.numpy as jnp
import numpy as np
from jax import lax
from jax.experimental import pallas as pl
from jax.experimental.pallas import tpu as pltpu
from jax.sharding import PartitionSpec as P

EPS = 1e-6
ROPE_BASE = 10000.0
F32 = jnp.float32
BF16 = jnp.bfloat16
MESH = pl.DeviceIdType.MESH

BLK = 512
CHUNK = 1024
B_DATTN, B_DACT_LO, B_QKV, B_GU, B_DACT_HI, N_BLK = 0, 2, 6, 9, 25, 29
X_UNITS = ((0, 1), (1, 1), (2, 2), (4, 2), (6, 3), (9, 4), (13, 4), (17, 4), (21, 4), (25, 2), (27, 2))


def dot(a, b, dims):
    return lax.dot_general(a, b, (dims, ((), ())), preferred_element_type=F32)


def mm(a, b):
    return dot(a, b, ((1,), (0,)))


def mm_bt(a, b):
    return dot(a, b, ((1,), (1,)))


def mm_at(a, b):
    return dot(a, b, ((0,), (0,)))


def rope(first, second, cos_t, sin_t):
    return first * cos_t - second * sin_t, second * cos_t + first * sin_t


def layer_kernel(d_model, x_hbm, pos_ref, freq_ref, dy_hbm, gamma_ref, wq_hbm, wg_hbm, wu_hbm, wk_hbm, wv_hbm, wo_hbm, wd_hbm,
                 y_hbm, dx_hbm, dgamma_ref, nrm_hbm, attn_hbm, act_hbm, dq_hbm, dkv_hbm, dg_hbm, du_hbm,
                 x_v, dy_v, wqkv_v, wg_v, wu_v, wo_v, wd_v,
                 keep, send, rcore, chip, rx, md, packed, attn_v, dq_v, dkv_part, dkv_rx, dkv_v, kv_acc,
                 nrm_v, xhat_v, inv_v, cos_v, sin_v, br_v, dh_v, kvdh_v, y_snd, y_rx, dh_snd, dh_rx, y_o, dx_o,
                 st_snd, st_rx, bst_snd, bst_rx,
                 ld_sem, st_sem, cs, cr, xs, xr, gs, gr, ps, pr, ts, tr, ss, sr):
    tx = lax.axis_index('tx')
    ty = lax.axis_index('ty')
    core = lax.rem(tx, 2)
    near = {'tx': tx + 1 - 2 * core}
    across = {'tx': lax.rem(tx + 2, 4)}
    far = {'tx': lax.rem(tx + 1 - 2 * core + 2, 4)}
    other_ty = {'ty': 1 - ty}
    n_tok = x_v.shape[0]
    half = n_tok // 2
    mine = pl.multiple_of(core * half, half)
    other = pl.multiple_of((1 - core) * half, half)
    head_dim = 256
    q_width = wo_v.shape[0]
    heads = q_width // head_dim

    def load(i, src, dst):
        return pltpu.make_async_copy(src, dst, ld_sem.at[i])

    d_half = wd_v.shape[0] // 2
    loads = [
        load(0, dy_hbm.at[pl.ds(mine, half)], dy_v.at[0:half]),
        load(1, dy_hbm.at[pl.ds(other, half)], dy_v.at[half:n_tok]),
        load(2, wo_hbm, wo_v),
        load(3, x_hbm.at[pl.ds(mine, half)], x_v.at[0:half]),
        load(4, x_hbm.at[pl.ds(other, half)], x_v.at[half:n_tok]),
        load(5, wd_hbm.at[0:d_half], wd_v.at[0:d_half]),
        load(6, wq_hbm, wqkv_v.at[:, 0:q_width]),
        load(7, wk_hbm, wqkv_v.at[:, q_width:q_width + head_dim]),
        load(8, wv_hbm, wqkv_v.at[:, q_width + head_dim:q_width + 2 * head_dim]),
        load(9, wg_hbm, wg_v),
        load(10, wu_hbm, wu_v),
        load(11, wd_hbm.at[d_half:2 * d_half], wd_v.at[d_half:2 * d_half]),
    ]
    for ld in loads:
        ld.start()

    barrier = pltpu.get_barrier_semaphore()
    for peer in (near, across, far, other_ty):
        pl.semaphore_signal(barrier, inc=1, device_id=peer, device_id_type=MESH)
    pl.semaphore_wait(barrier, 4)

    def remote(src, dst, send_sem, recv_sem, peer):
        return pltpu.make_async_remote_copy(src_ref=src, dst_ref=dst, send_sem=send_sem, recv_sem=recv_sem,
                                            device_id=peer, device_id_type=MESH)

    def core_copy(b):
        return remote(send.at[b], rcore.at[b], cs.at[b], cr.at[b], near)

    def x_copy(u):
        start, count = X_UNITS[u]
        return remote(chip.at[pl.ds(start, count)], rx.at[pl.ds(start, count)], xs.at[u], xr.at[u], across)

    def put(b, part):
        keep[b] = part[:half]
        send[b] = part[half:].astype(BF16)
        core_copy(b).start()

    def issue_bwd(b, w_ref, row):
        put(b, mm_bt(dy_v[...], w_ref[pl.ds(row, BLK), :]))

    def issue_fwd(b, w_ref, col):
        put(b, mm(nrm_v[...], w_ref[:, pl.ds(col, BLK)]))

    def combine(b):
        core_copy(b).wait_recv()
        chip[b] = (keep[b] + rcore[b].astype(F32)).astype(BF16)

    def total(b):
        return chip[b].astype(F32) + rx[b].astype(F32)

    for i in range(3):
        loads[i].wait()
    issue_bwd(0, wo_v, 0)
    issue_bwd(1, wo_v, BLK)

    def rows_of(col_a, col_b):
        lane = lax.broadcasted_iota(jnp.int32, (half, 128), 1)
        return jnp.where(lane == 0, col_a, col_b).T[0:8]

    def stats_copy(snd, got, k, i):
        return remote(snd, got.at[i], ss.at[k * 3 + i], sr.at[k * 3 + i], (near, across, far)[i])

    def stats_start(snd, got, k, col_a, col_b):
        for lo, at in ((0, mine), (half, other)):
            snd[:, pl.ds(at, half)] = rows_of(col_a[lo:lo + half], col_b[lo:lo + half])
        for i in range(3):
            stats_copy(snd, got, k, i).start()

    def stats_finish(snd, got, k):
        for i in range(3):
            stats_copy(snd, got, k, i).wait_recv()
        rows = (snd[...] + got[0]) + (got[1] + got[2])
        snd_sum = got
        snd_sum[0] = rows
        cols = []
        for at in (mine, other):
            tile = jnp.broadcast_to(snd_sum[0, 0:1, pl.ds(at, half)], (128, half)).T
            tile_b = jnp.broadcast_to(snd_sum[0, 1:2, pl.ds(at, half)], (128, half)).T
            cols.append((tile[:, 0:1], tile_b[:, 0:1]))
        return (jnp.concatenate([cols[0][0], cols[1][0]], axis=0), jnp.concatenate([cols[0][1], cols[1][1]], axis=0))

    loads[3].wait()
    loads[4].wait()
    x_f = x_v[...].astype(F32)
    stats_start(st_snd, st_rx, 0, jnp.sum(x_f, axis=1, keepdims=True), jnp.sum(x_f * x_f, axis=1, keepdims=True))

    combine(0)
    x_copy(0).start()
    combine(1)
    x_copy(1).start()

    loads[5].wait()
    for i in range(4):
        issue_bwd(B_DACT_LO + i, wd_v, i * BLK)
        if i >= 1:
            combine(B_DACT_LO + i - 1)
        if i == 2:
            x_copy(2).start()
    combine(B_DACT_LO + 3)
    x_copy(3).start()

    sum_x, sum_xx = stats_finish(st_snd, st_rx, 0)
    tok_mean = sum_x / d_model
    inv_std = lax.rsqrt(sum_xx / d_model - tok_mean * tok_mean + EPS)
    inv_v[...] = jnp.broadcast_to(inv_std, (n_tok, 128))
    x_hat = (x_v[...].astype(F32) - tok_mean) * inv_std
    xhat_v[...] = x_hat
    nrm_v[...] = (x_hat * gamma_ref[...]).astype(BF16)

    for i in range(6, 9):
        loads[i].wait()
    for i in range(3):
        issue_fwd(B_QKV + i, wqkv_v, i * BLK)
    for i in range(3):
        combine(B_QKV + i)
    x_copy(4).start()

    loads[9].wait()
    loads[10].wait()
    for k in range(4):
        def gu_issue(j, carry, k=k):
            col = pl.multiple_of(k * CHUNK + j * BLK, BLK)
            issue_fwd(B_GU + 4 * k + j, wg_v, col)
            issue_fwd(B_GU + 4 * k + 2 + j, wu_v, col)
            return carry

        def gu_combine(j, carry, k=k):
            combine(B_GU + 4 * k + j)
            return carry

        lax.fori_loop(0, 2, gu_issue, 0)
        lax.fori_loop(0, 4, gu_combine, 0)
        x_copy(5 + k).start()

    loads[11].wait()

    def hi_issue(j, carry):
        issue_bwd(B_DACT_HI + j, wd_v, pl.multiple_of(d_half + j * BLK, BLK))
        return carry

    lax.fori_loop(0, 4, hi_issue, 0)
    for j in range(4):
        combine(B_DACT_HI + j)
        if j % 2 == 1:
            x_copy(9 + j // 2).start()

    freq = freq_ref[...]
    for lo, at in ((0, mine), (half, other)):
        pos_col = jnp.broadcast_to(pos_ref[0:1, pl.ds(at, half)].astype(F32), (128, half)).T
        angles = pos_col * freq
        cos_v[lo:lo + half] = jnp.cos(angles)
        sin_v[lo:lo + half] = jnp.sin(angles)

    def store(i, src, dst):
        return pltpu.make_async_copy(src, dst, st_sem.at[i])

    def store_rows(i, src, dst, cols):
        return [store(i, src.at[0:half], dst.at[pl.ds(mine, half), cols]),
                store(i + 1, src.at[half:n_tok], dst.at[pl.ds(other, half), cols])]

    stores = store_rows(0, nrm_v, nrm_hbm, pl.ds(0, x_v.shape[1]))
    for st in stores:
        st.start()

    packed_copy = remote(packed.at[0:half], packed.at[half:n_tok], ps.at[0], pr.at[0], near)
    x_copy(0).wait_recv()
    x_copy(1).wait_recv()
    for j in range(2):
        packed[0:half, q_width + 512 + j * BLK:q_width + 512 + (j + 1) * BLK] = total(B_DATTN + j).astype(BF16)
    x_copy(4).wait_recv()
    cos_h, sin_h = cos_v[0:half], sin_v[0:half]
    for j in range(2):
        blk = total(B_QKV + j)
        for h in range(2):
            lo = h * head_dim
            first, second = rope(blk[:, lo:lo + 128], blk[:, lo + 128:lo + 256], cos_h, sin_h)
            packed[0:half, j * BLK + lo:j * BLK + lo + 128] = first.astype(BF16)
            packed[0:half, j * BLK + lo + 128:j * BLK + lo + 256] = second.astype(BF16)
    blk = total(B_QKV + 2)
    first, second = rope(blk[:, 0:128], blk[:, 128:256], cos_h, sin_h)
    packed[0:half, q_width:q_width + 128] = first.astype(BF16)
    packed[0:half, q_width + 128:q_width + 256] = second.astype(BF16)
    packed[0:half, q_width + 256:q_width + 512] = blk[:, 256:512].astype(BF16)
    packed_copy.start()
    packed_copy.wait_recv()

    row_i = lax.rem(lax.broadcasted_iota(jnp.int32, (n_tok, n_tok), 0) + core * half, n_tok)
    col_i = lax.rem(lax.broadcasted_iota(jnp.int32, (n_tok, n_tok), 1) + core * half, n_tok)
    scale = head_dim ** -0.5
    kv_acc[...] = jnp.zeros_like(kv_acc)

    def head_step(h, carry):
        cols = pl.ds(pl.multiple_of(h * head_dim, head_dim), head_dim)
        q_h = packed[:, cols]
        da_h = packed[:, pl.ds(pl.multiple_of(q_width + 512 + h * head_dim, head_dim), head_dim)]
        k_rot = packed[:, q_width:q_width + 256]
        v_val = packed[:, q_width + 256:q_width + 512]
        scores = jnp.where(row_i >= col_i, mm_bt(q_h, k_rot) * scale, -1e30)
        exps = jnp.exp(scores - jnp.max(scores, axis=1, keepdims=True))
        probs_f = exps / jnp.sum(exps, axis=1, keepdims=True)
        probs = probs_f.astype(BF16)
        attn_v[:, cols] = mm(probs, v_val).astype(BF16)
        d_probs = mm_bt(da_h, v_val).astype(BF16).astype(F32)
        d_scores = (probs_f * (d_probs - jnp.sum(d_probs * probs_f, axis=1, keepdims=True)) * scale).astype(BF16)
        dq_h = mm(d_scores, k_rot).astype(BF16).astype(F32)
        first, second = rope(dq_h[:, 0:128], dq_h[:, 128:256], cos_v[...], -sin_v[...])
        dq_v[:, pl.ds(pl.multiple_of(h * head_dim, head_dim), 128)] = first.astype(BF16)
        dq_v[:, pl.ds(pl.multiple_of(h * head_dim + 128, 128), 128)] = second.astype(BF16)
        kv_acc[:, 0:256] += mm_at(d_scores, q_h)
        kv_acc[:, 256:512] += mm_at(probs, da_h)
        return carry

    lax.fori_loop(0, heads, head_step, 0)
    dkv_part[...] = kv_acc[...].astype(BF16)
    dkv_copy = remote(dkv_part, dkv_rx, ts.at[0], tr.at[0], other_ty)
    dkv_copy.start()
    for st in store_rows(2, attn_v, attn_hbm, pl.ds(0, q_width)) + store_rows(4, dq_v, dq_hbm, pl.ds(0, q_width)):
        st.start()
        stores.append(st)
    br_v[...] = mm(attn_v[...], wo_v[...])
    dh_v[...] = mm_bt(dq_v[...], wqkv_v[:, 0:q_width])

    def gather_copy(k, i):
        return remote(md.at[k, i, 0:half], md.at[k, i, half:n_tok], gs.at[3 * k + i], gr.at[3 * k + i], near)

    def dact_block(k, j):
        return B_DACT_LO + 2 * k + j if k < 2 else B_DACT_HI + 2 * (k - 2) + j

    def gated(k, want_act, want_grad):
        def step(r, carry):
            rows = pl.ds(pl.multiple_of(r * 16, 16), 16)
            for j in range(2):
                bg, bu, bd = B_GU + 4 * k + j, B_GU + 4 * k + 2 + j, dact_block(k, j)
                gate = (chip[bg, rows].astype(F32) + rx[bg, rows].astype(F32)).astype(BF16).astype(F32)
                up = (chip[bu, rows].astype(F32) + rx[bu, rows].astype(F32)).astype(BF16).astype(F32)
                sig = jax.nn.sigmoid(gate)
                silu = gate * sig
                cols = slice(j * BLK, (j + 1) * BLK)
                if want_act:
                    md[k, 0, rows, cols] = (silu * up).astype(BF16)
                if want_grad:
                    d_act = (chip[bd, rows].astype(F32) + rx[bd, rows].astype(F32)).astype(BF16).astype(F32)
                    md[k, 1, rows, cols] = (d_act * up * sig * (1.0 + gate * (1.0 - sig))).astype(BF16)
                    md[k, 2, rows, cols] = (d_act * silu).astype(BF16)
            return carry

        lax.fori_loop(0, half // 16, step, 0)
        for i in ((0,) if want_act else ()) + ((1, 2) if want_grad else ()):
            gather_copy(k, i).start()

    def md_store(k, i):
        for st in store_rows(8 + 6 * k + 2 * i, md.at[k, i], (act_hbm, dg_hbm, du_hbm)[i], pl.ds(k * CHUNK, CHUNK)):
            st.start()
            stores.append(st)

    def use_act(k):
        gather_copy(k, 0).wait_recv()
        md_store(k, 0)
        br_v[...] += mm(md[k, 0], wd_v[k * CHUNK:(k + 1) * CHUNK, :])

    def use_grad(k):
        for i in (1, 2):
            gather_copy(k, i).wait_recv()
            md_store(k, i)
        dh_v[...] += (mm_bt(md[k, 1], wg_v[:, k * CHUNK:(k + 1) * CHUNK])
                      + mm_bt(md[k, 2], wu_v[:, k * CHUNK:(k + 1) * CHUNK]))

    x_copy(2).wait_recv()
    x_copy(3).wait_recv()
    for k in range(2):
        x_copy(5 + k).wait_recv()
        gated(k, True, True)
        use_act(k)
        use_grad(k)
        if k == 0:
            dkv_copy.wait_recv()
            d_k = dkv_part[:, 0:256].astype(F32) + dkv_rx[:, 0:256].astype(F32)
            d_k = d_k.astype(BF16).astype(F32)
            first, second = rope(d_k[:, 0:128], d_k[:, 128:256], cos_v[...], -sin_v[...])
            dkv_v[:, 0:128] = first.astype(BF16)
            dkv_v[:, 128:256] = second.astype(BF16)
            dkv_v[:, 256:512] = (dkv_part[:, 256:512].astype(F32) + dkv_rx[:, 256:512].astype(F32)).astype(BF16)
            for st in store_rows(6, dkv_v, dkv_hbm, pl.ds(0, 512)):
                st.start()
                stores.append(st)
            kvdh_v[...] = mm_bt(dkv_v[...], wqkv_v[:, q_width:q_width + 512])
    for k in (2, 3):
        x_copy(5 + k).wait_recv()
        gated(k, True, False)
        use_act(k)
    y_snd[...] = br_v[...].astype(BF16)
    y_copy = remote(y_snd, y_rx, ts.at[1], tr.at[1], other_ty)
    y_copy.start()
    for k in (2, 3):
        x_copy(7 + k).wait_recv()
        gated(k, False, True)
        use_grad(k)
    dh_snd[...] = dh_v[...].astype(BF16)
    dh_copy = remote(dh_snd, dh_rx, ts.at[2], tr.at[2], other_ty)
    dh_copy.start()

    y_copy.wait_recv()
    y_o[...] = (x_v[...].astype(F32) + (y_snd[...].astype(F32) + y_rx[...].astype(F32))).astype(BF16)
    for st in store_rows(32, y_o, y_hbm, pl.ds(0, x_v.shape[1])):
        st.start()
        stores.append(st)

    dh_copy.wait_recv()
    d_nrm = (dh_snd[...].astype(F32) + dh_rx[...].astype(F32)) + kvdh_v[...]
    dh_v[...] = d_nrm
    d_hat = d_nrm * gamma_ref[...]
    x_hat = xhat_v[...]
    dgamma_ref[...] = jnp.sum(d_nrm * x_hat, axis=0, keepdims=True)
    stats_start(bst_snd, bst_rx, 1, jnp.sum(d_hat, axis=1, keepdims=True), jnp.sum(d_hat * x_hat, axis=1, keepdims=True))
    sum_d, sum_dx = stats_finish(bst_snd, bst_rx, 1)
    d_hat = dh_v[...] * gamma_ref[...]
    d_x = dy_v[...].astype(F32) + inv_v[:, 0:1] * (d_hat - sum_d / d_model - xhat_v[...] * (sum_dx / d_model))
    dx_o[...] = d_x.astype(BF16)
    for st in store_rows(34, dx_o, dx_hbm, pl.ds(0, x_v.shape[1])):
        st.start()
        stores.append(st)

    def drain(b, carry):
        core_copy(b).wait_send()
        return carry

    lax.fori_loop(0, N_BLK, drain, 0)
    for u in range(len(X_UNITS)):
        x_copy(u).wait_send()
    for k in range(4):
        for i in range(3):
            gather_copy(k, i).wait_send()
    for copy in (packed_copy, dkv_copy, y_copy, dh_copy):
        copy.wait_send()
    for i in range(3):
        stats_copy(st_snd, st_rx, 0, i).wait_send()
        stats_copy(bst_snd, bst_rx, 1, i).wait_send()
    for st in stores:
        st.wait()


def solution(mesh):
    tx_size = mesh.shape['tx']
    tok_spec = P('dp', None, 'tx')
    in_specs = (tok_spec, P('dp', None), tok_spec, P('tx'), P('tx', 'ty'), P('tx', 'ty'), P('tx', 'ty'),
                P('tx', None), P('tx', None), P('ty', 'tx'), P('ty', 'tx'))
    out_specs = (tok_spec, tok_spec, P(('dp', 'tx')), P(('dp', 'tx'), 'ty'), P(('dp', 'tx'), 'ty'), P(('dp', 'tx'), 'ty'),
                 P(('dp', 'tx'), None), P(('dp', 'tx'), None), P(('dp', 'ty'), 'tx'), P(('dp', 'ty'), 'tx'))

    def local_layer(x_in, positions, d_y, ln_gamma, w_q, w_g, w_u, w_k, w_v, w_o, w_d):
        _, n_tok, d_local = x_in.shape
        half = n_tok // 2
        d_model = d_local * tx_size
        head_dim = w_k.shape[1]
        q_width = w_q.shape[1]
        d_ff = w_g.shape[1]
        freq = jnp.asarray((ROPE_BASE ** (-2.0 * np.arange(head_dim // 2) / head_dim)).astype(np.float32)[None])
        any_spec = pl.BlockSpec(memory_space=pl.ANY)
        vmem_spec = pl.BlockSpec(memory_space=pltpu.VMEM)
        tok = (n_tok, d_local)
        sem = pltpu.SemaphoreType.DMA
        y_loc, dx_loc, d_gamma, normed, attn_flat, act, d_q, d_kv, d_gate, d_up = pl.pallas_call(
            functools.partial(layer_kernel, d_model),
            out_shape=[jax.ShapeDtypeStruct(tok, BF16), jax.ShapeDtypeStruct(tok, BF16), jax.ShapeDtypeStruct((1, d_local), F32),
                       jax.ShapeDtypeStruct(tok, BF16), jax.ShapeDtypeStruct((n_tok, q_width), BF16),
                       jax.ShapeDtypeStruct((n_tok, d_ff), BF16), jax.ShapeDtypeStruct((n_tok, q_width), BF16),
                       jax.ShapeDtypeStruct((n_tok, 2 * head_dim), BF16), jax.ShapeDtypeStruct((n_tok, d_ff), BF16),
                       jax.ShapeDtypeStruct((n_tok, d_ff), BF16)],
            in_specs=[any_spec, vmem_spec, vmem_spec, any_spec, vmem_spec] + [any_spec] * 7,
            out_specs=[any_spec, any_spec, vmem_spec] + [any_spec] * 7,
            scratch_shapes=[
                pltpu.VMEM(tok, BF16), pltpu.VMEM(tok, BF16), pltpu.VMEM((d_local, q_width + 2 * head_dim), BF16),
                pltpu.VMEM((d_local, d_ff), BF16), pltpu.VMEM((d_local, d_ff), BF16), pltpu.VMEM((q_width, d_local), BF16),
                pltpu.VMEM((d_ff, d_local), BF16),
                pltpu.VMEM((N_BLK, half, BLK), F32), pltpu.VMEM((N_BLK, half, BLK), BF16), pltpu.VMEM((N_BLK, half, BLK), BF16),
                pltpu.VMEM((N_BLK, half, BLK), BF16), pltpu.VMEM((N_BLK, half, BLK), BF16),
                pltpu.VMEM((4, 3, n_tok, CHUNK), BF16), pltpu.VMEM((n_tok, 2 * q_width + 2 * head_dim), BF16),
                pltpu.VMEM((n_tok, q_width), BF16), pltpu.VMEM((n_tok, q_width), BF16),
                pltpu.VMEM((n_tok, 512), BF16), pltpu.VMEM((n_tok, 512), BF16), pltpu.VMEM((n_tok, 512), BF16),
                pltpu.VMEM((n_tok, 512), F32),
                pltpu.VMEM(tok, BF16), pltpu.VMEM(tok, F32), pltpu.VMEM((n_tok, 128), F32), pltpu.VMEM((n_tok, 128), F32),
                pltpu.VMEM((n_tok, 128), F32), pltpu.VMEM(tok, F32), pltpu.VMEM(tok, F32), pltpu.VMEM(tok, F32),
                pltpu.VMEM(tok, BF16), pltpu.VMEM(tok, BF16), pltpu.VMEM(tok, BF16), pltpu.VMEM(tok, BF16),
                pltpu.VMEM(tok, BF16), pltpu.VMEM(tok, BF16),
                pltpu.VMEM((8, n_tok), F32), pltpu.VMEM((3, 8, n_tok), F32), pltpu.VMEM((8, n_tok), F32), pltpu.VMEM((3, 8, n_tok), F32),
                sem((12,)), sem((36,)), sem((N_BLK,)), sem((N_BLK,)), sem((len(X_UNITS),)), sem((len(X_UNITS),)),
                sem((12,)), sem((12,)), sem((1,)), sem((1,)), sem((3,)), sem((3,)), sem((6,)), sem((6,))],
            compiler_params=pltpu.CompilerParams(collective_id=0, has_side_effects=True, vmem_limit_bytes=67043328),
            name='layer',
        )(x_in.reshape(tok), positions, freq, d_y.reshape(tok), ln_gamma[None], w_q, w_g, w_u, w_k, w_v, w_o, w_d)

        dy = d_y.reshape(tok)
        d_wo = mm_at(attn_flat, dy)
        d_wd = mm_at(act, dy)
        d_wq = mm_at(normed, d_q)
        d_wk = mm_at(normed, d_kv[:, :head_dim])
        d_wv = mm_at(normed, d_kv[:, head_dim:])
        d_wg = mm_at(normed, d_gate)
        d_wu = mm_at(normed, d_up)
        return (y_loc.reshape(x_in.shape), dx_loc.reshape(x_in.shape), d_gamma.reshape(d_local),
                d_wq, d_wg, d_wu, d_wk, d_wv, d_wo, d_wd)

    return jax.shard_map(local_layer, mesh=mesh, in_specs=in_specs, out_specs=out_specs, check_vma=False)
```

time: 262 us -> 133 us (0.51)
  waiting for transfers between devices: 155 us -> 0 us
  Pallas kernels: 0 us -> 106 us
  matrix products: 57.6 us -> 23.5 us
  blocking collectives: 15 us -> 0 us
  other arithmetic: 14.1 us -> 0 us
  between operations: 14.5 us -> 0.67 us
  local copies, waits for them, and re-layouts: 5.19 us -> 2.38 us
    psum x2 -> x0, waiting for transfers between devices: 155 us -> none  [the longest x1 134 us: local_layer(): q_lin, gate_proj, up_proj, k_lin, v_val = lax.psum(partials, 'tx')]
    pallas_call x0 -> x1, Pallas kernels: none -> 106 us  [local_layer(): pl.pallas_call(functools.partial(layer_kernel, d_model), out_shape=[jax.S...]
    dot_general x26 -> x7, matrix products: 56 us -> 23.5 us  [dot(): return lax.dot_general(a, b, (dims, ((), ())), preferred_element_type=F32)]
    psum x2 -> x0, blocking collectives: 15 us -> none  [the longest x1 8.75 us: local_layer(): lax.psum(jnp.stack([jnp.sum(x_f, axis=1), jnp.sum(x_f * x_f, axis=1)], ax...]
    convert_element_type x5 -> x0, other arithmetic: 5.67 us -> none  [the longest x1 2.92 us: local_layer(): (d_act_f * up_f * sig_gate * (1.0 + gate_f * (1.0 - sig_gate))).astype(jn...]
    another operation x5 -> x0, other arithmetic: 2.66 us -> none
  transfers between devices with their start and end apart: 2 -> 0, of which waited for: 2 -> 0; matrix products, arithmetic and copies ran while one was open for 3% -> 0% of each run, Pallas kernels for 0% -> 0%
where the time goes in v1:
time: 133 us
  Pallas kernels  106 us (80%)
  matrix products  23.5 us (18%)
  local copies, waits for them, and re-layouts  2.38 us (2%)
    pallas_call x1, Pallas kernels, local_layer(): pl.pallas_call(functools.partial(layer_kernel, d_model), out_shape=[jax.S...  106 us
    dot_general x7, matrix products, dot(): return lax.dot_general(a, b, (dims, ((), ())), preferred_element_type=F32)  23.5 us

profile of v1, /device:TPU:0, one launch (start us, length us, event | category | flops | bytes accessed | tf_op | source)
XLA Modules:
  0.0 132.8 jit_solution(4992807499808188807)
XLA Ops:
  0.6 106.3 %layer.1 = (bf16[256,512]{1,0:T(8,128)(2,1)}, bf16[256,512]{1,0:T(8,128)(2,1)}, f32[1,512]{1,0:T(1,128)}, bf16[256,512]{1,0:T(8,128)(2,1)}, bf16[256,1024]{1,0:T...) custom-call(bf16[256,512]{1,0:T(8,128)(2,1)} %bitcast.21, ...), custom_call_target="tpu_custom_call" | custom-call | tf_op jit(solution)/shard_map/layer/pallas_call | solution.py:431
  106.9 2.0 %fusion = f32[512,256]{1,0:T(8,128)} fusion(bf16[256,512]{1,0:T(8,128)(2,1)} %get-tuple-element.23, bf16[256,512]{1,0:T(8,128)(2,1)} %get-tuple-element.27), kind=kOutput, calls=%fused_computation | convolution fusion | flops 67108864 | bytes 917504 | tf_op jit(solution)/shard_map/dot_general | solution.py:24
  109.0 2.0 %fusion.2 = f32[512,256]{1,0:T(8,128)} fusion(bf16[256,512]{1,0:T(8,128)(2,1)} %get-tuple-element.23, bf16[256,512]{1,0:T(8,128)(2,1)} %get-tuple-element.27), kind=kOutput, calls=%fused_computation.2 | convolution fusion | flops 67108864 | bytes 917504 | tf_op jit(solution)/shard_map/dot_general | solution.py:24
  111.0 0.0 copy-start
  111.0 0.0 copy-start.3
  111.0 6.5 %fusion.10 = f32[512,4096]{1,0:T(8,128)} fusion(bf16[256,512]{1,0:T(8,128)(2,1)} %get-tuple-element.23, bf16[256,4096]{1,0:T(8,128)(2,1)} %get-tuple-element.26), kind=kOutput, calls=%fused_computation.10 | convolution fusion | flops 1073741824 | bytes 10747904 | tf_op jit(solution)/shard_map/dot_general | solution.py:24
  117.5 0.0 copy-done
  117.5 0.0 copy-done.3
  117.5 4.7 %fusion.9 = f32[512,4096]{1,0:T(8,128)} fusion(bf16[256,512]{1,0:T(8,128)(2,1)S(1)} %copy-done, bf16[256,4096]{1,0:T(8,128)(2,1)S(1)} %copy-done.3), kind=kOutput, calls=%fused_computation.9 | convolution fusion | flops 1073741824 | bytes 10747904 | tf_op jit(solution)/shard_map/dot_general | solution.py:24
  122.2 0.0 copy-start.1
  122.2 0.0 copy-start.2
  122.2 0.0 copy-done.5
  122.2 1.8 %fusion.8 = f32[512,1024]{1,0:T(8,128)} fusion(bf16[256,512]{1,0:T(8,128)(2,1)S(1)} %copy-done, bf16[256,1024]{1,0:T(8,128)(2,1)S(1)} %copy-done.5), kind=kOutput, calls=%fused_computation.8 | convolution fusion | flops 268435456 | bytes 2883584 | tf_op jit(solution)/shard_map/dot_general | solution.py:24
  124.0 0.2 copy-done.1
  124.2 0.2 copy-done.2
  124.4 4.7 %fusion.4 = f32[4096,512]{1,0:T(8,128)} fusion(bf16[256,4096]{1,0:T(8,128)(2,1)S(1)} %copy-done.1, bf16[1,256,512]{2,1,0:T(8,128)(2,1)S(1)} %copy-done.2), kind=kOutput, calls=%fused_computation.4 | convolution fusion | flops 1073741824 | bytes 10747904 | tf_op jit(solution)/shard_map/dot_general | solution.py:24
  129.1 0.0 copy-done.4
  129.1 1.8 %fusion.6 = f32[1024,512]{1,0:T(8,128)} fusion(bf16[256,1024]{1,0:T(8,128)(2,1)S(1)} %copy-done.4, bf16[1,256,512]{2,1,0:T(8,128)(2,1)S(1)} %copy-done.2), kind=kOutput, calls=%fused_computation.6 | convolution fusion | flops 268435456 | bytes 2883584 | tf_op jit(solution)/shard_map/dot_general | solution.py:24
  130.9 0.0 copy-done.7
  130.9 0.7 copy.25
  131.6 0.0 copy-done.6
  131.6 0.7 copy.26
  132.3 0.0 copy-done.8
  132.3 0.6 copy.27
  (5 shorter events, 0.0 us)
Async XLA Ops:
  111.0 6.5 %copy-start = (bf16[256,512]{1,0:T(8,128)(2,1)S(1)}, bf16[256,512]{1,0:T(8,128)(2,1)}, u32[]{:S(2)}) copy-start(bf16[256,512]{1,0:T(8,128)(2,1)} %get-tuple-element.23) | copy-start | bytes 786436
  111.0 6.5 %copy-start.3 = (bf16[256,4096]{1,0:T(8,128)(2,1)S(1)}, bf16[256,4096]{1,0:T(8,128)(2,1)}, u32[]{:S(2)}) copy-start(bf16[256,4096]{1,0:T(8,128)(2,1)} %get-tuple-element.25) | copy-start | bytes 6291460
  117.5 4.7 %copy-start.5 = (bf16[256,1024]{1,0:T(8,128)(2,1)S(1)}, bf16[256,1024]{1,0:T(8,128)(2,1)}, u32[]{:S(2)}) copy-start(bf16[256,1024]{1,0:T(8,128)(2,1)} %get-tuple-element.24) | copy-start | bytes 1572868
  122.2 2.0 %copy-start.1 = (bf16[256,4096]{1,0:T(8,128)(2,1)S(1)}, bf16[256,4096]{1,0:T(8,128)(2,1)}, u32[]{:S(2)}) copy-start(bf16[256,4096]{1,0:T(8,128)(2,1)} %get-tuple-element.29) | copy-start | bytes 6291460
  122.2 2.1 %copy-start.2 = (bf16[1,256,512]{2,1,0:T(8,128)(2,1)S(1)}, bf16[1,256,512]{2,1,0:T(8,128)(2,1)}, u32[]{:S(2)}) copy-start(bf16[1,256,512]{2,1,0:T(8,128)(2,1)} %param.14) | copy-start | bytes 786436
  124.4 4.7 %copy-start.4 = (bf16[256,1024]{1,0:T(8,128)(2,1)S(1)}, bf16[256,1024]{1,0:T(8,128)(2,1)}, u32[]{:S(2)}) copy-start(bf16[256,1024]{1,0:T(8,128)(2,1)} %get-tuple-element.28) | copy-start | bytes 1572868
  129.1 1.8 %copy-start.7 = (bf16[256,512]{1,0:T(8,128)(2,1)S(1)}, bf16[256,512]{1,0:T(8,128)(2,1)}, u32[]{:S(2)}) copy-start(bf16[256,512]{1,0:T(8,128)(2,1)} %get-tuple-element.20) | copy-start | bytes 786436
  129.1 2.5 %copy-start.6 = (bf16[256,512]{1,0:T(8,128)(2,1)S(1)}, bf16[256,512]{1,0:T(8,128)(2,1)}, u32[]{:S(2)}) copy-start(bf16[256,512]{1,0:T(8,128)(2,1)} %get-tuple-element.21) | copy-start | bytes 786436
  129.1 3.2 %copy-start.8 = (f32[1,512]{1,0:T(1,128)S(1)}, f32[1,512]{1,0:T(1,128)}, u32[]{:S(2)}) copy-start(f32[1,512]{1,0:T(1,128)} %get-tuple-element.22) | copy-start | bytes 6148

commit v2 on v1

--- a/solution.py
+++ b/solution.py
@@ -406,6 +406,93 @@
         stats_copy(bst_snd, bst_rx, 1, i).wait_send()
     for st in stores:
         st.wait()
+
+
+def grad_kernel(nrm_hbm, attn_hbm, act_hbm, dq_hbm, dkv_hbm, dg_hbm, du_hbm, dy_hbm, y_in, dx_in, dgamma_in,
+                y_hbm, dx_hbm, dgamma_ref, dwq_hbm, dwg_hbm, dwu_hbm, dwk_hbm, dwv_hbm, dwo_hbm, dwd_hbm,
+                nrm_v, nrm_t, attn_v, act_v, dq_v, dkv_v, dg_v, du_v, dy_v, y_v, dx_v, ring, ld_sem, out_sem, cp_sem):
+    width = nrm_v.shape[1]
+    n_ring = ring.shape[0]
+
+    def load(i, src, dst):
+        return pltpu.make_async_copy(src, dst, ld_sem.at[i])
+
+    pairs = [(nrm_hbm, nrm_v), (dq_hbm, dq_v), (dkv_hbm, dkv_v), (dg_hbm, dg_v), (du_hbm, du_v), (dy_hbm, dy_v), (attn_hbm, attn_v), (act_hbm, act_v)]
+    loads = [load(i, src, dst) for i, (src, dst) in enumerate(pairs)]
+    for ld in loads:
+        ld.start()
+    hand_in = [load(8, y_in, y_v), load(9, dx_in, dx_v)]
+    for ld in hand_in:
+        ld.start()
+    dgamma_ref[...] = dgamma_in[...]
+
+    def tile_copy(slot, dst):
+        return pltpu.make_async_copy(ring.at[slot], dst, out_sem.at[slot])
+
+    def emit(t, value, dst):
+        slot = lax.rem(t, n_ring)
+
+        @pl.when(t >= n_ring)
+        def _():
+            tile_copy(slot, dwq_hbm.at[:, 0:BLK]).wait()
+
+        ring[slot] = value
+        tile_copy(slot, dst).start()
+
+    loads[0].wait()
+    nrm_t[...] = nrm_v[...].T
+
+    def columns(base, count, grads, out):
+        def step(j, carry):
+            cols = pl.ds(pl.multiple_of(j * BLK, BLK), BLK)
+            emit(base + j, mm(nrm_t[...], grads[:, cols]), out.at[:, cols])
+            return carry
+
+        lax.fori_loop(0, count, step, 0)
+
+    def rows(base, count, acts, out):
+        def step(j, carry):
+            at = pl.ds(pl.multiple_of(j * width, width), width)
+            emit(base + j, mm_at(acts[:, at], dy_v[...]), out.at[at, :])
+            return carry
+
+        lax.fori_loop(0, count, step, 0)
+
+    t = 0
+    n_q, n_f = dq_v.shape[1] // BLK, dg_v.shape[1] // BLK
+    loads[1].wait()
+    columns(t, n_q, dq_v, dwq_hbm)
+    t += n_q
+    loads[3].wait()
+    columns(t, n_f, dg_v, dwg_hbm)
+    t += n_f
+    loads[4].wait()
+    columns(t, n_f, du_v, dwu_hbm)
+    t += n_f
+    loads[5].wait()
+    loads[6].wait()
+    rows(t, n_q, attn_v, dwo_hbm)
+    t += n_q
+    loads[7].wait()
+    rows(t, n_f, act_v, dwd_hbm)
+    t += n_f
+    loads[2].wait()
+    for ld in hand_in:
+        ld.wait()
+    hand_out = [pltpu.make_async_copy(y_v, y_hbm, cp_sem.at[0]), pltpu.make_async_copy(dx_v, dx_hbm, cp_sem.at[1])]
+    for cp in hand_out:
+        cp.start()
+    slot = t % n_ring
+    tile_copy(slot, dwq_hbm.at[:, 0:BLK]).wait()
+    ring[slot] = mm(nrm_t[...], dkv_v[...])
+    kv_out = [pltpu.make_async_copy(ring.at[slot, :, 0:256], dwk_hbm, cp_sem.at[2]),
+              pltpu.make_async_copy(ring.at[slot, :, 256:512], dwv_hbm, cp_sem.at[3])]
+    for cp in kv_out:
+        cp.start()
+    for i in range(1, n_ring):
+        tile_copy((t + i) % n_ring, dwq_hbm.at[:, 0:BLK]).wait()
+    for cp in hand_out + kv_out:
+        cp.wait()
 
 
 def solution(mesh):
@@ -458,15 +545,20 @@
             name='layer',
         )(x_in.reshape(tok), positions, freq, d_y.reshape(tok), ln_gamma[None], w_q, w_g, w_u, w_k, w_v, w_o, w_d)
 
-        dy = d_y.reshape(tok)
-        d_wo = mm_at(attn_flat, dy)
-        d_wd = mm_at(act, dy)
-        d_wq = mm_at(normed, d_q)
-        d_wk = mm_at(normed, d_kv[:, :head_dim])
-        d_wv = mm_at(normed, d_kv[:, head_dim:])
-        d_wg = mm_at(normed, d_gate)
-        d_wu = mm_at(normed, d_up)
-        return (y_loc.reshape(x_in.shape), dx_loc.reshape(x_in.shape), d_gamma.reshape(d_local),
+        vm = pltpu.VMEM
+        y_out, d_x, d_gamma, d_wq, d_wg, d_wu, d_wk, d_wv, d_wo, d_wd = pl.pallas_call(
+            grad_kernel,
+            out_shape=[jax.ShapeDtypeStruct(tok, BF16), jax.ShapeDtypeStruct(tok, BF16), jax.ShapeDtypeStruct((1, d_local), F32)]
+            + [jax.ShapeDtypeStruct(w.shape, F32) for w in (w_q, w_g, w_u, w_k, w_v, w_o, w_d)],
+            in_specs=[any_spec] * 10 + [vmem_spec],
+            out_specs=[any_spec, any_spec, vmem_spec] + [any_spec] * 7,
+            scratch_shapes=[vm(tok, BF16), vm((d_local, n_tok), BF16), vm((n_tok, q_width), BF16), vm((n_tok, d_ff), BF16),
+                            vm((n_tok, q_width), BF16), vm((n_tok, 2 * head_dim), BF16), vm((n_tok, d_ff), BF16), vm((n_tok, d_ff), BF16),
+                            vm(tok, BF16), vm(tok, BF16), vm(tok, BF16), vm((8, d_local, BLK), F32), sem((10,)), sem((8,)), sem((4,))],
+            compiler_params=pltpu.CompilerParams(vmem_limit_bytes=60 * 1024 * 1024),
+            name='weight_grads',
+        )(normed, attn_flat, act, d_q, d_kv, d_gate, d_up, d_y.reshape(tok), y_loc, dx_loc, d_gamma)
+        return (y_out.reshape(x_in.shape), d_x.reshape(x_in.shape), d_gamma.reshape(d_local),
                 d_wq, d_wg, d_wu, d_wk, d_wv, d_wo, d_wd)
 
     return jax.shard_map(local_layer, mesh=mesh, in_specs=in_specs, out_specs=out_specs, check_vma=False)

time: 133 us -> 122 us (0.917)
  matrix products: 23.5 us -> 0 us
  Pallas kernels: 106 us -> 121 us
  local copies, waits for them, and re-layouts: 2.38 us -> 0 us
    dot_general x7 -> x0, matrix products: 23.5 us -> none  [dot(): return lax.dot_general(a, b, (dims, ((), ())), preferred_element_type=F32)]
    pallas_call x0 -> x1, Pallas kernels: none -> 14.6 us  [local_layer(): pl.pallas_call(grad_kernel, out_shape=[jax.ShapeDtypeStruct(tok, BF16), j...]
    unnamed x21 -> x0, local copies, waits for them, and re-layouts: 2.38 us -> none
where the time goes in v2:
time: 122 us
  Pallas kernels  121 us (99%)
    pallas_call x1, Pallas kernels, local_layer(): pl.pallas_call(functools.partial(layer_kernel, d_model), out_shape=[jax.S...  106 us
    pallas_call x1, Pallas kernels, local_layer(): pl.pallas_call(grad_kernel, out_shape=[jax.ShapeDtypeStruct(tok, BF16), j...  14.6 us

profile of v2, /device:TPU:0, one launch (start us, length us, event | category | flops | bytes accessed | tf_op | source)
XLA Modules:
  0.0 121.6 jit_solution(1365662053795674214)
XLA Ops:
  0.6 106.3 %layer.1 = (bf16[256,512]{1,0:T(8,128)(2,1)}, bf16[256,512]{1,0:T(8,128)(2,1)}, f32[1,512]{1,0:T(1,128)}, bf16[256,512]{1,0:T(8,128)(2,1)}, bf16[256,1024]{1,0:T...) custom-call(bf16[256,512]{1,0:T(8,128)(2,1)} %bitcast.8, ...), custom_call_target="tpu_custom_call" | custom-call | tf_op jit(solution)/shard_map/layer/pallas_call | solution.py:518
  106.9 14.6 %weight_grads.1 = (bf16[256,512]{1,0:T(8,128)(2,1)}, bf16[256,512]{1,0:T(8,128)(2,1)}, f32[1,512]{1,0:T(1,128)}, f32[512,1024]{1,0:T(8,128)}, f32[512,4096]{1,0:...) custom-call(bf16[256,512]{1,0:T(8,128)(2,1)} %get-tuple-element.30.n, ...), custom_call_target="tpu_custom_call" | custom-call | tf_op jit(solution)/shard_map/weight_grads/pallas_call | solution.py:549

commit v3 on v2

--- a/solution.py
+++ b/solution.py
@@ -17,7 +17,11 @@
 BLK = 512
 CHUNK = 1024
 B_DATTN, B_DACT_LO, B_QKV, B_GU, B_DACT_HI, N_BLK = 0, 2, 6, 9, 25, 29
-X_UNITS = ((0, 1), (1, 1), (2, 2), (4, 2), (6, 3), (9, 4), (13, 4), (17, 4), (21, 4), (25, 2), (27, 2))
+X_UNITS = ((0, 1), (1, 1), (2, 2), (4, 2), (6, 2), (9, 4), (13, 4), (17, 4), (21, 4), (25, 2))
+SPLITS = 4
+X_KV = len(X_UNITS)
+X_LAST = X_KV + 1
+N_X = X_LAST + SPLITS
 
 
 def dot(a, b, dims):
@@ -44,9 +48,9 @@
                  y_hbm, dx_hbm, dgamma_ref, nrm_hbm, attn_hbm, act_hbm, dq_hbm, dkv_hbm, dg_hbm, du_hbm,
                  x_v, dy_v, wqkv_v, wg_v, wu_v, wo_v, wd_v,
                  keep, send, rcore, chip, rx, md, packed, attn_v, dq_v, dkv_part, dkv_rx, dkv_v, kv_acc,
-                 nrm_v, xhat_v, inv_v, cos_v, sin_v, br_v, dh_v, kvdh_v, y_snd, y_rx, dh_snd, dh_rx, y_o, dx_o,
-                 st_snd, st_rx, bst_snd, bst_rx,
-                 ld_sem, st_sem, cs, cr, xs, xr, gs, gr, ps, pr, ts, tr, ss, sr):
+                 nrm_v, xhat_v, inv_v, cos_v, sin_v, br_v, dh_v, y_snd, y_rx, dh_snd, dh_rx, y_o, dx_o,
+                 st_snd, st_rx, st_sum, bst_snd, bst_rx,
+                 ld_sem, st_sem, cs, cr, xs, xr, gs, gr, ps, pr, ts, tr, ss, sr, ds, dr):
     tx = lax.axis_index('tx')
     ty = lax.axis_index('ty')
     core = lax.rem(tx, 2)
@@ -54,6 +58,7 @@
     across = {'tx': lax.rem(tx + 2, 4)}
     far = {'tx': lax.rem(tx + 1 - 2 * core + 2, 4)}
     other_ty = {'ty': 1 - ty}
+    peers = [near, across, far, other_ty] + [{'tx': p['tx'], 'ty': 1 - ty} for p in (near, across, far)]
     n_tok = x_v.shape[0]
     half = n_tok // 2
     mine = pl.multiple_of(core * half, half)
@@ -61,6 +66,7 @@
     head_dim = 256
     q_width = wo_v.shape[0]
     heads = q_width // head_dim
+    piece = half // SPLITS
 
     def load(i, src, dst):
         return pltpu.make_async_copy(src, dst, ld_sem.at[i])
@@ -80,13 +86,17 @@
         load(10, wu_hbm, wu_v),
         load(11, wd_hbm.at[d_half:2 * d_half], wd_v.at[d_half:2 * d_half]),
     ]
-    for ld in loads:
+    for ld in loads[:5]:
         ld.start()
 
     barrier = pltpu.get_barrier_semaphore()
-    for peer in (near, across, far, other_ty):
+    for peer in peers:
         pl.semaphore_signal(barrier, inc=1, device_id=peer, device_id_type=MESH)
-    pl.semaphore_wait(barrier, 4)
+    for ld in loads[:3]:
+        ld.wait()
+    for ld in loads[5:]:
+        ld.start()
+    pl.semaphore_wait(barrier, len(peers))
 
     def remote(src, dst, send_sem, recv_sem, peer):
         return pltpu.make_async_remote_copy(src_ref=src, dst_ref=dst, send_sem=send_sem, recv_sem=recv_sem,
@@ -96,6 +106,12 @@
         return remote(send.at[b], rcore.at[b], cs.at[b], cr.at[b], near)
 
     def x_copy(u):
+        if u >= X_LAST:
+            rows = pl.ds((u - X_LAST) * piece, piece)
+            return remote(chip.at[pl.ds(N_BLK - 2, 2), rows], rx.at[pl.ds(N_BLK - 2, 2), rows], xs.at[u], xr.at[u], across)
+        if u == X_KV:
+            cols = pl.ds(pl.multiple_of(ty * head_dim, head_dim), head_dim)
+            return remote(chip.at[B_QKV + 2, :, cols], rx.at[B_QKV + 2, :, cols], xs.at[u], xr.at[u], across)
         start, count = X_UNITS[u]
         return remote(chip.at[pl.ds(start, count)], rx.at[pl.ds(start, count)], xs.at[u], xr.at[u], across)
 
@@ -117,8 +133,6 @@
     def total(b):
         return chip[b].astype(F32) + rx[b].astype(F32)
 
-    for i in range(3):
-        loads[i].wait()
     issue_bwd(0, wo_v, 0)
     issue_bwd(1, wo_v, BLK)
 
@@ -126,32 +140,27 @@
         lane = lax.broadcasted_iota(jnp.int32, (half, 128), 1)
         return jnp.where(lane == 0, col_a, col_b).T[0:8]
 
-    def stats_copy(snd, got, k, i):
-        return remote(snd, got.at[i], ss.at[k * 3 + i], sr.at[k * 3 + i], (near, across, far)[i])
-
-    def stats_start(snd, got, k, col_a, col_b):
+    def stats_copies(snd, got, base, to):
+        return [remote(snd, got.at[i], ss.at[base + i], sr.at[base + i], peer) for i, peer in enumerate(to)]
+
+    def stats_put(snd, col_a, col_b):
         for lo, at in ((0, mine), (half, other)):
             snd[:, pl.ds(at, half)] = rows_of(col_a[lo:lo + half], col_b[lo:lo + half])
-        for i in range(3):
-            stats_copy(snd, got, k, i).start()
-
-    def stats_finish(snd, got, k):
-        for i in range(3):
-            stats_copy(snd, got, k, i).wait_recv()
-        rows = (snd[...] + got[0]) + (got[1] + got[2])
-        snd_sum = got
-        snd_sum[0] = rows
+
+    def stats_columns(rows_ref):
         cols = []
-        for at in (mine, other):
-            tile = jnp.broadcast_to(snd_sum[0, 0:1, pl.ds(at, half)], (128, half)).T
-            tile_b = jnp.broadcast_to(snd_sum[0, 1:2, pl.ds(at, half)], (128, half)).T
-            cols.append((tile[:, 0:1], tile_b[:, 0:1]))
-        return (jnp.concatenate([cols[0][0], cols[1][0]], axis=0), jnp.concatenate([cols[0][1], cols[1][1]], axis=0))
+        for i in range(2):
+            parts = [jnp.broadcast_to(rows_ref[i:i + 1, pl.ds(at, half)], (128, half)).T[:, 0:1] for at in (mine, other)]
+            cols.append(jnp.concatenate(parts, axis=0))
+        return cols
 
     loads[3].wait()
     loads[4].wait()
     x_f = x_v[...].astype(F32)
-    stats_start(st_snd, st_rx, 0, jnp.sum(x_f, axis=1, keepdims=True), jnp.sum(x_f * x_f, axis=1, keepdims=True))
+    stats_put(st_snd, jnp.sum(x_f, axis=1, keepdims=True), jnp.sum(x_f * x_f, axis=1, keepdims=True))
+    fwd_stats = stats_copies(st_snd, st_rx, 0, (near, across, far))
+    for copy in fwd_stats:
+        copy.start()
 
     combine(0)
     x_copy(0).start()
@@ -168,7 +177,10 @@
     combine(B_DACT_LO + 3)
     x_copy(3).start()
 
-    sum_x, sum_xx = stats_finish(st_snd, st_rx, 0)
+    for copy in fwd_stats:
+        copy.wait_recv()
+    st_sum[...] = (st_snd[...] + st_rx[0]) + (st_rx[1] + st_rx[2])
+    sum_x, sum_xx = stats_columns(st_sum)
     tok_mean = sum_x / d_model
     inv_std = lax.rsqrt(sum_xx / d_model - tok_mean * tok_mean + EPS)
     inv_v[...] = jnp.broadcast_to(inv_std, (n_tok, 128))
@@ -180,8 +192,10 @@
         loads[i].wait()
     for i in range(3):
         issue_fwd(B_QKV + i, wqkv_v, i * BLK)
-    for i in range(3):
+    for i in (2, 0, 1):
         combine(B_QKV + i)
+        if i == 2:
+            x_copy(X_KV).start()
     x_copy(4).start()
 
     loads[9].wait()
@@ -210,8 +224,10 @@
     lax.fori_loop(0, 4, hi_issue, 0)
     for j in range(4):
         combine(B_DACT_HI + j)
-        if j % 2 == 1:
-            x_copy(9 + j // 2).start()
+        if j == 1:
+            x_copy(9).start()
+    for r in range(SPLITS):
+        x_copy(X_LAST + r).start()
 
     freq = freq_ref[...]
     for lo, at in ((0, mine), (half, other)):
@@ -245,11 +261,16 @@
             first, second = rope(blk[:, lo:lo + 128], blk[:, lo + 128:lo + 256], cos_h, sin_h)
             packed[0:half, j * BLK + lo:j * BLK + lo + 128] = first.astype(BF16)
             packed[0:half, j * BLK + lo + 128:j * BLK + lo + 256] = second.astype(BF16)
-    blk = total(B_QKV + 2)
+    x_copy(X_KV).wait_recv()
+    kv_cols = pl.ds(pl.multiple_of(ty * head_dim, head_dim), head_dim)
+    blk = chip[B_QKV + 2, :, kv_cols].astype(F32) + rx[B_QKV + 2, :, kv_cols].astype(F32)
     first, second = rope(blk[:, 0:128], blk[:, 128:256], cos_h, sin_h)
-    packed[0:half, q_width:q_width + 128] = first.astype(BF16)
-    packed[0:half, q_width + 128:q_width + 256] = second.astype(BF16)
-    packed[0:half, q_width + 256:q_width + 512] = blk[:, 256:512].astype(BF16)
+    kv_mine = jnp.where(ty == 0, jnp.concatenate([first, second], axis=1), blk).astype(BF16)
+    kv_dst = packed.at[0:half, pl.ds(pl.multiple_of(q_width + ty * head_dim, head_dim), head_dim)]
+    kv_dst[...] = kv_mine
+    kv_copy = remote(kv_dst, kv_dst, ts.at[3], tr.at[3], other_ty)
+    kv_copy.start()
+    kv_copy.wait_recv()
     packed_copy.start()
     packed_copy.wait_recv()
 
@@ -289,13 +310,17 @@
     br_v[...] = mm(attn_v[...], wo_v[...])
     dh_v[...] = mm_bt(dq_v[...], wqkv_v[:, 0:q_width])
 
+    def piece_copy(r, i):
+        at = 12 + 2 * r + i - 1
+        return remote(md.at[3, i, r * piece:(r + 1) * piece], md.at[3, i, half + r * piece:half + (r + 1) * piece], gs.at[at], gr.at[at], near)
+
     def gather_copy(k, i):
         return remote(md.at[k, i, 0:half], md.at[k, i, half:n_tok], gs.at[3 * k + i], gr.at[3 * k + i], near)
 
     def dact_block(k, j):
         return B_DACT_LO + 2 * k + j if k < 2 else B_DACT_HI + 2 * (k - 2) + j
 
-    def gated(k, want_act, want_grad):
+    def gated(k, want_act, want_grad, lo=0, hi=None):
         def step(r, carry):
             rows = pl.ds(pl.multiple_of(r * 16, 16), 16)
             for j in range(2):
@@ -313,9 +338,10 @@
                     md[k, 2, rows, cols] = (d_act * silu).astype(BF16)
             return carry
 
-        lax.fori_loop(0, half // 16, step, 0)
-        for i in ((0,) if want_act else ()) + ((1, 2) if want_grad else ()):
-            gather_copy(k, i).start()
+        lax.fori_loop(lo // 16, (half if hi is None else hi) // 16, step, 0)
+        if hi is None:
+            for i in ((0,) if want_act else ()) + ((1, 2) if want_grad else ()):
+                gather_copy(k, i).start()
 
     def md_store(k, i):
         for st in store_rows(8 + 6 * k + 2 * i, md.at[k, i], (act_hbm, dg_hbm, du_hbm)[i], pl.ds(k * CHUNK, CHUNK)):
@@ -352,7 +378,7 @@
             for st in store_rows(6, dkv_v, dkv_hbm, pl.ds(0, 512)):
                 st.start()
                 stores.append(st)
-            kvdh_v[...] = mm_bt(dkv_v[...], wqkv_v[:, q_width:q_width + 512])
+            dh_v[...] += 0.5 * mm_bt(dkv_v[...], wqkv_v[:, q_width:q_width + 512])
     for k in (2, 3):
         x_copy(5 + k).wait_recv()
         gated(k, True, False)
@@ -360,13 +386,44 @@
     y_snd[...] = br_v[...].astype(BF16)
     y_copy = remote(y_snd, y_rx, ts.at[1], tr.at[1], other_ty)
     y_copy.start()
-    for k in (2, 3):
-        x_copy(7 + k).wait_recv()
-        gated(k, False, True)
-        use_grad(k)
-    dh_snd[...] = dh_v[...].astype(BF16)
-    dh_copy = remote(dh_snd, dh_rx, ts.at[2], tr.at[2], other_ty)
-    dh_copy.start()
+    x_copy(9).wait_recv()
+    gated(2, False, True)
+    use_grad(2)
+
+    def dh_copy(r):
+        return remote(dh_snd.at[r], dh_rx.at[r], ds.at[r], dr.at[r], other_ty)
+
+    def both(ref, r):
+        return jnp.concatenate([ref[r * piece:(r + 1) * piece], ref[half + r * piece:half + (r + 1) * piece]], axis=0)
+
+    sums = []
+
+    def piece_grad(r):
+        x_copy(X_LAST + r).wait_recv()
+        gated(3, False, True, r * piece, (r + 1) * piece)
+        for i in (1, 2):
+            piece_copy(r, i).start()
+
+    def piece_dh(r):
+        for i in (1, 2):
+            piece_copy(r, i).wait_recv()
+        part = both(dh_v, r) + mm_bt(both(md.at[3, 1], r), wg_v[:, 3 * CHUNK:4 * CHUNK]) + mm_bt(both(md.at[3, 2], r), wu_v[:, 3 * CHUNK:4 * CHUNK])
+        part_b = part.astype(BF16)
+        dh_snd[r] = part_b
+        dh_copy(r).start()
+        d_hat = part_b.astype(F32) * gamma_ref[...]
+        sums.append((jnp.sum(d_hat, axis=1, keepdims=True), jnp.sum(d_hat * both(xhat_v, r), axis=1, keepdims=True)))
+
+    for r in range(SPLITS):
+        piece_grad(r)
+        piece_dh(r)
+    cols = [jnp.concatenate([sums[r][i][:piece] for r in range(SPLITS)] + [sums[r][i][piece:] for r in range(SPLITS)], axis=0) for i in range(2)]
+    stats_put(bst_snd, cols[0], cols[1])
+    bwd_stats = stats_copies(bst_snd, bst_rx, 3, peers)
+    for copy in bwd_stats:
+        copy.start()
+    md_store(3, 1)
+    md_store(3, 2)
 
     y_copy.wait_recv()
     y_o[...] = (x_v[...].astype(F32) + (y_snd[...].astype(F32) + y_rx[...].astype(F32))).astype(BF16)
@@ -374,14 +431,18 @@
         st.start()
         stores.append(st)
 
-    dh_copy.wait_recv()
-    d_nrm = (dh_snd[...].astype(F32) + dh_rx[...].astype(F32)) + kvdh_v[...]
-    dh_v[...] = d_nrm
-    d_hat = d_nrm * gamma_ref[...]
-    x_hat = xhat_v[...]
-    dgamma_ref[...] = jnp.sum(d_nrm * x_hat, axis=0, keepdims=True)
-    stats_start(bst_snd, bst_rx, 1, jnp.sum(d_hat, axis=1, keepdims=True), jnp.sum(d_hat * x_hat, axis=1, keepdims=True))
-    sum_d, sum_dx = stats_finish(bst_snd, bst_rx, 1)
+    d_gamma = jnp.zeros_like(dgamma_ref)
+    for r in range(SPLITS):
+        dh_copy(r).wait_recv()
+        d_nrm = dh_snd[r].astype(F32) + dh_rx[r].astype(F32)
+        d_gamma = d_gamma + jnp.sum(d_nrm * both(xhat_v, r), axis=0, keepdims=True)
+        dh_v[r * piece:(r + 1) * piece] = d_nrm[:piece]
+        dh_v[half + r * piece:half + (r + 1) * piece] = d_nrm[piece:]
+    dgamma_ref[...] = d_gamma
+    for copy in bwd_stats:
+        copy.wait_recv()
+    st_sum[...] = ((bst_snd[...] + bst_rx[0]) + (bst_rx[1] + bst_rx[2])) + ((bst_rx[3] + bst_rx[4]) + (bst_rx[5] + bst_rx[6]))
+    sum_d, sum_dx = stats_columns(st_sum)
     d_hat = dh_v[...] * gamma_ref[...]
     d_x = dy_v[...].astype(F32) + inv_v[:, 0:1] * (d_hat - sum_d / d_model - xhat_v[...] * (sum_dx / d_model))
     dx_o[...] = d_x.astype(BF16)
@@ -394,16 +455,17 @@
         return carry
 
     lax.fori_loop(0, N_BLK, drain, 0)
-    for u in range(len(X_UNITS)):
+    for u in range(N_X):
         x_copy(u).wait_send()
     for k in range(4):
-        for i in range(3):
+        for i in range(3 if k < 3 else 1):
             gather_copy(k, i).wait_send()
-    for copy in (packed_copy, dkv_copy, y_copy, dh_copy):
+    for r in range(SPLITS):
+        for i in (1, 2):
+            piece_copy(r, i).wait_send()
+        dh_copy(r).wait_send()
+    for copy in [packed_copy, dkv_copy, y_copy, kv_copy] + fwd_stats + bwd_stats:
         copy.wait_send()
-    for i in range(3):
-        stats_copy(st_snd, st_rx, 0, i).wait_send()
-        stats_copy(bst_snd, bst_rx, 1, i).wait_send()
     for st in stores:
         st.wait()
 
@@ -535,12 +597,13 @@
                 pltpu.VMEM((n_tok, 512), BF16), pltpu.VMEM((n_tok, 512), BF16), pltpu.VMEM((n_tok, 512), BF16),
                 pltpu.VMEM((n_tok, 512), F32),
                 pltpu.VMEM(tok, BF16), pltpu.VMEM(tok, F32), pltpu.VMEM((n_tok, 128), F32), pltpu.VMEM((n_tok, 128), F32),
-                pltpu.VMEM((n_tok, 128), F32), pltpu.VMEM(tok, F32), pltpu.VMEM(tok, F32), pltpu.VMEM(tok, F32),
-                pltpu.VMEM(tok, BF16), pltpu.VMEM(tok, BF16), pltpu.VMEM(tok, BF16), pltpu.VMEM(tok, BF16),
+                pltpu.VMEM((n_tok, 128), F32), pltpu.VMEM(tok, F32), pltpu.VMEM(tok, F32),
+                pltpu.VMEM(tok, BF16), pltpu.VMEM(tok, BF16), pltpu.VMEM((SPLITS, n_tok // SPLITS, d_local), BF16), pltpu.VMEM((SPLITS, n_tok // SPLITS, d_local), BF16),
                 pltpu.VMEM(tok, BF16), pltpu.VMEM(tok, BF16),
-                pltpu.VMEM((8, n_tok), F32), pltpu.VMEM((3, 8, n_tok), F32), pltpu.VMEM((8, n_tok), F32), pltpu.VMEM((3, 8, n_tok), F32),
-                sem((12,)), sem((36,)), sem((N_BLK,)), sem((N_BLK,)), sem((len(X_UNITS),)), sem((len(X_UNITS),)),
-                sem((12,)), sem((12,)), sem((1,)), sem((1,)), sem((3,)), sem((3,)), sem((6,)), sem((6,))],
+                pltpu.VMEM((8, n_tok), F32), pltpu.VMEM((3, 8, n_tok), F32), pltpu.VMEM((8, n_tok), F32), pltpu.VMEM((8, n_tok), F32), pltpu.VMEM((7, 8, n_tok), F32),
+                sem((12,)), sem((36,)), sem((N_BLK,)), sem((N_BLK,)), sem((N_X,)), sem((N_X,)),
+                sem((12 + 2 * SPLITS,)), sem((12 + 2 * SPLITS,)), sem((1,)), sem((1,)), sem((4,)), sem((4,)), sem((10,)), sem((10,)),
+                sem((SPLITS,)), sem((SPLITS,))],
             compiler_params=pltpu.CompilerParams(collective_id=0, has_side_effects=True, vmem_limit_bytes=67043328),
             name='layer',
         )(x_in.reshape(tok), positions, freq, d_y.reshape(tok), ln_gamma[None], w_q, w_g, w_u, w_k, w_v, w_o, w_d)

time: 122 us -> 117 us (0.959)
  Pallas kernels: 121 us -> 116 us
    pallas_call x1, Pallas kernels: 106 us -> 101 us  [local_layer(): pl.pallas_call(functools.partial(layer_kernel, d_model), out_shape=[jax.S...]
where the time goes in v3:
time: 117 us
  Pallas kernels  116 us (99%)
    pallas_call x1, Pallas kernels, local_layer(): pl.pallas_call(functools.partial(layer_kernel, d_model), out_shape=[jax.S...  101 us
    pallas_call x1, Pallas kernels, local_layer(): pl.pallas_call(grad_kernel, out_shape=[jax.ShapeDtypeStruct(tok, BF16), j...  14.7 us

profile of v3, /device:TPU:0, one launch (start us, length us, event | category | flops | bytes accessed | tf_op | source)
XLA Modules:
  0.0 116.8 jit_solution(13724834447926392134)
XLA Ops:
  0.6 101.5 %layer.1 = (bf16[256,512]{1,0:T(8,128)(2,1)}, bf16[256,512]{1,0:T(8,128)(2,1)}, f32[1,512]{1,0:T(1,128)}, bf16[256,512]{1,0:T(8,128)(2,1)}, bf16[256,1024]{1,0:T...) custom-call(bf16[256,512]{1,0:T(8,128)(2,1)} %bitcast.8, ...), custom_call_target="tpu_custom_call" | custom-call | tf_op jit(solution)/shard_map/layer/pallas_call | solution.py:580
  102.1 14.7 %weight_grads.1 = (bf16[256,512]{1,0:T(8,128)(2,1)}, bf16[256,512]{1,0:T(8,128)(2,1)}, f32[1,512]{1,0:T(1,128)}, f32[512,1024]{1,0:T(8,128)}, f32[512,4096]{1,0:...) custom-call(bf16[256,512]{1,0:T(8,128)(2,1)} %get-tuple-element.30.n, ...), custom_call_target="tpu_custom_call" | custom-call | tf_op jit(solution)/shard_map/weight_grads/pallas_call | solution.py:612

commit v4 on v3

--- a/solution.py
+++ b/solution.py
@@ -45,12 +45,12 @@
 
 
 def layer_kernel(d_model, x_hbm, pos_ref, freq_ref, dy_hbm, gamma_ref, wq_hbm, wg_hbm, wu_hbm, wk_hbm, wv_hbm, wo_hbm, wd_hbm,
-                 y_hbm, dx_hbm, dgamma_ref, nrm_hbm, attn_hbm, act_hbm, dq_hbm, dkv_hbm, dg_hbm, du_hbm,
-                 x_v, dy_v, wqkv_v, wg_v, wu_v, wo_v, wd_v,
-                 keep, send, rcore, chip, rx, md, packed, attn_v, dq_v, dkv_part, dkv_rx, dkv_v, kv_acc,
-                 nrm_v, xhat_v, inv_v, cos_v, sin_v, br_v, dh_v, y_snd, y_rx, dh_snd, dh_rx, y_o, dx_o,
+                 y_o, dx_o, dgamma_ref, nrm_v, attn_v, md, dq_v, dkv_v, dy_v,
+                 x_v, wqkv_v, wg_v, wu_v, wo_v, wd_v,
+                 keep, send, rcore, chip, rx, packed, dkv_part, dkv_rx, kv_acc,
+                 xhat_v, inv_v, cos_v, sin_v, br_v, dh_v, y_snd, y_rx, dh_snd, dh_rx,
                  st_snd, st_rx, st_sum, bst_snd, bst_rx,
-                 ld_sem, st_sem, cs, cr, xs, xr, gs, gr, ps, pr, ts, tr, ss, sr, ds, dr):
+                 ld_sem, cs, cr, xs, xr, gs, gr, ps, pr, ts, tr, ss, sr, ds, dr):
     tx = lax.axis_index('tx')
     ty = lax.axis_index('ty')
     core = lax.rem(tx, 2)
@@ -235,17 +235,6 @@
         angles = pos_col * freq
         cos_v[lo:lo + half] = jnp.cos(angles)
         sin_v[lo:lo + half] = jnp.sin(angles)
-
-    def store(i, src, dst):
-        return pltpu.make_async_copy(src, dst, st_sem.at[i])
-
-    def store_rows(i, src, dst, cols):
-        return [store(i, src.at[0:half], dst.at[pl.ds(mine, half), cols]),
-                store(i + 1, src.at[half:n_tok], dst.at[pl.ds(other, half), cols])]
-
-    stores = store_rows(0, nrm_v, nrm_hbm, pl.ds(0, x_v.shape[1]))
-    for st in stores:
-        st.start()
 
     packed_copy = remote(packed.at[0:half], packed.at[half:n_tok], ps.at[0], pr.at[0], near)
     x_copy(0).wait_recv()
@@ -304,9 +293,6 @@
     dkv_part[...] = kv_acc[...].astype(BF16)
     dkv_copy = remote(dkv_part, dkv_rx, ts.at[0], tr.at[0], other_ty)
     dkv_copy.start()
-    for st in store_rows(2, attn_v, attn_hbm, pl.ds(0, q_width)) + store_rows(4, dq_v, dq_hbm, pl.ds(0, q_width)):
-        st.start()
-        stores.append(st)
     br_v[...] = mm(attn_v[...], wo_v[...])
     dh_v[...] = mm_bt(dq_v[...], wqkv_v[:, 0:q_width])
 
@@ -343,20 +329,13 @@
             for i in ((0,) if want_act else ()) + ((1, 2) if want_grad else ()):
                 gather_copy(k, i).start()
 
-    def md_store(k, i):
-        for st in store_rows(8 + 6 * k + 2 * i, md.at[k, i], (act_hbm, dg_hbm, du_hbm)[i], pl.ds(k * CHUNK, CHUNK)):
-            st.start()
-            stores.append(st)
-
     def use_act(k):
         gather_copy(k, 0).wait_recv()
-        md_store(k, 0)
         br_v[...] += mm(md[k, 0], wd_v[k * CHUNK:(k + 1) * CHUNK, :])
 
     def use_grad(k):
         for i in (1, 2):
             gather_copy(k, i).wait_recv()
-            md_store(k, i)
         dh_v[...] += (mm_bt(md[k, 1], wg_v[:, k * CHUNK:(k + 1) * CHUNK])
                       + mm_bt(md[k, 2], wu_v[:, k * CHUNK:(k + 1) * CHUNK]))
 
@@ -375,9 +354,6 @@
             dkv_v[:, 0:128] = first.astype(BF16)
             dkv_v[:, 128:256] = second.astype(BF16)
             dkv_v[:, 256:512] = (dkv_part[:, 256:512].astype(F32) + dkv_rx[:, 256:512].astype(F32)).astype(BF16)
-            for st in store_rows(6, dkv_v, dkv_hbm, pl.ds(0, 512)):
-                st.start()
-                stores.append(st)
             dh_v[...] += 0.5 * mm_bt(dkv_v[...], wqkv_v[:, q_width:q_width + 512])
     for k in (2, 3):
         x_copy(5 + k).wait_recv()
@@ -422,14 +398,9 @@
     bwd_stats = stats_copies(bst_snd, bst_rx, 3, peers)
     for copy in bwd_stats:
         copy.start()
-    md_store(3, 1)
-    md_store(3, 2)
 
     y_copy.wait_recv()
     y_o[...] = (x_v[...].astype(F32) + (y_snd[...].astype(F32) + y_rx[...].astype(F32))).astype(BF16)
-    for st in store_rows(32, y_o, y_hbm, pl.ds(0, x_v.shape[1])):
-        st.start()
-        stores.append(st)
 
     d_gamma = jnp.zeros_like(dgamma_ref)
     for r in range(SPLITS):
@@ -446,9 +417,6 @@
     d_hat = dh_v[...] * gamma_ref[...]
     d_x = dy_v[...].astype(F32) + inv_v[:, 0:1] * (d_hat - sum_d / d_model - xhat_v[...] * (sum_dx / d_model))
     dx_o[...] = d_x.astype(BF16)
-    for st in store_rows(34, dx_o, dx_hbm, pl.ds(0, x_v.shape[1])):
-        st.start()
-        stores.append(st)
 
     def drain(b, carry):
         core_copy(b).wait_send()
@@ -466,26 +434,21 @@
         dh_copy(r).wait_send()
     for copy in [packed_copy, dkv_copy, y_copy, kv_copy] + fwd_stats + bwd_stats:
         copy.wait_send()
-    for st in stores:
-        st.wait()
-
-
-def grad_kernel(nrm_hbm, attn_hbm, act_hbm, dq_hbm, dkv_hbm, dg_hbm, du_hbm, dy_hbm, y_in, dx_in, dgamma_in,
+
+
+def grad_kernel(y_v, dx_v, dgamma_in, nrm_v, attn_v, md, dq_v, dkv_v, dy_v,
                 y_hbm, dx_hbm, dgamma_ref, dwq_hbm, dwg_hbm, dwu_hbm, dwk_hbm, dwv_hbm, dwo_hbm, dwd_hbm,
-                nrm_v, nrm_t, attn_v, act_v, dq_v, dkv_v, dg_v, du_v, dy_v, y_v, dx_v, ring, ld_sem, out_sem, cp_sem):
-    width = nrm_v.shape[1]
+                nrm_t, ring, out_sem, cp_sem):
+    n_tok, width = nrm_v.shape
+    half = n_tok // 2
     n_ring = ring.shape[0]
-
-    def load(i, src, dst):
-        return pltpu.make_async_copy(src, dst, ld_sem.at[i])
-
-    pairs = [(nrm_hbm, nrm_v), (dq_hbm, dq_v), (dkv_hbm, dkv_v), (dg_hbm, dg_v), (du_hbm, du_v), (dy_hbm, dy_v), (attn_hbm, attn_v), (act_hbm, act_v)]
-    loads = [load(i, src, dst) for i, (src, dst) in enumerate(pairs)]
-    for ld in loads:
-        ld.start()
-    hand_in = [load(8, y_in, y_v), load(9, dx_in, dx_v)]
-    for ld in hand_in:
-        ld.start()
+    core = lax.rem(lax.axis_index('tx'), 2)
+    mine = pl.multiple_of(core * half, half)
+    other = pl.multiple_of((1 - core) * half, half)
+    hand_out = [pltpu.make_async_copy(src.at[lo:lo + half], dst.at[pl.ds(at, half)], cp_sem.at[i])
+                for i, (src, dst, lo, at) in enumerate(((y_v, y_hbm, 0, mine), (y_v, y_hbm, half, other), (dx_v, dx_hbm, 0, mine), (dx_v, dx_hbm, half, other)))]
+    for cp in hand_out:
+        cp.start()
     dgamma_ref[...] = dgamma_in[...]
 
     def tile_copy(slot, dst):
@@ -501,54 +464,40 @@
         ring[slot] = value
         tile_copy(slot, dst).start()
 
-    loads[0].wait()
     nrm_t[...] = nrm_v[...].T
 
-    def columns(base, count, grads, out):
+    def columns(base, count, grads, out, col0=0):
         def step(j, carry):
             cols = pl.ds(pl.multiple_of(j * BLK, BLK), BLK)
-            emit(base + j, mm(nrm_t[...], grads[:, cols]), out.at[:, cols])
+            emit(base + j, mm(nrm_t[...], grads[:, cols]), out.at[:, pl.ds(pl.multiple_of(col0 + j * BLK, BLK), BLK)])
             return carry
 
         lax.fori_loop(0, count, step, 0)
 
-    def rows(base, count, acts, out):
+    def rows(base, count, acts, out, row0=0):
         def step(j, carry):
             at = pl.ds(pl.multiple_of(j * width, width), width)
-            emit(base + j, mm_at(acts[:, at], dy_v[...]), out.at[at, :])
+            emit(base + j, mm_at(acts[:, at], dy_v[...]), out.at[pl.ds(pl.multiple_of(row0 + j * width, width), width), :])
             return carry
 
         lax.fori_loop(0, count, step, 0)
 
-    t = 0
-    n_q, n_f = dq_v.shape[1] // BLK, dg_v.shape[1] // BLK
-    loads[1].wait()
-    columns(t, n_q, dq_v, dwq_hbm)
-    t += n_q
-    loads[3].wait()
-    columns(t, n_f, dg_v, dwg_hbm)
-    t += n_f
-    loads[4].wait()
-    columns(t, n_f, du_v, dwu_hbm)
-    t += n_f
-    loads[5].wait()
-    loads[6].wait()
-    rows(t, n_q, attn_v, dwo_hbm)
-    t += n_q
-    loads[7].wait()
-    rows(t, n_f, act_v, dwd_hbm)
-    t += n_f
-    loads[2].wait()
-    for ld in hand_in:
-        ld.wait()
-    hand_out = [pltpu.make_async_copy(y_v, y_hbm, cp_sem.at[0]), pltpu.make_async_copy(dx_v, dx_hbm, cp_sem.at[1])]
-    for cp in hand_out:
-        cp.start()
+    columns(0, 2, dq_v, dwq_hbm)
+
+    def chunk_step(k, carry):
+        columns(2 + 6 * k, 2, md.at[k, 1], dwg_hbm, k * CHUNK)
+        columns(4 + 6 * k, 2, md.at[k, 2], dwu_hbm, k * CHUNK)
+        rows(6 + 6 * k, 2, md.at[k, 0], dwd_hbm, k * CHUNK)
+        return carry
+
+    lax.fori_loop(0, 4, chunk_step, 0)
+    rows(26, 2, attn_v, dwo_hbm)
+    t = 28
     slot = t % n_ring
     tile_copy(slot, dwq_hbm.at[:, 0:BLK]).wait()
     ring[slot] = mm(nrm_t[...], dkv_v[...])
-    kv_out = [pltpu.make_async_copy(ring.at[slot, :, 0:256], dwk_hbm, cp_sem.at[2]),
-              pltpu.make_async_copy(ring.at[slot, :, 256:512], dwv_hbm, cp_sem.at[3])]
+    kv_out = [pltpu.make_async_copy(ring.at[slot, :, 0:256], dwk_hbm, cp_sem.at[4]),
+              pltpu.make_async_copy(ring.at[slot, :, 256:512], dwv_hbm, cp_sem.at[5])]
     for cp in kv_out:
         cp.start()
     for i in range(1, n_ring):
@@ -577,50 +526,39 @@
         vmem_spec = pl.BlockSpec(memory_space=pltpu.VMEM)
         tok = (n_tok, d_local)
         sem = pltpu.SemaphoreType.DMA
-        y_loc, dx_loc, d_gamma, normed, attn_flat, act, d_q, d_kv, d_gate, d_up = pl.pallas_call(
+        vm = pltpu.VMEM
+        kept = pl.pallas_call(
             functools.partial(layer_kernel, d_model),
-            out_shape=[jax.ShapeDtypeStruct(tok, BF16), jax.ShapeDtypeStruct(tok, BF16), jax.ShapeDtypeStruct((1, d_local), F32),
-                       jax.ShapeDtypeStruct(tok, BF16), jax.ShapeDtypeStruct((n_tok, q_width), BF16),
-                       jax.ShapeDtypeStruct((n_tok, d_ff), BF16), jax.ShapeDtypeStruct((n_tok, q_width), BF16),
-                       jax.ShapeDtypeStruct((n_tok, 2 * head_dim), BF16), jax.ShapeDtypeStruct((n_tok, d_ff), BF16),
-                       jax.ShapeDtypeStruct((n_tok, d_ff), BF16)],
+            out_shape=[vm(tok, BF16), vm(tok, BF16), vm((1, d_local), F32), vm(tok, BF16), vm((n_tok, q_width), BF16),
+                       vm((4, 3, n_tok, CHUNK), BF16), vm((n_tok, q_width), BF16), vm((n_tok, 2 * head_dim), BF16), vm(tok, BF16)],
             in_specs=[any_spec, vmem_spec, vmem_spec, any_spec, vmem_spec] + [any_spec] * 7,
-            out_specs=[any_spec, any_spec, vmem_spec] + [any_spec] * 7,
+            out_specs=[vmem_spec] * 9,
             scratch_shapes=[
-                pltpu.VMEM(tok, BF16), pltpu.VMEM(tok, BF16), pltpu.VMEM((d_local, q_width + 2 * head_dim), BF16),
-                pltpu.VMEM((d_local, d_ff), BF16), pltpu.VMEM((d_local, d_ff), BF16), pltpu.VMEM((q_width, d_local), BF16),
-                pltpu.VMEM((d_ff, d_local), BF16),
-                pltpu.VMEM((N_BLK, half, BLK), F32), pltpu.VMEM((N_BLK, half, BLK), BF16), pltpu.VMEM((N_BLK, half, BLK), BF16),
-                pltpu.VMEM((N_BLK, half, BLK), BF16), pltpu.VMEM((N_BLK, half, BLK), BF16),
-                pltpu.VMEM((4, 3, n_tok, CHUNK), BF16), pltpu.VMEM((n_tok, 2 * q_width + 2 * head_dim), BF16),
-                pltpu.VMEM((n_tok, q_width), BF16), pltpu.VMEM((n_tok, q_width), BF16),
-                pltpu.VMEM((n_tok, 512), BF16), pltpu.VMEM((n_tok, 512), BF16), pltpu.VMEM((n_tok, 512), BF16),
-                pltpu.VMEM((n_tok, 512), F32),
-                pltpu.VMEM(tok, BF16), pltpu.VMEM(tok, F32), pltpu.VMEM((n_tok, 128), F32), pltpu.VMEM((n_tok, 128), F32),
-                pltpu.VMEM((n_tok, 128), F32), pltpu.VMEM(tok, F32), pltpu.VMEM(tok, F32),
-                pltpu.VMEM(tok, BF16), pltpu.VMEM(tok, BF16), pltpu.VMEM((SPLITS, n_tok // SPLITS, d_local), BF16), pltpu.VMEM((SPLITS, n_tok // SPLITS, d_local), BF16),
-                pltpu.VMEM(tok, BF16), pltpu.VMEM(tok, BF16),
-                pltpu.VMEM((8, n_tok), F32), pltpu.VMEM((3, 8, n_tok), F32), pltpu.VMEM((8, n_tok), F32), pltpu.VMEM((8, n_tok), F32), pltpu.VMEM((7, 8, n_tok), F32),
-                sem((12,)), sem((36,)), sem((N_BLK,)), sem((N_BLK,)), sem((N_X,)), sem((N_X,)),
+                vm(tok, BF16), vm((d_local, q_width + 2 * head_dim), BF16), vm((d_local, d_ff), BF16), vm((d_local, d_ff), BF16),
+                vm((q_width, d_local), BF16), vm((d_ff, d_local), BF16),
+                vm((N_BLK, half, BLK), F32), vm((N_BLK, half, BLK), BF16), vm((N_BLK, half, BLK), BF16),
+                vm((N_BLK, half, BLK), BF16), vm((N_BLK, half, BLK), BF16), vm((n_tok, 2 * q_width + 2 * head_dim), BF16),
+                vm((n_tok, 512), BF16), vm((n_tok, 512), BF16), vm((n_tok, 512), F32),
+                vm(tok, F32), vm((n_tok, 128), F32), vm((n_tok, 128), F32), vm((n_tok, 128), F32), vm(tok, F32), vm(tok, F32),
+                vm(tok, BF16), vm(tok, BF16), vm((SPLITS, n_tok // SPLITS, d_local), BF16), vm((SPLITS, n_tok // SPLITS, d_local), BF16),
+                vm((8, n_tok), F32), vm((3, 8, n_tok), F32), vm((8, n_tok), F32), vm((8, n_tok), F32), vm((7, 8, n_tok), F32),
+                sem((12,)), sem((N_BLK,)), sem((N_BLK,)), sem((N_X,)), sem((N_X,)),
                 sem((12 + 2 * SPLITS,)), sem((12 + 2 * SPLITS,)), sem((1,)), sem((1,)), sem((4,)), sem((4,)), sem((10,)), sem((10,)),
                 sem((SPLITS,)), sem((SPLITS,))],
-            compiler_params=pltpu.CompilerParams(collective_id=0, has_side_effects=True, vmem_limit_bytes=67043328),
+            compiler_params=pltpu.CompilerParams(collective_id=0, has_side_effects=True, vmem_limit_bytes=50 * 1024 * 1024),
             name='layer',
         )(x_in.reshape(tok), positions, freq, d_y.reshape(tok), ln_gamma[None], w_q, w_g, w_u, w_k, w_v, w_o, w_d)
 
-        vm = pltpu.VMEM
         y_out, d_x, d_gamma, d_wq, d_wg, d_wu, d_wk, d_wv, d_wo, d_wd = pl.pallas_call(
             grad_kernel,
             out_shape=[jax.ShapeDtypeStruct(tok, BF16), jax.ShapeDtypeStruct(tok, BF16), jax.ShapeDtypeStruct((1, d_local), F32)]
             + [jax.ShapeDtypeStruct(w.shape, F32) for w in (w_q, w_g, w_u, w_k, w_v, w_o, w_d)],
-            in_specs=[any_spec] * 10 + [vmem_spec],
+            in_specs=[vmem_spec] * 9,
             out_specs=[any_spec, any_spec, vmem_spec] + [any_spec] * 7,
-            scratch_shapes=[vm(tok, BF16), vm((d_local, n_tok), BF16), vm((n_tok, q_width), BF16), vm((n_tok, d_ff), BF16),
-                            vm((n_tok, q_width), BF16), vm((n_tok, 2 * head_dim), BF16), vm((n_tok, d_ff), BF16), vm((n_tok, d_ff), BF16),
-                            vm(tok, BF16), vm(tok, BF16), vm(tok, BF16), vm((8, d_local, BLK), F32), sem((10,)), sem((8,)), sem((4,))],
-            compiler_params=pltpu.CompilerParams(vmem_limit_bytes=60 * 1024 * 1024),
+            scratch_shapes=[vm((d_local, n_tok), BF16), vm((8, d_local, BLK), F32), sem((8,)), sem((6,))],
+            compiler_params=pltpu.CompilerParams(vmem_limit_bytes=40 * 1024 * 1024),
             name='weight_grads',
-        )(normed, attn_flat, act, d_q, d_kv, d_gate, d_up, d_y.reshape(tok), y_loc, dx_loc, d_gamma)
+        )(*kept)
         return (y_out.reshape(x_in.shape), d_x.reshape(x_in.shape), d_gamma.reshape(d_local),
                 d_wq, d_wg, d_wu, d_wk, d_wv, d_wo, d_wd)
 

time: 117 us -> 114 us (0.974)
  Pallas kernels: 116 us -> 113 us
    pallas_call x1, Pallas kernels: 14.7 us -> 12.7 us  [local_layer(): pl.pallas_call(grad_kernel, out_shape=[jax.ShapeDtypeStruct(tok, BF16), j...]
    pallas_call x1, Pallas kernels: 101 us -> 100 us  [local_layer(): pl.pallas_call(functools.partial(layer_kernel, d_model), out_shape=[vm(to...]
where the time goes in v4:
time: 114 us
  Pallas kernels  113 us (99%)
    pallas_call x1, Pallas kernels, local_layer(): pl.pallas_call(functools.partial(layer_kernel, d_model), out_shape=[vm(to...  100 us
    pallas_call x1, Pallas kernels, local_layer(): pl.pallas_call(grad_kernel, out_shape=[jax.ShapeDtypeStruct(tok, BF16), j...  12.7 us

profile of v4, /device:TPU:0, one launch (start us, length us, event | category | flops | bytes accessed | tf_op | source)
XLA Modules:
  0.0 113.6 jit_solution(3910546341418875898)
XLA Ops:
  0.6 100.2 %layer.1 = (bf16[256,512]{1,0:T(8,128)(2,1)S(1)}, bf16[256,512]{1,0:T(8,128)(2,1)S(1)}, f32[1,512]{1,0:T(1,128)S(1)}, bf16[256,512]{1,0:T(8,128)(2,1)S(1)}, bf16...) custom-call(bf16[256,512]{1,0:T(8,128)(2,1)} %bitcast.6, ...), custom_call_target="tpu_custom_call" | custom-call | tf_op jit(solution)/shard_map/layer/pallas_call | solution.py:530
  100.8 12.7 %weight_grads.1 = (bf16[256,512]{1,0:T(8,128)(2,1)}, bf16[256,512]{1,0:T(8,128)(2,1)}, f32[1,512]{1,0:T(1,128)}, f32[512,1024]{1,0:T(8,128)}, f32[512,4096]{1,0:...) custom-call(bf16[256,512]{1,0:T(8,128)(2,1)S(1)} %get-tuple-element., ...), custom_call_target="tpu_custom_call" | custom-call | tf_op jit(solution)/shard_map/weight_grads/pallas_call | solution.py:552

commit v5 on v4

--- a/solution.py
+++ b/solution.py
@@ -451,58 +451,44 @@
         cp.start()
     dgamma_ref[...] = dgamma_in[...]
 
-    def tile_copy(slot, dst):
-        return pltpu.make_async_copy(ring.at[slot], dst, out_sem.at[slot])
-
-    def emit(t, value, dst):
-        slot = lax.rem(t, n_ring)
-
-        @pl.when(t >= n_ring)
-        def _():
-            tile_copy(slot, dwq_hbm.at[:, 0:BLK]).wait()
-
+    flight = []
+
+    def emit(value, dsts):
+        t = len(flight)
+        slot = t % n_ring
+        if t >= n_ring:
+            for cp in flight[t - n_ring]:
+                cp.wait()
         ring[slot] = value
-        tile_copy(slot, dst).start()
+        copies = [pltpu.make_async_copy(ring.at[slot, :, lo:hi], dst, out_sem.at[slot, i]) for i, (lo, hi, dst) in enumerate(dsts)]
+        for cp in copies:
+            cp.start()
+        flight.append(copies)
 
     nrm_t[...] = nrm_v[...].T
 
-    def columns(base, count, grads, out, col0=0):
-        def step(j, carry):
-            cols = pl.ds(pl.multiple_of(j * BLK, BLK), BLK)
-            emit(base + j, mm(nrm_t[...], grads[:, cols]), out.at[:, pl.ds(pl.multiple_of(col0 + j * BLK, BLK), BLK)])
-            return carry
-
-        lax.fori_loop(0, count, step, 0)
-
-    def rows(base, count, acts, out, row0=0):
-        def step(j, carry):
-            at = pl.ds(pl.multiple_of(j * width, width), width)
-            emit(base + j, mm_at(acts[:, at], dy_v[...]), out.at[pl.ds(pl.multiple_of(row0 + j * width, width), width), :])
-            return carry
-
-        lax.fori_loop(0, count, step, 0)
-
-    columns(0, 2, dq_v, dwq_hbm)
-
-    def chunk_step(k, carry):
-        columns(2 + 6 * k, 2, md.at[k, 1], dwg_hbm, k * CHUNK)
-        columns(4 + 6 * k, 2, md.at[k, 2], dwu_hbm, k * CHUNK)
-        rows(6 + 6 * k, 2, md.at[k, 0], dwd_hbm, k * CHUNK)
-        return carry
-
-    lax.fori_loop(0, 4, chunk_step, 0)
-    rows(26, 2, attn_v, dwo_hbm)
-    t = 28
-    slot = t % n_ring
-    tile_copy(slot, dwq_hbm.at[:, 0:BLK]).wait()
-    ring[slot] = mm(nrm_t[...], dkv_v[...])
-    kv_out = [pltpu.make_async_copy(ring.at[slot, :, 0:256], dwk_hbm, cp_sem.at[4]),
-              pltpu.make_async_copy(ring.at[slot, :, 256:512], dwv_hbm, cp_sem.at[5])]
-    for cp in kv_out:
-        cp.start()
-    for i in range(1, n_ring):
-        tile_copy((t + i) % n_ring, dwq_hbm.at[:, 0:BLK]).wait()
-    for cp in hand_out + kv_out:
+    def columns(grads, col, out, to):
+        emit(mm(nrm_t[...], grads[:, col:col + BLK]), [(0, BLK, out.at[:, to:to + BLK])])
+
+    def rows(acts, col, out, to):
+        emit(mm_at(acts[:, col:col + width], dy_v[...]), [(0, BLK, out.at[to:to + width, :])])
+
+    for j in range(2):
+        columns(dq_v, j * BLK, dwq_hbm, j * BLK)
+    for k in range(4):
+        for j in range(2):
+            columns(md.at[k, 1], j * BLK, dwg_hbm, k * CHUNK + j * BLK)
+        for j in range(2):
+            columns(md.at[k, 2], j * BLK, dwu_hbm, k * CHUNK + j * BLK)
+        for j in range(2):
+            rows(md.at[k, 0], j * BLK, dwd_hbm, k * CHUNK + j * BLK)
+    for j in range(2):
+        rows(attn_v, j * BLK, dwo_hbm, j * BLK)
+    emit(mm(nrm_t[...], dkv_v[...]), [(0, 256, dwk_hbm), (256, 512, dwv_hbm)])
+    for copies in flight[-n_ring:]:
+        for cp in copies:
+            cp.wait()
+    for cp in hand_out:
         cp.wait()
 
 
@@ -555,7 +541,7 @@
             + [jax.ShapeDtypeStruct(w.shape, F32) for w in (w_q, w_g, w_u, w_k, w_v, w_o, w_d)],
             in_specs=[vmem_spec] * 9,
             out_specs=[any_spec, any_spec, vmem_spec] + [any_spec] * 7,
-            scratch_shapes=[vm((d_local, n_tok), BF16), vm((8, d_local, BLK), F32), sem((8,)), sem((6,))],
+            scratch_shapes=[vm((d_local, n_tok), BF16), vm((12, d_local, BLK), F32), sem((12, 2)), sem((4,))],
             compiler_params=pltpu.CompilerParams(vmem_limit_bytes=40 * 1024 * 1024),
             name='weight_grads',
         )(*kept)

time: 114 us -> 113 us (level)
    pallas_call x1, Pallas kernels: 12.7 us -> 11.2 us  [local_layer(): pl.pallas_call(grad_kernel, out_shape=[jax.ShapeDtypeStruct(tok, BF16), j...]
where the time goes in v5:
time: 113 us; the launch traced here: 112 us
  Pallas kernels  112 us (99%)
    pallas_call x1, Pallas kernels, local_layer(): pl.pallas_call(functools.partial(layer_kernel, d_model), out_shape=[vm(to...  100 us
    pallas_call x1, Pallas kernels, local_layer(): pl.pallas_call(grad_kernel, out_shape=[jax.ShapeDtypeStruct(tok, BF16), j...  11.2 us

profile of v5, /device:TPU:0, one launch (start us, length us, event | category | flops | bytes accessed | tf_op | source)
XLA Modules:
  0.0 112.4 jit_solution(5088765756034879043)
XLA Ops:
  0.6 100.4 %layer.1 = (bf16[256,512]{1,0:T(8,128)(2,1)S(1)}, bf16[256,512]{1,0:T(8,128)(2,1)S(1)}, f32[1,512]{1,0:T(1,128)S(1)}, bf16[256,512]{1,0:T(8,128)(2,1)S(1)}, bf16...) custom-call(bf16[256,512]{1,0:T(8,128)(2,1)} %bitcast.6, ...), custom_call_target="tpu_custom_call" | custom-call | tf_op jit(solution)/shard_map/layer/pallas_call | solution.py:516
  101.0 11.2 %weight_grads.1 = (bf16[256,512]{1,0:T(8,128)(2,1)}, bf16[256,512]{1,0:T(8,128)(2,1)}, f32[1,512]{1,0:T(1,128)}, f32[512,1024]{1,0:T(8,128)}, f32[512,4096]{1,0:...) custom-call(bf16[256,512]{1,0:T(8,128)(2,1)S(1)} %get-tuple-element., ...), custom_call_target="tpu_custom_call" | custom-call | tf_op jit(solution)/shard_map/weight_grads/pallas_call | solution.py:538

commit v6 on v5

--- a/solution.py
+++ b/solution.py
@@ -49,7 +49,7 @@
                  x_v, wqkv_v, wg_v, wu_v, wo_v, wd_v,
                  keep, send, rcore, chip, rx, packed, dkv_part, dkv_rx, kv_acc,
                  xhat_v, inv_v, cos_v, sin_v, br_v, dh_v, y_snd, y_rx, dh_snd, dh_rx,
-                 st_snd, st_rx, st_sum, bst_snd, bst_rx,
+                 st_snd, st_rx, st_sum, bst_snd, bst_rx, factors,
                  ld_sem, cs, cr, xs, xr, gs, gr, ps, pr, ts, tr, ss, sr, ds, dr):
     tx = lax.axis_index('tx')
     ty = lax.axis_index('ty')
@@ -296,9 +296,9 @@
     br_v[...] = mm(attn_v[...], wo_v[...])
     dh_v[...] = mm_bt(dq_v[...], wqkv_v[:, 0:q_width])
 
-    def piece_copy(r, i):
-        at = 12 + 2 * r + i - 1
-        return remote(md.at[3, i, r * piece:(r + 1) * piece], md.at[3, i, half + r * piece:half + (r + 1) * piece], gs.at[at], gr.at[at], near)
+    def piece_copy(r):
+        return remote(md.at[3, 1:3, r * piece:(r + 1) * piece], md.at[3, 1:3, half + r * piece:half + (r + 1) * piece],
+                      gs.at[12 + r], gr.at[12 + r], near)
 
     def gather_copy(k, i):
         return remote(md.at[k, i, 0:half], md.at[k, i, half:n_tok], gs.at[3 * k + i], gr.at[3 * k + i], near)
@@ -306,7 +306,7 @@
     def dact_block(k, j):
         return B_DACT_LO + 2 * k + j if k < 2 else B_DACT_HI + 2 * (k - 2) + j
 
-    def gated(k, want_act, want_grad, lo=0, hi=None):
+    def gated(k, want_act, want_grad):
         def step(r, carry):
             rows = pl.ds(pl.multiple_of(r * 16, 16), 16)
             for j in range(2):
@@ -318,16 +318,18 @@
                 cols = slice(j * BLK, (j + 1) * BLK)
                 if want_act:
                     md[k, 0, rows, cols] = (silu * up).astype(BF16)
+                if k == 3:
+                    factors[0, rows, cols] = up * sig * (1.0 + gate * (1.0 - sig))
+                    factors[1, rows, cols] = silu
                 if want_grad:
                     d_act = (chip[bd, rows].astype(F32) + rx[bd, rows].astype(F32)).astype(BF16).astype(F32)
                     md[k, 1, rows, cols] = (d_act * up * sig * (1.0 + gate * (1.0 - sig))).astype(BF16)
                     md[k, 2, rows, cols] = (d_act * silu).astype(BF16)
             return carry
 
-        lax.fori_loop(lo // 16, (half if hi is None else hi) // 16, step, 0)
-        if hi is None:
-            for i in ((0,) if want_act else ()) + ((1, 2) if want_grad else ()):
-                gather_copy(k, i).start()
+        lax.fori_loop(0, half // 16, step, 0)
+        for i in ((0,) if want_act else ()) + ((1, 2) if want_grad else ()):
+            gather_copy(k, i).start()
 
     def use_act(k):
         gather_copy(k, 0).wait_recv()
@@ -364,7 +366,6 @@
     y_copy.start()
     x_copy(9).wait_recv()
     gated(2, False, True)
-    use_grad(2)
 
     def dh_copy(r):
         return remote(dh_snd.at[r], dh_rx.at[r], ds.at[r], dr.at[r], other_ty)
@@ -376,13 +377,17 @@
 
     def piece_grad(r):
         x_copy(X_LAST + r).wait_recv()
-        gated(3, False, True, r * piece, (r + 1) * piece)
-        for i in (1, 2):
-            piece_copy(r, i).start()
+        rows = slice(r * piece, (r + 1) * piece)
+        for j in range(2):
+            cols = slice(j * BLK, (j + 1) * BLK)
+            b = dact_block(3, j)
+            d_act = (chip[b, rows].astype(F32) + rx[b, rows].astype(F32)).astype(BF16).astype(F32)
+            for i in range(2):
+                md[3, 1 + i, rows, cols] = (d_act * factors[i, rows, cols]).astype(BF16)
+        piece_copy(r).start()
 
     def piece_dh(r):
-        for i in (1, 2):
-            piece_copy(r, i).wait_recv()
+        piece_copy(r).wait_recv()
         part = both(dh_v, r) + mm_bt(both(md.at[3, 1], r), wg_v[:, 3 * CHUNK:4 * CHUNK]) + mm_bt(both(md.at[3, 2], r), wu_v[:, 3 * CHUNK:4 * CHUNK])
         part_b = part.astype(BF16)
         dh_snd[r] = part_b
@@ -390,9 +395,12 @@
         d_hat = part_b.astype(F32) * gamma_ref[...]
         sums.append((jnp.sum(d_hat, axis=1, keepdims=True), jnp.sum(d_hat * both(xhat_v, r), axis=1, keepdims=True)))
 
-    for r in range(SPLITS):
+    piece_grad(0)
+    use_grad(2)
+    for r in range(1, SPLITS):
         piece_grad(r)
-        piece_dh(r)
+        piece_dh(r - 1)
+    piece_dh(SPLITS - 1)
     cols = [jnp.concatenate([sums[r][i][:piece] for r in range(SPLITS)] + [sums[r][i][piece:] for r in range(SPLITS)], axis=0) for i in range(2)]
     stats_put(bst_snd, cols[0], cols[1])
     bwd_stats = stats_copies(bst_snd, bst_rx, 3, peers)
@@ -429,8 +437,7 @@
         for i in range(3 if k < 3 else 1):
             gather_copy(k, i).wait_send()
     for r in range(SPLITS):
-        for i in (1, 2):
-            piece_copy(r, i).wait_send()
+        piece_copy(r).wait_send()
         dh_copy(r).wait_send()
     for copy in [packed_copy, dkv_copy, y_copy, kv_copy] + fwd_stats + bwd_stats:
         copy.wait_send()
@@ -527,9 +534,9 @@
                 vm((n_tok, 512), BF16), vm((n_tok, 512), BF16), vm((n_tok, 512), F32),
                 vm(tok, F32), vm((n_tok, 128), F32), vm((n_tok, 128), F32), vm((n_tok, 128), F32), vm(tok, F32), vm(tok, F32),
                 vm(tok, BF16), vm(tok, BF16), vm((SPLITS, n_tok // SPLITS, d_local), BF16), vm((SPLITS, n_tok // SPLITS, d_local), BF16),
-                vm((8, n_tok), F32), vm((3, 8, n_tok), F32), vm((8, n_tok), F32), vm((8, n_tok), F32), vm((7, 8, n_tok), F32),
+                vm((8, n_tok), F32), vm((3, 8, n_tok), F32), vm((8, n_tok), F32), vm((8, n_tok), F32), vm((7, 8, n_tok), F32), vm((2, half, CHUNK), F32),
                 sem((12,)), sem((N_BLK,)), sem((N_BLK,)), sem((N_X,)), sem((N_X,)),
-                sem((12 + 2 * SPLITS,)), sem((12 + 2 * SPLITS,)), sem((1,)), sem((1,)), sem((4,)), sem((4,)), sem((10,)), sem((10,)),
+                sem((12 + SPLITS,)), sem((12 + SPLITS,)), sem((1,)), sem((1,)), sem((4,)), sem((4,)), sem((10,)), sem((10,)),
                 sem((SPLITS,)), sem((SPLITS,))],
             compiler_params=pltpu.CompilerParams(collective_id=0, has_side_effects=True, vmem_limit_bytes=50 * 1024 * 1024),
             name='layer',

time: 113 us -> 109 us (0.965)
  Pallas kernels: 112 us -> 108 us
    pallas_call x1, Pallas kernels: 100 us -> 97.2 us  [local_layer(): pl.pallas_call(functools.partial(layer_kernel, d_model), out_shape=[vm(to...]
where the time goes in v6:
time: 109 us
  Pallas kernels  108 us (99%)
    pallas_call x1, Pallas kernels, local_layer(): pl.pallas_call(functools.partial(layer_kernel, d_model), out_shape=[vm(to...  97.2 us
    pallas_call x1, Pallas kernels, local_layer(): pl.pallas_call(grad_kernel, out_shape=[jax.ShapeDtypeStruct(tok, BF16), j...  11.2 us

profile of v6, /device:TPU:0, one launch (start us, length us, event | category | flops | bytes accessed | tf_op | source)
XLA Modules:
  0.0 109.2 jit_solution(11170377691548893217)
XLA Ops:
  0.6 97.2 %layer.1 = (bf16[256,512]{1,0:T(8,128)(2,1)S(1)}, bf16[256,512]{1,0:T(8,128)(2,1)S(1)}, f32[1,512]{1,0:T(1,128)S(1)}, bf16[256,512]{1,0:T(8,128)(2,1)S(1)}, bf16...) custom-call(bf16[256,512]{1,0:T(8,128)(2,1)} %bitcast.6, ...), custom_call_target="tpu_custom_call" | custom-call | tf_op jit(solution)/shard_map/layer/pallas_call | solution.py:523
  97.8 11.2 %weight_grads.1 = (bf16[256,512]{1,0:T(8,128)(2,1)}, bf16[256,512]{1,0:T(8,128)(2,1)}, f32[1,512]{1,0:T(1,128)}, f32[512,1024]{1,0:T(8,128)}, f32[512,4096]{1,0:...) custom-call(bf16[256,512]{1,0:T(8,128)(2,1)S(1)} %get-tuple-element., ...), custom_call_target="tpu_custom_call" | custom-call | tf_op jit(solution)/shard_map/weight_grads/pallas_call | solution.py:545

commit v7 on v6

--- a/solution.py
+++ b/solution.py
@@ -18,7 +18,7 @@
 CHUNK = 1024
 B_DATTN, B_DACT_LO, B_QKV, B_GU, B_DACT_HI, N_BLK = 0, 2, 6, 9, 25, 29
 X_UNITS = ((0, 1), (1, 1), (2, 2), (4, 2), (6, 2), (9, 4), (13, 4), (17, 4), (21, 4), (25, 2))
-SPLITS = 4
+SPLITS = 8
 X_KV = len(X_UNITS)
 X_LAST = X_KV + 1
 N_X = X_LAST + SPLITS
@@ -44,9 +44,9 @@
     return first * cos_t - second * sin_t, second * cos_t + first * sin_t
 
 
-def layer_kernel(d_model, x_hbm, pos_ref, freq_ref, dy_hbm, gamma_ref, wq_hbm, wg_hbm, wu_hbm, wk_hbm, wv_hbm, wo_hbm, wd_hbm,
-                 y_o, dx_o, dgamma_ref, nrm_v, attn_v, md, dq_v, dkv_v, dy_v,
-                 x_v, wqkv_v, wg_v, wu_v, wo_v, wd_v,
+def layer_kernel(d_model, x_hbm, pos_hbm, freq_hbm, dy_hbm, gamma_hbm, wq_hbm, wg_hbm, wu_hbm, wk_hbm, wv_hbm, wo_hbm, wd_hbm,
+                 y_o, dx_o, dgamma_ref, nrm_t, attn_v, md, dq_v, dkv_v, dy_v, tiles,
+                 pos_ref, freq_ref, gamma_ref, nrm_v, x_v, wqkv_v, wg_v, wu_v, wo_v, wd_v,
                  keep, send, rcore, chip, rx, packed, dkv_part, dkv_rx, kv_acc,
                  xhat_v, inv_v, cos_v, sin_v, br_v, dh_v, y_snd, y_rx, dh_snd, dh_rx,
                  st_snd, st_rx, st_sum, bst_snd, bst_rx, factors,
@@ -85,6 +85,9 @@
         load(9, wg_hbm, wg_v),
         load(10, wu_hbm, wu_v),
         load(11, wd_hbm.at[d_half:2 * d_half], wd_v.at[d_half:2 * d_half]),
+        load(12, gamma_hbm, gamma_ref),
+        load(13, pos_hbm, pos_ref),
+        load(14, freq_hbm, freq_ref),
     ]
     for ld in loads[:5]:
         ld.start()
@@ -96,7 +99,6 @@
         ld.wait()
     for ld in loads[5:]:
         ld.start()
-    pl.semaphore_wait(barrier, len(peers))
 
     def remote(src, dst, send_sem, recv_sem, peer):
         return pltpu.make_async_remote_copy(src_ref=src, dst_ref=dst, send_sem=send_sem, recv_sem=recv_sem,
@@ -133,7 +135,11 @@
     def total(b):
         return chip[b].astype(F32) + rx[b].astype(F32)
 
-    issue_bwd(0, wo_v, 0)
+    part = mm_bt(dy_v[...], wo_v[0:BLK, :])
+    keep[0] = part[:half]
+    send[0] = part[half:].astype(BF16)
+    pl.semaphore_wait(barrier, len(peers))
+    core_copy(0).start()
     issue_bwd(1, wo_v, BLK)
 
     def rows_of(col_a, col_b):
@@ -177,6 +183,7 @@
     combine(B_DACT_LO + 3)
     x_copy(3).start()
 
+    loads[12].wait()
     for copy in fwd_stats:
         copy.wait_recv()
     st_sum[...] = (st_snd[...] + st_rx[0]) + (st_rx[1] + st_rx[2])
@@ -229,6 +236,10 @@
     for r in range(SPLITS):
         x_copy(X_LAST + r).start()
 
+    nrm_t[...] = nrm_v[...].T
+
+    loads[13].wait()
+    loads[14].wait()
     freq = freq_ref[...]
     for lo, at in ((0, mine), (half, other)):
         pos_col = jnp.broadcast_to(pos_ref[0:1, pl.ds(at, half)].astype(F32), (128, half)).T
@@ -296,6 +307,10 @@
     br_v[...] = mm(attn_v[...], wo_v[...])
     dh_v[...] = mm_bt(dq_v[...], wqkv_v[:, 0:q_width])
 
+    for j in range(2):
+        tiles[j] = mm(nrm_t[...], dq_v[:, j * BLK:(j + 1) * BLK])
+        tiles[2 + j] = mm_at(attn_v[:, j * BLK:(j + 1) * BLK], dy_v[...])
+
     def piece_copy(r):
         return remote(md.at[3, 1:3, r * piece:(r + 1) * piece], md.at[3, 1:3, half + r * piece:half + (r + 1) * piece],
                       gs.at[12 + r], gr.at[12 + r], near)
@@ -357,6 +372,9 @@
             dkv_v[:, 128:256] = second.astype(BF16)
             dkv_v[:, 256:512] = (dkv_part[:, 256:512].astype(F32) + dkv_rx[:, 256:512].astype(F32)).astype(BF16)
             dh_v[...] += 0.5 * mm_bt(dkv_v[...], wqkv_v[:, q_width:q_width + 512])
+            tiles[4] = mm(nrm_t[...], dkv_v[...])
+            for j in range(2):
+                tiles[5 + j] = mm_at(md[0, 0, :, j * BLK:(j + 1) * BLK], dy_v[...])
     for k in (2, 3):
         x_copy(5 + k).wait_recv()
         gated(k, True, False)
@@ -443,10 +461,10 @@
         copy.wait_send()
 
 
-def grad_kernel(y_v, dx_v, dgamma_in, nrm_v, attn_v, md, dq_v, dkv_v, dy_v,
+def grad_kernel(y_v, dx_v, dgamma_in, nrm_t, attn_v, md, dq_v, dkv_v, dy_v, tiles,
                 y_hbm, dx_hbm, dgamma_ref, dwq_hbm, dwg_hbm, dwu_hbm, dwk_hbm, dwv_hbm, dwo_hbm, dwd_hbm,
-                nrm_t, ring, out_sem, cp_sem):
-    n_tok, width = nrm_v.shape
+                ring, out_sem, cp_sem):
+    width, n_tok = nrm_t.shape
     half = n_tok // 2
     n_ring = ring.shape[0]
     core = lax.rem(lax.axis_index('tx'), 2)
@@ -457,6 +475,13 @@
     for cp in hand_out:
         cp.start()
     dgamma_ref[...] = dgamma_in[...]
+
+    ready = [(0, dwq_hbm.at[:, 0:BLK]), (1, dwq_hbm.at[:, BLK:2 * BLK]), (2, dwo_hbm.at[0:BLK, :]), (3, dwo_hbm.at[BLK:2 * BLK, :]),
+             (5, dwd_hbm.at[0:BLK, :]), (6, dwd_hbm.at[BLK:2 * BLK, :])]
+    ready = [(tiles.at[i], dst) for i, dst in ready] + [(tiles.at[4, :, 0:256], dwk_hbm), (tiles.at[4, :, 256:512], dwv_hbm)]
+    for i, (src, dst) in enumerate(ready):
+        hand_out.append(pltpu.make_async_copy(src, dst, cp_sem.at[4 + i]))
+        hand_out[-1].start()
 
     flight = []
 
@@ -472,26 +497,19 @@
             cp.start()
         flight.append(copies)
 
-    nrm_t[...] = nrm_v[...].T
-
     def columns(grads, col, out, to):
         emit(mm(nrm_t[...], grads[:, col:col + BLK]), [(0, BLK, out.at[:, to:to + BLK])])
 
     def rows(acts, col, out, to):
         emit(mm_at(acts[:, col:col + width], dy_v[...]), [(0, BLK, out.at[to:to + width, :])])
 
-    for j in range(2):
-        columns(dq_v, j * BLK, dwq_hbm, j * BLK)
     for k in range(4):
         for j in range(2):
             columns(md.at[k, 1], j * BLK, dwg_hbm, k * CHUNK + j * BLK)
         for j in range(2):
             columns(md.at[k, 2], j * BLK, dwu_hbm, k * CHUNK + j * BLK)
-        for j in range(2):
+        for j in range(2 if k > 0 else 0):
             rows(md.at[k, 0], j * BLK, dwd_hbm, k * CHUNK + j * BLK)
-    for j in range(2):
-        rows(attn_v, j * BLK, dwo_hbm, j * BLK)
-    emit(mm(nrm_t[...], dkv_v[...]), [(0, 256, dwk_hbm), (256, 512, dwv_hbm)])
     for copies in flight[-n_ring:]:
         for cp in copies:
             cp.wait()
@@ -522,11 +540,13 @@
         vm = pltpu.VMEM
         kept = pl.pallas_call(
             functools.partial(layer_kernel, d_model),
-            out_shape=[vm(tok, BF16), vm(tok, BF16), vm((1, d_local), F32), vm(tok, BF16), vm((n_tok, q_width), BF16),
-                       vm((4, 3, n_tok, CHUNK), BF16), vm((n_tok, q_width), BF16), vm((n_tok, 2 * head_dim), BF16), vm(tok, BF16)],
-            in_specs=[any_spec, vmem_spec, vmem_spec, any_spec, vmem_spec] + [any_spec] * 7,
-            out_specs=[vmem_spec] * 9,
+            out_shape=[vm(tok, BF16), vm(tok, BF16), vm((1, d_local), F32), vm((d_local, n_tok), BF16), vm((n_tok, q_width), BF16),
+                       vm((4, 3, n_tok, CHUNK), BF16), vm((n_tok, q_width), BF16), vm((n_tok, 2 * head_dim), BF16), vm(tok, BF16),
+                       vm((7, BLK, BLK), F32)],
+            in_specs=[any_spec] * 12,
+            out_specs=[vmem_spec] * 10,
             scratch_shapes=[
+                vm((1, n_tok), jnp.int32), vm((1, head_dim // 2), F32), vm((1, d_local), F32), vm(tok, BF16),
                 vm(tok, BF16), vm((d_local, q_width + 2 * head_dim), BF16), vm((d_local, d_ff), BF16), vm((d_local, d_ff), BF16),
                 vm((q_width, d_local), BF16), vm((d_ff, d_local), BF16),
                 vm((N_BLK, half, BLK), F32), vm((N_BLK, half, BLK), BF16), vm((N_BLK, half, BLK), BF16),
@@ -535,10 +555,10 @@
                 vm(tok, F32), vm((n_tok, 128), F32), vm((n_tok, 128), F32), vm((n_tok, 128), F32), vm(tok, F32), vm(tok, F32),
                 vm(tok, BF16), vm(tok, BF16), vm((SPLITS, n_tok // SPLITS, d_local), BF16), vm((SPLITS, n_tok // SPLITS, d_local), BF16),
                 vm((8, n_tok), F32), vm((3, 8, n_tok), F32), vm((8, n_tok), F32), vm((8, n_tok), F32), vm((7, 8, n_tok), F32), vm((2, half, CHUNK), F32),
-                sem((12,)), sem((N_BLK,)), sem((N_BLK,)), sem((N_X,)), sem((N_X,)),
+                sem((15,)), sem((N_BLK,)), sem((N_BLK,)), sem((N_X,)), sem((N_X,)),
                 sem((12 + SPLITS,)), sem((12 + SPLITS,)), sem((1,)), sem((1,)), sem((4,)), sem((4,)), sem((10,)), sem((10,)),
                 sem((SPLITS,)), sem((SPLITS,))],
-            compiler_params=pltpu.CompilerParams(collective_id=0, has_side_effects=True, vmem_limit_bytes=50 * 1024 * 1024),
+            compiler_params=pltpu.CompilerParams(collective_id=0, has_side_effects=True, vmem_limit_bytes=46 * 1024 * 1024),
             name='layer',
         )(x_in.reshape(tok), positions, freq, d_y.reshape(tok), ln_gamma[None], w_q, w_g, w_u, w_k, w_v, w_o, w_d)
 
@@ -546,10 +566,10 @@
             grad_kernel,
             out_shape=[jax.ShapeDtypeStruct(tok, BF16), jax.ShapeDtypeStruct(tok, BF16), jax.ShapeDtypeStruct((1, d_local), F32)]
             + [jax.ShapeDtypeStruct(w.shape, F32) for w in (w_q, w_g, w_u, w_k, w_v, w_o, w_d)],
-            in_specs=[vmem_spec] * 9,
+            in_specs=[vmem_spec] * 10,
             out_specs=[any_spec, any_spec, vmem_spec] + [any_spec] * 7,
-            scratch_shapes=[vm((d_local, n_tok), BF16), vm((12, d_local, BLK), F32), sem((12, 2)), sem((4,))],
-            compiler_params=pltpu.CompilerParams(vmem_limit_bytes=40 * 1024 * 1024),
+            scratch_shapes=[vm((10, d_local, BLK), F32), sem((10, 2)), sem((12,))],
+            compiler_params=pltpu.CompilerParams(vmem_limit_bytes=30 * 1024 * 1024),
             name='weight_grads',
         )(*kept)
         return (y_out.reshape(x_in.shape), d_x.reshape(x_in.shape), d_gamma.reshape(d_local),

time: 109 us -> 110 us (level)
  Pallas kernels: 108 us -> 110 us
where the time goes in v7:
time: 110 us
  Pallas kernels  110 us (100%)
    pallas_call x1, Pallas kernels, local_layer(): pl.pallas_call(functools.partial(layer_kernel, d_model), out_shape=[vm(to...  98.2 us
    pallas_call x1, Pallas kernels, local_layer(): pl.pallas_call(grad_kernel, out_shape=[jax.ShapeDtypeStruct(tok, BF16), j...  11.3 us

profile of v7, /device:TPU:0, one launch (start us, length us, event | category | flops | bytes accessed | tf_op | source)
XLA Modules:
  0.0 110.3 jit_solution(15256814081605194809)
XLA Ops:
  0.6 98.2 %layer.1 = (bf16[256,512]{1,0:T(8,128)(2,1)S(1)}, bf16[256,512]{1,0:T(8,128)(2,1)S(1)}, f32[1,512]{1,0:T(1,128)S(1)}, bf16[512,256]{1,0:T(8,128)(2,1)S(1)}, bf16...) custom-call(bf16[256,512]{1,0:T(8,128)(2,1)} %bitcast.6, ...), custom_call_target="tpu_custom_call" | custom-call | tf_op jit(solution)/shard_map/layer/pallas_call | solution.py:541
  98.9 11.3 %weight_grads.1 = (bf16[256,512]{1,0:T(8,128)(2,1)}, bf16[256,512]{1,0:T(8,128)(2,1)}, f32[1,512]{1,0:T(1,128)}, f32[512,1024]{1,0:T(8,128)}, f32[512,4096]{1,0:...) custom-call(bf16[256,512]{1,0:T(8,128)(2,1)S(1)} %get-tuple-element., ...), custom_call_target="tpu_custom_call" | custom-call | tf_op jit(solution)/shard_map/weight_grads/pallas_call | solution.py:565

commit v8 on v7

--- a/solution.py
+++ b/solution.py
@@ -18,7 +18,7 @@
 CHUNK = 1024
 B_DATTN, B_DACT_LO, B_QKV, B_GU, B_DACT_HI, N_BLK = 0, 2, 6, 9, 25, 29
 X_UNITS = ((0, 1), (1, 1), (2, 2), (4, 2), (6, 2), (9, 4), (13, 4), (17, 4), (21, 4), (25, 2))
-SPLITS = 8
+SPLITS = 4
 X_KV = len(X_UNITS)
 X_LAST = X_KV + 1
 N_X = X_LAST + SPLITS
@@ -463,10 +463,9 @@
 
 def grad_kernel(y_v, dx_v, dgamma_in, nrm_t, attn_v, md, dq_v, dkv_v, dy_v, tiles,
                 y_hbm, dx_hbm, dgamma_ref, dwq_hbm, dwg_hbm, dwu_hbm, dwk_hbm, dwv_hbm, dwo_hbm, dwd_hbm,
-                ring, out_sem, cp_sem):
+                ring, wide, out_sem, cp_sem):
     width, n_tok = nrm_t.shape
     half = n_tok // 2
-    n_ring = ring.shape[0]
     core = lax.rem(lax.axis_index('tx'), 2)
     mine = pl.multiple_of(core * half, half)
     other = pl.multiple_of((1 - core) * half, half)
@@ -483,36 +482,22 @@
         hand_out.append(pltpu.make_async_copy(src, dst, cp_sem.at[4 + i]))
         hand_out[-1].start()
 
-    flight = []
-
-    def emit(value, dsts):
-        t = len(flight)
-        slot = t % n_ring
-        if t >= n_ring:
-            for cp in flight[t - n_ring]:
-                cp.wait()
-        ring[slot] = value
-        copies = [pltpu.make_async_copy(ring.at[slot, :, lo:hi], dst, out_sem.at[slot, i]) for i, (lo, hi, dst) in enumerate(dsts)]
-        for cp in copies:
-            cp.start()
-        flight.append(copies)
-
-    def columns(grads, col, out, to):
-        emit(mm(nrm_t[...], grads[:, col:col + BLK]), [(0, BLK, out.at[:, to:to + BLK])])
-
-    def rows(acts, col, out, to):
-        emit(mm_at(acts[:, col:col + width], dy_v[...]), [(0, BLK, out.at[to:to + width, :])])
-
-    for k in range(4):
-        for j in range(2):
-            columns(md.at[k, 1], j * BLK, dwg_hbm, k * CHUNK + j * BLK)
-        for j in range(2):
-            columns(md.at[k, 2], j * BLK, dwu_hbm, k * CHUNK + j * BLK)
-        for j in range(2 if k > 0 else 0):
-            rows(md.at[k, 0], j * BLK, dwd_hbm, k * CHUNK + j * BLK)
-    for copies in flight[-n_ring:]:
-        for cp in copies:
-            cp.wait()
+    def put(src, dst, i):
+        hand_out.append(pltpu.make_async_copy(src, dst, out_sem.at[i]))
+        hand_out[-1].start()
+
+    for t in range(6):
+        k, j = 1 + t // 2, t % 2
+        ring[t] = mm_at(md[k, 0, :, j * BLK:(j + 1) * BLK], dy_v[...])
+        put(ring.at[t], dwd_hbm.at[k * CHUNK + j * BLK:k * CHUNK + (j + 1) * BLK, :], t)
+    n_row = 128
+    for i, (out, at) in enumerate(((dwg_hbm, 6), (dwu_hbm, 10))):
+        for k in range(4):
+            for j in range(2):
+                lo = k * CHUNK + j * BLK
+                wide[i, :, lo:lo + BLK] = mm(nrm_t[...], md[k, 1 + i, :, j * BLK:(j + 1) * BLK])
+        for r in range(width // n_row):
+            put(wide.at[i, r * n_row:(r + 1) * n_row], out.at[r * n_row:(r + 1) * n_row], at + r)
     for cp in hand_out:
         cp.wait()
 
@@ -568,7 +553,7 @@
             + [jax.ShapeDtypeStruct(w.shape, F32) for w in (w_q, w_g, w_u, w_k, w_v, w_o, w_d)],
             in_specs=[vmem_spec] * 10,
             out_specs=[any_spec, any_spec, vmem_spec] + [any_spec] * 7,
-            scratch_shapes=[vm((10, d_local, BLK), F32), sem((10, 2)), sem((12,))],
+            scratch_shapes=[vm((6, d_local, BLK), F32), vm((2, d_local, d_ff), F32), sem((14,)), sem((12,))],
             compiler_params=pltpu.CompilerParams(vmem_limit_bytes=30 * 1024 * 1024),
             name='weight_grads',
         )(*kept)

time: 110 us -> 108 us (0.982)
  Pallas kernels: 110 us -> 107 us
    pallas_call x1, Pallas kernels: 98.2 us -> 96.5 us  [local_layer(): pl.pallas_call(functools.partial(layer_kernel, d_model), out_shape=[vm(to...]
where the time goes in v8:
time: 108 us
  Pallas kernels  107 us (99%)
    pallas_call x1, Pallas kernels, local_layer(): pl.pallas_call(functools.partial(layer_kernel, d_model), out_shape=[vm(to...  96.5 us
    pallas_call x1, Pallas kernels, local_layer(): pl.pallas_call(grad_kernel, out_shape=[jax.ShapeDtypeStruct(tok, BF16), j...  11 us

profile of v8, /device:TPU:0, one launch (start us, length us, event | category | flops | bytes accessed | tf_op | source)
XLA Modules:
  0.0 108.3 jit_solution(11148213917830450166)
XLA Ops:
  0.6 96.5 %layer.1 = (bf16[256,512]{1,0:T(8,128)(2,1)S(1)}, bf16[256,512]{1,0:T(8,128)(2,1)S(1)}, f32[1,512]{1,0:T(1,128)S(1)}, bf16[512,256]{1,0:T(8,128)(2,1)S(1)}, bf16...) custom-call(bf16[256,512]{1,0:T(8,128)(2,1)} %bitcast.6, ...), custom_call_target="tpu_custom_call" | custom-call | tf_op jit(solution)/shard_map/layer/pallas_call | solution.py:526
  97.1 11.0 %weight_grads.1 = (bf16[256,512]{1,0:T(8,128)(2,1)}, bf16[256,512]{1,0:T(8,128)(2,1)}, f32[1,512]{1,0:T(1,128)}, f32[512,1024]{1,0:T(8,128)}, f32[512,4096]{1,0:...) custom-call(bf16[256,512]{1,0:T(8,128)(2,1)S(1)} %get-tuple-element., ...), custom_call_target="tpu_custom_call" | custom-call | tf_op jit(solution)/shard_map/weight_grads/pallas_call | solution.py:550

commit v9 on v8

--- a/solution.py
+++ b/solution.py
@@ -18,7 +18,8 @@
 CHUNK = 1024
 B_DATTN, B_DACT_LO, B_QKV, B_GU, B_DACT_HI, N_BLK = 0, 2, 6, 9, 25, 29
 X_UNITS = ((0, 1), (1, 1), (2, 2), (4, 2), (6, 2), (9, 4), (13, 4), (17, 4), (21, 4), (25, 2))
-SPLITS = 4
+PIECES = ((0, 16), (16, 32), (48, 32), (80, 32), (112, 16))
+SPLITS = len(PIECES)
 X_KV = len(X_UNITS)
 X_LAST = X_KV + 1
 N_X = X_LAST + SPLITS
@@ -66,7 +67,6 @@
     head_dim = 256
     q_width = wo_v.shape[0]
     heads = q_width // head_dim
-    piece = half // SPLITS
 
     def load(i, src, dst):
         return pltpu.make_async_copy(src, dst, ld_sem.at[i])
@@ -75,7 +75,7 @@
     loads = [
         load(0, dy_hbm.at[pl.ds(mine, half)], dy_v.at[0:half]),
         load(1, dy_hbm.at[pl.ds(other, half)], dy_v.at[half:n_tok]),
-        load(2, wo_hbm, wo_v),
+        load(2, wo_hbm.at[0:BLK], wo_v.at[0:BLK]),
         load(3, x_hbm.at[pl.ds(mine, half)], x_v.at[0:half]),
         load(4, x_hbm.at[pl.ds(other, half)], x_v.at[half:n_tok]),
         load(5, wd_hbm.at[0:d_half], wd_v.at[0:d_half]),
@@ -88,16 +88,17 @@
         load(12, gamma_hbm, gamma_ref),
         load(13, pos_hbm, pos_ref),
         load(14, freq_hbm, freq_ref),
+        load(15, wo_hbm.at[BLK:q_width], wo_v.at[BLK:q_width]),
     ]
-    for ld in loads[:5]:
-        ld.start()
+    for i in (0, 1, 2, 15, 3, 4):
+        loads[i].start()
 
     barrier = pltpu.get_barrier_semaphore()
     for peer in peers:
         pl.semaphore_signal(barrier, inc=1, device_id=peer, device_id_type=MESH)
     for ld in loads[:3]:
         ld.wait()
-    for ld in loads[5:]:
+    for ld in loads[5:15]:
         ld.start()
 
     def remote(src, dst, send_sem, recv_sem, peer):
@@ -109,7 +110,7 @@
 
     def x_copy(u):
         if u >= X_LAST:
-            rows = pl.ds((u - X_LAST) * piece, piece)
+            rows = pl.ds(*PIECES[u - X_LAST])
             return remote(chip.at[pl.ds(N_BLK - 2, 2), rows], rx.at[pl.ds(N_BLK - 2, 2), rows], xs.at[u], xr.at[u], across)
         if u == X_KV:
             cols = pl.ds(pl.multiple_of(ty * head_dim, head_dim), head_dim)
@@ -140,6 +141,7 @@
     send[0] = part[half:].astype(BF16)
     pl.semaphore_wait(barrier, len(peers))
     core_copy(0).start()
+    loads[15].wait()
     issue_bwd(1, wo_v, BLK)
 
     def rows_of(col_a, col_b):
@@ -312,8 +314,8 @@
         tiles[2 + j] = mm_at(attn_v[:, j * BLK:(j + 1) * BLK], dy_v[...])
 
     def piece_copy(r):
-        return remote(md.at[3, 1:3, r * piece:(r + 1) * piece], md.at[3, 1:3, half + r * piece:half + (r + 1) * piece],
-                      gs.at[12 + r], gr.at[12 + r], near)
+        lo, size = PIECES[r]
+        return remote(md.at[3, 1:3, lo:lo + size], md.at[3, 1:3, half + lo:half + lo + size], gs.at[12 + r], gr.at[12 + r], near)
 
     def gather_copy(k, i):
         return remote(md.at[k, i, 0:half], md.at[k, i, half:n_tok], gs.at[3 * k + i], gr.at[3 * k + i], near)
@@ -386,16 +388,18 @@
     gated(2, False, True)
 
     def dh_copy(r):
-        return remote(dh_snd.at[r], dh_rx.at[r], ds.at[r], dr.at[r], other_ty)
+        at = pl.ds(2 * PIECES[r][0], 2 * PIECES[r][1])
+        return remote(dh_snd.at[at], dh_rx.at[at], ds.at[r], dr.at[r], other_ty)
 
     def both(ref, r):
-        return jnp.concatenate([ref[r * piece:(r + 1) * piece], ref[half + r * piece:half + (r + 1) * piece]], axis=0)
+        lo, size = PIECES[r]
+        return jnp.concatenate([ref[lo:lo + size], ref[half + lo:half + lo + size]], axis=0)
 
     sums = []
 
     def piece_grad(r):
         x_copy(X_LAST + r).wait_recv()
-        rows = slice(r * piece, (r + 1) * piece)
+        rows = slice(PIECES[r][0], PIECES[r][0] + PIECES[r][1])
         for j in range(2):
             cols = slice(j * BLK, (j + 1) * BLK)
             b = dact_block(3, j)
@@ -408,7 +412,7 @@
         piece_copy(r).wait_recv()
         part = both(dh_v, r) + mm_bt(both(md.at[3, 1], r), wg_v[:, 3 * CHUNK:4 * CHUNK]) + mm_bt(both(md.at[3, 2], r), wu_v[:, 3 * CHUNK:4 * CHUNK])
         part_b = part.astype(BF16)
-        dh_snd[r] = part_b
+        dh_snd[2 * PIECES[r][0]:2 * (PIECES[r][0] + PIECES[r][1])] = part_b
         dh_copy(r).start()
         d_hat = part_b.astype(F32) * gamma_ref[...]
         sums.append((jnp.sum(d_hat, axis=1, keepdims=True), jnp.sum(d_hat * both(xhat_v, r), axis=1, keepdims=True)))
@@ -419,7 +423,7 @@
         piece_grad(r)
         piece_dh(r - 1)
     piece_dh(SPLITS - 1)
-    cols = [jnp.concatenate([sums[r][i][:piece] for r in range(SPLITS)] + [sums[r][i][piece:] for r in range(SPLITS)], axis=0) for i in range(2)]
+    cols = [jnp.concatenate([sums[r][i][:PIECES[r][1]] for r in range(SPLITS)] + [sums[r][i][PIECES[r][1]:] for r in range(SPLITS)], axis=0) for i in range(2)]
     stats_put(bst_snd, cols[0], cols[1])
     bwd_stats = stats_copies(bst_snd, bst_rx, 3, peers)
     for copy in bwd_stats:
@@ -428,13 +432,29 @@
     y_copy.wait_recv()
     y_o[...] = (x_v[...].astype(F32) + (y_snd[...].astype(F32) + y_rx[...].astype(F32))).astype(BF16)
 
+    def drain(b, carry):
+        core_copy(b).wait_send()
+        return carry
+
+    lax.fori_loop(0, N_BLK, drain, 0)
+    for u in range(N_X):
+        x_copy(u).wait_send()
+    for k in range(4):
+        for i in range(3 if k < 3 else 1):
+            gather_copy(k, i).wait_send()
+    for r in range(SPLITS):
+        piece_copy(r).wait_send()
+    for copy in [packed_copy, dkv_copy, y_copy, kv_copy] + fwd_stats:
+        copy.wait_send()
+
     d_gamma = jnp.zeros_like(dgamma_ref)
     for r in range(SPLITS):
         dh_copy(r).wait_recv()
-        d_nrm = dh_snd[r].astype(F32) + dh_rx[r].astype(F32)
+        lo, size = PIECES[r]
+        d_nrm = dh_snd[2 * lo:2 * (lo + size)].astype(F32) + dh_rx[2 * lo:2 * (lo + size)].astype(F32)
         d_gamma = d_gamma + jnp.sum(d_nrm * both(xhat_v, r), axis=0, keepdims=True)
-        dh_v[r * piece:(r + 1) * piece] = d_nrm[:piece]
-        dh_v[half + r * piece:half + (r + 1) * piece] = d_nrm[piece:]
+        dh_v[lo:lo + size] = d_nrm[:size]
+        dh_v[half + lo:half + lo + size] = d_nrm[size:]
     dgamma_ref[...] = d_gamma
     for copy in bwd_stats:
         copy.wait_recv()
@@ -444,25 +464,14 @@
     d_x = dy_v[...].astype(F32) + inv_v[:, 0:1] * (d_hat - sum_d / d_model - xhat_v[...] * (sum_dx / d_model))
     dx_o[...] = d_x.astype(BF16)
 
-    def drain(b, carry):
-        core_copy(b).wait_send()
-        return carry
-
-    lax.fori_loop(0, N_BLK, drain, 0)
-    for u in range(N_X):
-        x_copy(u).wait_send()
-    for k in range(4):
-        for i in range(3 if k < 3 else 1):
-            gather_copy(k, i).wait_send()
     for r in range(SPLITS):
-        piece_copy(r).wait_send()
         dh_copy(r).wait_send()
-    for copy in [packed_copy, dkv_copy, y_copy, kv_copy] + fwd_stats + bwd_stats:
+    for copy in bwd_stats:
         copy.wait_send()
 
 
 def grad_kernel(y_v, dx_v, dgamma_in, nrm_t, attn_v, md, dq_v, dkv_v, dy_v, tiles,
-                y_hbm, dx_hbm, dgamma_ref, dwq_hbm, dwg_hbm, dwu_hbm, dwk_hbm, dwv_hbm, dwo_hbm, dwd_hbm,
+                y_hbm, dx_hbm, dgamma_hbm, dwq_hbm, dwg_hbm, dwu_hbm, dwk_hbm, dwv_hbm, dwo_hbm, dwd_hbm,
                 ring, wide, out_sem, cp_sem):
     width, n_tok = nrm_t.shape
     half = n_tok // 2
@@ -473,7 +482,8 @@
                 for i, (src, dst, lo, at) in enumerate(((y_v, y_hbm, 0, mine), (y_v, y_hbm, half, other), (dx_v, dx_hbm, 0, mine), (dx_v, dx_hbm, half, other)))]
     for cp in hand_out:
         cp.start()
-    dgamma_ref[...] = dgamma_in[...]
+    hand_out.append(pltpu.make_async_copy(dgamma_in, dgamma_hbm, cp_sem.at[12]))
+    hand_out[-1].start()
 
     ready = [(0, dwq_hbm.at[:, 0:BLK]), (1, dwq_hbm.at[:, BLK:2 * BLK]), (2, dwo_hbm.at[0:BLK, :]), (3, dwo_hbm.at[BLK:2 * BLK, :]),
              (5, dwd_hbm.at[0:BLK, :]), (6, dwd_hbm.at[BLK:2 * BLK, :])]
@@ -538,9 +548,9 @@
                 vm((N_BLK, half, BLK), BF16), vm((N_BLK, half, BLK), BF16), vm((n_tok, 2 * q_width + 2 * head_dim), BF16),
                 vm((n_tok, 512), BF16), vm((n_tok, 512), BF16), vm((n_tok, 512), F32),
                 vm(tok, F32), vm((n_tok, 128), F32), vm((n_tok, 128), F32), vm((n_tok, 128), F32), vm(tok, F32), vm(tok, F32),
-                vm(tok, BF16), vm(tok, BF16), vm((SPLITS, n_tok // SPLITS, d_local), BF16), vm((SPLITS, n_tok // SPLITS, d_local), BF16),
+                vm(tok, BF16), vm(tok, BF16), vm(tok, BF16), vm(tok, BF16),
                 vm((8, n_tok), F32), vm((3, 8, n_tok), F32), vm((8, n_tok), F32), vm((8, n_tok), F32), vm((7, 8, n_tok), F32), vm((2, half, CHUNK), F32),
-                sem((15,)), sem((N_BLK,)), sem((N_BLK,)), sem((N_X,)), sem((N_X,)),
+                sem((16,)), sem((N_BLK,)), sem((N_BLK,)), sem((N_X,)), sem((N_X,)),
                 sem((12 + SPLITS,)), sem((12 + SPLITS,)), sem((1,)), sem((1,)), sem((4,)), sem((4,)), sem((10,)), sem((10,)),
                 sem((SPLITS,)), sem((SPLITS,))],
             compiler_params=pltpu.CompilerParams(collective_id=0, has_side_effects=True, vmem_limit_bytes=46 * 1024 * 1024),
@@ -552,8 +562,8 @@
             out_shape=[jax.ShapeDtypeStruct(tok, BF16), jax.ShapeDtypeStruct(tok, BF16), jax.ShapeDtypeStruct((1, d_local), F32)]
             + [jax.ShapeDtypeStruct(w.shape, F32) for w in (w_q, w_g, w_u, w_k, w_v, w_o, w_d)],
             in_specs=[vmem_spec] * 10,
-            out_specs=[any_spec, any_spec, vmem_spec] + [any_spec] * 7,
-            scratch_shapes=[vm((6, d_local, BLK), F32), vm((2, d_local, d_ff), F32), sem((14,)), sem((12,))],
+            out_specs=[any_spec] * 10,
+            scratch_shapes=[vm((6, d_local, BLK), F32), vm((2, d_local, d_ff), F32), sem((14,)), sem((13,))],
             compiler_params=pltpu.CompilerParams(vmem_limit_bytes=30 * 1024 * 1024),
             name='weight_grads',
         )(*kept)

time: 108 us -> 107 us (level)
  no operation moved by 1% of the time
where the time goes in v9:
time: 107 us
  Pallas kernels  107 us (100%)
    pallas_call x1, Pallas kernels, local_layer(): pl.pallas_call(functools.partial(layer_kernel, d_model), out_shape=[vm(to...  96.2 us
    pallas_call x1, Pallas kernels, local_layer(): pl.pallas_call(grad_kernel, out_shape=[jax.ShapeDtypeStruct(tok, BF16), j...  10.4 us

profile of v9, /device:TPU:0, one launch (start us, length us, event | category | flops | bytes accessed | tf_op | source)
XLA Modules:
  0.0 107.4 jit_solution(12589423612875554947)
XLA Ops:
  0.6 96.2 %layer.1 = (bf16[256,512]{1,0:T(8,128)(2,1)S(1)}, bf16[256,512]{1,0:T(8,128)(2,1)S(1)}, f32[1,512]{1,0:T(1,128)S(1)}, bf16[512,256]{1,0:T(8,128)(2,1)S(1)}, bf16...) custom-call(bf16[256,512]{1,0:T(8,128)(2,1)} %bitcast.6, ...), custom_call_target="tpu_custom_call" | custom-call | tf_op jit(solution)/shard_map/layer/pallas_call | solution.py:536
  96.8 10.4 %weight_grads.1 = (bf16[256,512]{1,0:T(8,128)(2,1)}, bf16[256,512]{1,0:T(8,128)(2,1)}, f32[1,512]{1,0:T(1,128)}, f32[512,1024]{1,0:T(8,128)}, f32[512,4096]{1,0:...) custom-call(bf16[256,512]{1,0:T(8,128)(2,1)S(1)} %get-tuple-element., ...), custom_call_target="tpu_custom_call" | custom-call | tf_op jit(solution)/shard_map/weight_grads/pallas_call | solution.py:560

commit v10 on v9

--- a/solution.py
+++ b/solution.py
@@ -16,8 +16,8 @@
 
 BLK = 512
 CHUNK = 1024
-B_DATTN, B_DACT_LO, B_QKV, B_GU, B_DACT_HI, N_BLK = 0, 2, 6, 9, 25, 29
-X_UNITS = ((0, 1), (1, 1), (2, 2), (4, 2), (6, 2), (9, 4), (13, 4), (17, 4), (21, 4), (25, 2))
+B_DATTN, B_DACT_LO, B_QKV, B_GU, B_DACT_HI, N_BLK = 0, 2, 4, 7, 23, 29
+X_UNITS = ((0, 1), (1, 1), (2, 2), (4, 2), (7, 4), (11, 4), (15, 4), (19, 4), (23, 2), (25, 2))
 PIECES = ((0, 16), (16, 32), (48, 32), (80, 32), (112, 16))
 SPLITS = len(PIECES)
 X_KV = len(X_UNITS)
@@ -71,26 +71,25 @@
     def load(i, src, dst):
         return pltpu.make_async_copy(src, dst, ld_sem.at[i])
 
-    d_half = wd_v.shape[0] // 2
     loads = [
         load(0, dy_hbm.at[pl.ds(mine, half)], dy_v.at[0:half]),
         load(1, dy_hbm.at[pl.ds(other, half)], dy_v.at[half:n_tok]),
         load(2, wo_hbm.at[0:BLK], wo_v.at[0:BLK]),
         load(3, x_hbm.at[pl.ds(mine, half)], x_v.at[0:half]),
         load(4, x_hbm.at[pl.ds(other, half)], x_v.at[half:n_tok]),
-        load(5, wd_hbm.at[0:d_half], wd_v.at[0:d_half]),
+        load(5, wd_hbm.at[0:CHUNK], wd_v.at[0:CHUNK]),
         load(6, wq_hbm, wqkv_v.at[:, 0:q_width]),
         load(7, wk_hbm, wqkv_v.at[:, q_width:q_width + head_dim]),
         load(8, wv_hbm, wqkv_v.at[:, q_width + head_dim:q_width + 2 * head_dim]),
         load(9, wg_hbm, wg_v),
         load(10, wu_hbm, wu_v),
-        load(11, wd_hbm.at[d_half:2 * d_half], wd_v.at[d_half:2 * d_half]),
+        load(11, wd_hbm.at[CHUNK:4 * CHUNK], wd_v.at[CHUNK:4 * CHUNK]),
         load(12, gamma_hbm, gamma_ref),
         load(13, pos_hbm, pos_ref),
         load(14, freq_hbm, freq_ref),
         load(15, wo_hbm.at[BLK:q_width], wo_v.at[BLK:q_width]),
     ]
-    for i in (0, 1, 2, 15, 3, 4):
+    for i in (0, 1, 2, 15, 3, 4, 5):
         loads[i].start()
 
     barrier = pltpu.get_barrier_semaphore()
@@ -98,8 +97,8 @@
         pl.semaphore_signal(barrier, inc=1, device_id=peer, device_id_type=MESH)
     for ld in loads[:3]:
         ld.wait()
-    for ld in loads[5:15]:
-        ld.start()
+    for i in (12, 6, 7, 8):
+        loads[i].start()
 
     def remote(src, dst, send_sem, recv_sem, peer):
         return pltpu.make_async_remote_copy(src_ref=src, dst_ref=dst, send_sem=send_sem, recv_sem=recv_sem,
@@ -164,6 +163,8 @@
 
     loads[3].wait()
     loads[4].wait()
+    for i in (9, 10, 11, 13, 14):
+        loads[i].start()
     x_f = x_v[...].astype(F32)
     stats_put(st_snd, jnp.sum(x_f, axis=1, keepdims=True), jnp.sum(x_f * x_f, axis=1, keepdims=True))
     fwd_stats = stats_copies(st_snd, st_rx, 0, (near, across, far))
@@ -176,14 +177,11 @@
     x_copy(1).start()
 
     loads[5].wait()
-    for i in range(4):
+    for i in range(2):
         issue_bwd(B_DACT_LO + i, wd_v, i * BLK)
-        if i >= 1:
-            combine(B_DACT_LO + i - 1)
-        if i == 2:
-            x_copy(2).start()
-    combine(B_DACT_LO + 3)
-    x_copy(3).start()
+    for i in range(2):
+        combine(B_DACT_LO + i)
+    x_copy(2).start()
 
     loads[12].wait()
     for copy in fwd_stats:
@@ -205,7 +203,7 @@
         combine(B_QKV + i)
         if i == 2:
             x_copy(X_KV).start()
-    x_copy(4).start()
+    x_copy(3).start()
 
     loads[9].wait()
     loads[10].wait()
@@ -222,19 +220,19 @@
 
         lax.fori_loop(0, 2, gu_issue, 0)
         lax.fori_loop(0, 4, gu_combine, 0)
-        x_copy(5 + k).start()
+        x_copy(4 + k).start()
 
     loads[11].wait()
 
     def hi_issue(j, carry):
-        issue_bwd(B_DACT_HI + j, wd_v, pl.multiple_of(d_half + j * BLK, BLK))
+        issue_bwd(B_DACT_HI + j, wd_v, pl.multiple_of(CHUNK + j * BLK, BLK))
         return carry
 
-    lax.fori_loop(0, 4, hi_issue, 0)
-    for j in range(4):
+    lax.fori_loop(0, 6, hi_issue, 0)
+    for j in range(6):
         combine(B_DACT_HI + j)
-        if j == 1:
-            x_copy(9).start()
+        if j == 1 or j == 3:
+            x_copy(8 + j // 2).start()
     for r in range(SPLITS):
         x_copy(X_LAST + r).start()
 
@@ -254,7 +252,7 @@
     x_copy(1).wait_recv()
     for j in range(2):
         packed[0:half, q_width + 512 + j * BLK:q_width + 512 + (j + 1) * BLK] = total(B_DATTN + j).astype(BF16)
-    x_copy(4).wait_recv()
+    x_copy(3).wait_recv()
     cos_h, sin_h = cos_v[0:half], sin_v[0:half]
     for j in range(2):
         blk = total(B_QKV + j)
@@ -321,7 +319,7 @@
         return remote(md.at[k, i, 0:half], md.at[k, i, half:n_tok], gs.at[3 * k + i], gr.at[3 * k + i], near)
 
     def dact_block(k, j):
-        return B_DACT_LO + 2 * k + j if k < 2 else B_DACT_HI + 2 * (k - 2) + j
+        return B_DACT_LO + j if k == 0 else B_DACT_HI + 2 * (k - 1) + j
 
     def gated(k, want_act, want_grad):
         def step(r, carry):
@@ -359,13 +357,12 @@
                       + mm_bt(md[k, 2], wu_v[:, k * CHUNK:(k + 1) * CHUNK]))
 
     x_copy(2).wait_recv()
-    x_copy(3).wait_recv()
-    for k in range(2):
-        x_copy(5 + k).wait_recv()
-        gated(k, True, True)
+    for k in range(4):
+        x_copy(4 + k).wait_recv()
+        gated(k, True, k == 0)
         use_act(k)
-        use_grad(k)
         if k == 0:
+            use_grad(0)
             dkv_copy.wait_recv()
             d_k = dkv_part[:, 0:256].astype(F32) + dkv_rx[:, 0:256].astype(F32)
             d_k = d_k.astype(BF16).astype(F32)
@@ -377,13 +374,12 @@
             tiles[4] = mm(nrm_t[...], dkv_v[...])
             for j in range(2):
                 tiles[5 + j] = mm_at(md[0, 0, :, j * BLK:(j + 1) * BLK], dy_v[...])
-    for k in (2, 3):
-        x_copy(5 + k).wait_recv()
-        gated(k, True, False)
-        use_act(k)
     y_snd[...] = br_v[...].astype(BF16)
     y_copy = remote(y_snd, y_rx, ts.at[1], tr.at[1], other_ty)
     y_copy.start()
+    x_copy(8).wait_recv()
+    gated(1, False, True)
+    use_grad(1)
     x_copy(9).wait_recv()
     gated(2, False, True)
 

time: 107 us -> 107 us (level)
  no operation moved by 1% of the time
where the time goes in v10:
time: 107 us
  Pallas kernels  107 us (100%)
    pallas_call x1, Pallas kernels, local_layer(): pl.pallas_call(functools.partial(layer_kernel, d_model), out_shape=[vm(to...  96.1 us
    pallas_call x1, Pallas kernels, local_layer(): pl.pallas_call(grad_kernel, out_shape=[jax.ShapeDtypeStruct(tok, BF16), j...  10.4 us

profile of v10, /device:TPU:0, one launch (start us, length us, event | category | flops | bytes accessed | tf_op | source)
XLA Modules:
  0.0 107.3 jit_solution(4373754821374902723)
XLA Ops:
  0.6 96.1 %layer.1 = (bf16[256,512]{1,0:T(8,128)(2,1)S(1)}, bf16[256,512]{1,0:T(8,128)(2,1)S(1)}, f32[1,512]{1,0:T(1,128)S(1)}, bf16[512,256]{1,0:T(8,128)(2,1)S(1)}, bf16...) custom-call(bf16[256,512]{1,0:T(8,128)(2,1)} %bitcast.6, ...), custom_call_target="tpu_custom_call" | custom-call | tf_op jit(solution)/shard_map/layer/pallas_call | solution.py:532
  96.8 10.4 %weight_grads.1 = (bf16[256,512]{1,0:T(8,128)(2,1)}, bf16[256,512]{1,0:T(8,128)(2,1)}, f32[1,512]{1,0:T(1,128)}, f32[512,1024]{1,0:T(8,128)}, f32[512,4096]{1,0:...) custom-call(bf16[256,512]{1,0:T(8,128)(2,1)S(1)} %get-tuple-element., ...), custom_call_target="tpu_custom_call" | custom-call | tf_op jit(solution)/shard_map/weight_grads/pallas_call | solution.py:556

commit v11 on v10

--- a/solution.py
+++ b/solution.py
@@ -20,6 +20,7 @@
 X_UNITS = ((0, 1), (1, 1), (2, 2), (4, 2), (7, 4), (11, 4), (15, 4), (19, 4), (23, 2), (25, 2))
 PIECES = ((0, 16), (16, 32), (48, 32), (80, 32), (112, 16))
 SPLITS = len(PIECES)
+EARLY = 128
 X_KV = len(X_UNITS)
 X_LAST = X_KV + 1
 N_X = X_LAST + SPLITS
@@ -51,7 +52,7 @@
                  keep, send, rcore, chip, rx, packed, dkv_part, dkv_rx, kv_acc,
                  xhat_v, inv_v, cos_v, sin_v, br_v, dh_v, y_snd, y_rx, dh_snd, dh_rx,
                  st_snd, st_rx, st_sum, bst_snd, bst_rx, factors,
-                 ld_sem, cs, cr, xs, xr, gs, gr, ps, pr, ts, tr, ss, sr, ds, dr):
+                 ld_sem, cs, cr, xs, xr, gs, gr, ps, pr, ts, tr, ss, sr, ds, dr, early_snd, early_rx, es, er):
     tx = lax.axis_index('tx')
     ty = lax.axis_index('ty')
     core = lax.rem(tx, 2)
@@ -114,6 +115,8 @@
         if u == X_KV:
             cols = pl.ds(pl.multiple_of(ty * head_dim, head_dim), head_dim)
             return remote(chip.at[B_QKV + 2, :, cols], rx.at[B_QKV + 2, :, cols], xs.at[u], xr.at[u], across)
+        if u == 0:
+            return remote(chip.at[0, :, EARLY:BLK], rx.at[0, :, EARLY:BLK], xs.at[u], xr.at[u], across)
         start, count = X_UNITS[u]
         return remote(chip.at[pl.ds(start, count)], rx.at[pl.ds(start, count)], xs.at[u], xr.at[u], across)
 
@@ -138,8 +141,13 @@
     part = mm_bt(dy_v[...], wo_v[0:BLK, :])
     keep[0] = part[:half]
     send[0] = part[half:].astype(BF16)
+    early_snd[...] = part[:, 0:EARLY].astype(BF16)
     pl.semaphore_wait(barrier, len(peers))
+    early = [remote(early_snd.at[0:half], early_rx.at[0], es.at[0], er.at[0], across),
+             remote(early_snd.at[half:n_tok], early_rx.at[1], es.at[1], er.at[1], far)]
     core_copy(0).start()
+    for copy in early:
+        copy.start()
     loads[15].wait()
     issue_bwd(1, wo_v, BLK)
 
@@ -250,6 +258,9 @@
     packed_copy = remote(packed.at[0:half], packed.at[half:n_tok], ps.at[0], pr.at[0], near)
     x_copy(0).wait_recv()
     x_copy(1).wait_recv()
+    for copy in early:
+        copy.wait_recv()
+    rx[0, :, 0:EARLY] = (early_rx[0].astype(F32) + early_rx[1].astype(F32)).astype(BF16)
     for j in range(2):
         packed[0:half, q_width + 512 + j * BLK:q_width + 512 + (j + 1) * BLK] = total(B_DATTN + j).astype(BF16)
     x_copy(3).wait_recv()
@@ -440,24 +451,25 @@
             gather_copy(k, i).wait_send()
     for r in range(SPLITS):
         piece_copy(r).wait_send()
-    for copy in [packed_copy, dkv_copy, y_copy, kv_copy] + fwd_stats:
+    for copy in [packed_copy, dkv_copy, y_copy, kv_copy] + early + fwd_stats:
         copy.wait_send()
 
+    br_v[...] = inv_v[:, 0:1] * xhat_v[...]
     d_gamma = jnp.zeros_like(dgamma_ref)
     for r in range(SPLITS):
         dh_copy(r).wait_recv()
         lo, size = PIECES[r]
         d_nrm = dh_snd[2 * lo:2 * (lo + size)].astype(F32) + dh_rx[2 * lo:2 * (lo + size)].astype(F32)
         d_gamma = d_gamma + jnp.sum(d_nrm * both(xhat_v, r), axis=0, keepdims=True)
-        dh_v[lo:lo + size] = d_nrm[:size]
-        dh_v[half + lo:half + lo + size] = d_nrm[size:]
+        base = both(dy_v, r).astype(F32) + both(inv_v, r)[:, 0:1] * (d_nrm * gamma_ref[...])
+        dh_v[lo:lo + size] = base[:size]
+        dh_v[half + lo:half + lo + size] = base[size:]
     dgamma_ref[...] = d_gamma
     for copy in bwd_stats:
         copy.wait_recv()
     st_sum[...] = ((bst_snd[...] + bst_rx[0]) + (bst_rx[1] + bst_rx[2])) + ((bst_rx[3] + bst_rx[4]) + (bst_rx[5] + bst_rx[6]))
     sum_d, sum_dx = stats_columns(st_sum)
-    d_hat = dh_v[...] * gamma_ref[...]
-    d_x = dy_v[...].astype(F32) + inv_v[:, 0:1] * (d_hat - sum_d / d_model - xhat_v[...] * (sum_dx / d_model))
+    d_x = dh_v[...] - inv_v[:, 0:1] * (sum_d / d_model) - br_v[...] * (sum_dx / d_model)
     dx_o[...] = d_x.astype(BF16)
 
     for r in range(SPLITS):
@@ -548,7 +560,7 @@
                 vm((8, n_tok), F32), vm((3, 8, n_tok), F32), vm((8, n_tok), F32), vm((8, n_tok), F32), vm((7, 8, n_tok), F32), vm((2, half, CHUNK), F32),
                 sem((16,)), sem((N_BLK,)), sem((N_BLK,)), sem((N_X,)), sem((N_X,)),
                 sem((12 + SPLITS,)), sem((12 + SPLITS,)), sem((1,)), sem((1,)), sem((4,)), sem((4,)), sem((10,)), sem((10,)),
-                sem((SPLITS,)), sem((SPLITS,))],
+                sem((SPLITS,)), sem((SPLITS,)), vm((n_tok, EARLY), BF16), vm((2, half, EARLY), BF16), sem((2,)), sem((2,))],
             compiler_params=pltpu.CompilerParams(collective_id=0, has_side_effects=True, vmem_limit_bytes=46 * 1024 * 1024),
             name='layer',
         )(x_in.reshape(tok), positions, freq, d_y.reshape(tok), ln_gamma[None], w_q, w_g, w_u, w_k, w_v, w_o, w_d)

time: 107 us -> 107 us (level)
  no operation moved by 1% of the time
where the time goes in v11:
time: 107 us
  Pallas kernels  106 us (99%)
    pallas_call x1, Pallas kernels, local_layer(): pl.pallas_call(functools.partial(layer_kernel, d_model), out_shape=[vm(to...  95.7 us
    pallas_call x1, Pallas kernels, local_layer(): pl.pallas_call(grad_kernel, out_shape=[jax.ShapeDtypeStruct(tok, BF16), j...  10.4 us

profile of v11, /device:TPU:0, one launch (start us, length us, event | category | flops | bytes accessed | tf_op | source)
XLA Modules:
  0.0 106.9 jit_solution(10857289996541941151)
XLA Ops:
  0.6 95.7 %layer.1 = (bf16[256,512]{1,0:T(8,128)(2,1)S(1)}, bf16[256,512]{1,0:T(8,128)(2,1)S(1)}, f32[1,512]{1,0:T(1,128)S(1)}, bf16[512,256]{1,0:T(8,128)(2,1)S(1)}, bf16...) custom-call(bf16[256,512]{1,0:T(8,128)(2,1)} %bitcast.6, ...), custom_call_target="tpu_custom_call" | custom-call | tf_op jit(solution)/shard_map/layer/pallas_call | solution.py:544
  96.4 10.4 %weight_grads.1 = (bf16[256,512]{1,0:T(8,128)(2,1)}, bf16[256,512]{1,0:T(8,128)(2,1)}, f32[1,512]{1,0:T(1,128)}, f32[512,1024]{1,0:T(8,128)}, f32[512,4096]{1,0:...) custom-call(bf16[256,512]{1,0:T(8,128)(2,1)S(1)} %get-tuple-element., ...), custom_call_target="tpu_custom_call" | custom-call | tf_op jit(solution)/shard_map/weight_grads/pallas_call | solution.py:568

commit v12 on v11

--- a/solution.py
+++ b/solution.py
@@ -61,6 +61,7 @@
     far = {'tx': lax.rem(tx + 1 - 2 * core + 2, 4)}
     other_ty = {'ty': 1 - ty}
     peers = [near, across, far, other_ty] + [{'tx': p['tx'], 'ty': 1 - ty} for p in (near, across, far)]
+    close = peers[:5]
     n_tok = x_v.shape[0]
     half = n_tok // 2
     mine = pl.multiple_of(core * half, half)
@@ -75,7 +76,7 @@
     loads = [
         load(0, dy_hbm.at[pl.ds(mine, half)], dy_v.at[0:half]),
         load(1, dy_hbm.at[pl.ds(other, half)], dy_v.at[half:n_tok]),
-        load(2, wo_hbm.at[0:BLK], wo_v.at[0:BLK]),
+        load(2, wo_hbm.at[0:EARLY], wo_v.at[0:EARLY]),
         load(3, x_hbm.at[pl.ds(mine, half)], x_v.at[0:half]),
         load(4, x_hbm.at[pl.ds(other, half)], x_v.at[half:n_tok]),
         load(5, wd_hbm.at[0:CHUNK], wd_v.at[0:CHUNK]),
@@ -89,12 +90,13 @@
         load(13, pos_hbm, pos_ref),
         load(14, freq_hbm, freq_ref),
         load(15, wo_hbm.at[BLK:q_width], wo_v.at[BLK:q_width]),
+        load(16, wo_hbm.at[EARLY:BLK], wo_v.at[EARLY:BLK]),
     ]
-    for i in (0, 1, 2, 15, 3, 4, 5):
+    for i in (0, 1, 2, 16, 15, 3, 4, 5):
         loads[i].start()
 
     barrier = pltpu.get_barrier_semaphore()
-    for peer in peers:
+    for peer in close:
         pl.semaphore_signal(barrier, inc=1, device_id=peer, device_id_type=MESH)
     for ld in loads[:3]:
         ld.wait()
@@ -138,16 +140,14 @@
     def total(b):
         return chip[b].astype(F32) + rx[b].astype(F32)
 
-    part = mm_bt(dy_v[...], wo_v[0:BLK, :])
-    keep[0] = part[:half]
-    send[0] = part[half:].astype(BF16)
-    early_snd[...] = part[:, 0:EARLY].astype(BF16)
-    pl.semaphore_wait(barrier, len(peers))
+    early_snd[...] = mm_bt(dy_v[...], wo_v[0:EARLY, :]).astype(BF16)
+    pl.semaphore_wait(barrier, len(close))
     early = [remote(early_snd.at[0:half], early_rx.at[0], es.at[0], er.at[0], across),
              remote(early_snd.at[half:n_tok], early_rx.at[1], es.at[1], er.at[1], far)]
-    core_copy(0).start()
     for copy in early:
         copy.start()
+    loads[16].wait()
+    issue_bwd(0, wo_v, 0)
     loads[15].wait()
     issue_bwd(1, wo_v, BLK)
 
@@ -558,7 +558,7 @@
                 vm(tok, F32), vm((n_tok, 128), F32), vm((n_tok, 128), F32), vm((n_tok, 128), F32), vm(tok, F32), vm(tok, F32),
                 vm(tok, BF16), vm(tok, BF16), vm(tok, BF16), vm(tok, BF16),
                 vm((8, n_tok), F32), vm((3, 8, n_tok), F32), vm((8, n_tok), F32), vm((8, n_tok), F32), vm((7, 8, n_tok), F32), vm((2, half, CHUNK), F32),
-                sem((16,)), sem((N_BLK,)), sem((N_BLK,)), sem((N_X,)), sem((N_X,)),
+                sem((17,)), sem((N_BLK,)), sem((N_BLK,)), sem((N_X,)), sem((N_X,)),
                 sem((12 + SPLITS,)), sem((12 + SPLITS,)), sem((1,)), sem((1,)), sem((4,)), sem((4,)), sem((10,)), sem((10,)),
                 sem((SPLITS,)), sem((SPLITS,)), vm((n_tok, EARLY), BF16), vm((2, half, EARLY), BF16), sem((2,)), sem((2,))],
             compiler_params=pltpu.CompilerParams(collective_id=0, has_side_effects=True, vmem_limit_bytes=46 * 1024 * 1024),

time: 107 us -> 107 us (level)
  no operation moved by 1% of the time
where the time goes in v12:
time: 107 us
  Pallas kernels  106 us (99%)
    pallas_call x1, Pallas kernels, local_layer(): pl.pallas_call(functools.partial(layer_kernel, d_model), out_shape=[vm(to...  95.5 us
    pallas_call x1, Pallas kernels, local_layer(): pl.pallas_call(grad_kernel, out_shape=[jax.ShapeDtypeStruct(tok, BF16), j...  10.4 us

profile of v12, /device:TPU:0, one launch (start us, length us, event | category | flops | bytes accessed | tf_op | source)
XLA Modules:
  0.0 106.7 jit_solution(12934072438713558228)
XLA Ops:
  0.6 95.5 %layer.1 = (bf16[256,512]{1,0:T(8,128)(2,1)S(1)}, bf16[256,512]{1,0:T(8,128)(2,1)S(1)}, f32[1,512]{1,0:T(1,128)S(1)}, bf16[512,256]{1,0:T(8,128)(2,1)S(1)}, bf16...) custom-call(bf16[256,512]{1,0:T(8,128)(2,1)} %bitcast.6, ...), custom_call_target="tpu_custom_call" | custom-call | tf_op jit(solution)/shard_map/layer/pallas_call | solution.py:544
  96.1 10.4 %weight_grads.1 = (bf16[256,512]{1,0:T(8,128)(2,1)}, bf16[256,512]{1,0:T(8,128)(2,1)}, f32[1,512]{1,0:T(1,128)}, f32[512,1024]{1,0:T(8,128)}, f32[512,4096]{1,0:...) custom-call(bf16[256,512]{1,0:T(8,128)(2,1)S(1)} %get-tuple-element., ...), custom_call_target="tpu_custom_call" | custom-call | tf_op jit(solution)/shard_map/weight_grads/pallas_call | solution.py:568

commit v13 on v12

--- a/solution.py
+++ b/solution.py
@@ -344,9 +344,9 @@
                 cols = slice(j * BLK, (j + 1) * BLK)
                 if want_act:
                     md[k, 0, rows, cols] = (silu * up).astype(BF16)
-                if k == 3:
-                    factors[0, rows, cols] = up * sig * (1.0 + gate * (1.0 - sig))
-                    factors[1, rows, cols] = silu
+                if k >= 2:
+                    factors[k - 2, 0, rows, cols] = up * sig * (1.0 + gate * (1.0 - sig))
+                    factors[k - 2, 1, rows, cols] = silu
                 if want_grad:
                     d_act = (chip[bd, rows].astype(F32) + rx[bd, rows].astype(F32)).astype(BF16).astype(F32)
                     md[k, 1, rows, cols] = (d_act * up * sig * (1.0 + gate * (1.0 - sig))).astype(BF16)
@@ -392,7 +392,22 @@
     gated(1, False, True)
     use_grad(1)
     x_copy(9).wait_recv()
-    gated(2, False, True)
+
+    def scaled(k, rows):
+        for j in range(2):
+            cols = slice(j * BLK, (j + 1) * BLK)
+            b = dact_block(k, j)
+            d_act = (chip[b, rows].astype(F32) + rx[b, rows].astype(F32)).astype(BF16).astype(F32)
+            for i in range(2):
+                md[k, 1 + i, rows, cols] = (d_act * factors[k - 2, i, rows, cols]).astype(BF16)
+
+    def scaled_step(r, carry):
+        scaled(2, pl.ds(pl.multiple_of(r * 32, 32), 32))
+        return carry
+
+    lax.fori_loop(0, half // 32, scaled_step, 0)
+    for i in (1, 2):
+        gather_copy(2, i).start()
 
     def dh_copy(r):
         at = pl.ds(2 * PIECES[r][0], 2 * PIECES[r][1])
@@ -406,13 +421,7 @@
 
     def piece_grad(r):
         x_copy(X_LAST + r).wait_recv()
-        rows = slice(PIECES[r][0], PIECES[r][0] + PIECES[r][1])
-        for j in range(2):
-            cols = slice(j * BLK, (j + 1) * BLK)
-            b = dact_block(3, j)
-            d_act = (chip[b, rows].astype(F32) + rx[b, rows].astype(F32)).astype(BF16).astype(F32)
-            for i in range(2):
-                md[3, 1 + i, rows, cols] = (d_act * factors[i, rows, cols]).astype(BF16)
+        scaled(3, slice(PIECES[r][0], PIECES[r][0] + PIECES[r][1]))
         piece_copy(r).start()
 
     def piece_dh(r):
@@ -498,11 +507,11 @@
     ready = [(tiles.at[i], dst) for i, dst in ready] + [(tiles.at[4, :, 0:256], dwk_hbm), (tiles.at[4, :, 256:512], dwv_hbm)]
     for i, (src, dst) in enumerate(ready):
         hand_out.append(pltpu.make_async_copy(src, dst, cp_sem.at[4 + i]))
-        hand_out[-1].start()
+        hand_out[-1].start(priority=len(hand_out) % 2)
 
     def put(src, dst, i):
         hand_out.append(pltpu.make_async_copy(src, dst, out_sem.at[i]))
-        hand_out[-1].start()
+        hand_out[-1].start(priority=len(hand_out) % 2)
 
     for t in range(6):
         k, j = 1 + t // 2, t % 2
@@ -557,11 +566,11 @@
                 vm((n_tok, 512), BF16), vm((n_tok, 512), BF16), vm((n_tok, 512), F32),
                 vm(tok, F32), vm((n_tok, 128), F32), vm((n_tok, 128), F32), vm((n_tok, 128), F32), vm(tok, F32), vm(tok, F32),
                 vm(tok, BF16), vm(tok, BF16), vm(tok, BF16), vm(tok, BF16),
-                vm((8, n_tok), F32), vm((3, 8, n_tok), F32), vm((8, n_tok), F32), vm((8, n_tok), F32), vm((7, 8, n_tok), F32), vm((2, half, CHUNK), F32),
+                vm((8, n_tok), F32), vm((3, 8, n_tok), F32), vm((8, n_tok), F32), vm((8, n_tok), F32), vm((7, 8, n_tok), F32), vm((2, 2, half, CHUNK), F32),
                 sem((17,)), sem((N_BLK,)), sem((N_BLK,)), sem((N_X,)), sem((N_X,)),
                 sem((12 + SPLITS,)), sem((12 + SPLITS,)), sem((1,)), sem((1,)), sem((4,)), sem((4,)), sem((10,)), sem((10,)),
                 sem((SPLITS,)), sem((SPLITS,)), vm((n_tok, EARLY), BF16), vm((2, half, EARLY), BF16), sem((2,)), sem((2,))],
-            compiler_params=pltpu.CompilerParams(collective_id=0, has_side_effects=True, vmem_limit_bytes=46 * 1024 * 1024),
+            compiler_params=pltpu.CompilerParams(collective_id=0, has_side_effects=True, vmem_limit_bytes=47 * 1024 * 1024),
             name='layer',
         )(x_in.reshape(tok), positions, freq, d_y.reshape(tok), ln_gamma[None], w_q, w_g, w_u, w_k, w_v, w_o, w_d)
 

time: 107 us -> 106 us (level)
  no operation moved by 1% of the time
where the time goes in v13:
time: 106 us
  Pallas kernels  106 us (100%)
    pallas_call x1, Pallas kernels, local_layer(): pl.pallas_call(functools.partial(layer_kernel, d_model), out_shape=[vm(to...  95.2 us
    pallas_call x1, Pallas kernels, local_layer(): pl.pallas_call(grad_kernel, out_shape=[jax.ShapeDtypeStruct(tok, BF16), j...  10.4 us

profile of v13, /device:TPU:0, one launch (start us, length us, event | category | flops | bytes accessed | tf_op | source)
XLA Modules:
  0.0 106.4 jit_solution(18433363134109106401)
XLA Ops:
  0.6 95.2 %layer.1 = (bf16[256,512]{1,0:T(8,128)(2,1)S(1)}, bf16[256,512]{1,0:T(8,128)(2,1)S(1)}, f32[1,512]{1,0:T(1,128)S(1)}, bf16[512,256]{1,0:T(8,128)(2,1)S(1)}, bf16...) custom-call(bf16[256,512]{1,0:T(8,128)(2,1)} %bitcast.6, ...), custom_call_target="tpu_custom_call" | custom-call | tf_op jit(solution)/shard_map/layer/pallas_call | solution.py:553
  95.8 10.4 %weight_grads.1 = (bf16[256,512]{1,0:T(8,128)(2,1)}, bf16[256,512]{1,0:T(8,128)(2,1)}, f32[1,512]{1,0:T(1,128)}, f32[512,1024]{1,0:T(8,128)}, f32[512,4096]{1,0:...) custom-call(bf16[256,512]{1,0:T(8,128)(2,1)S(1)} %get-tuple-element., ...), custom_call_target="tpu_custom_call" | custom-call | tf_op jit(solution)/shard_map/weight_grads/pallas_call | solution.py:577

commit v14 on v13

--- a/solution.py
+++ b/solution.py
@@ -18,7 +18,7 @@
 CHUNK = 1024
 B_DATTN, B_DACT_LO, B_QKV, B_GU, B_DACT_HI, N_BLK = 0, 2, 4, 7, 23, 29
 X_UNITS = ((0, 1), (1, 1), (2, 2), (4, 2), (7, 4), (11, 4), (15, 4), (19, 4), (23, 2), (25, 2))
-PIECES = ((0, 16), (16, 32), (48, 32), (80, 32), (112, 16))
+PIECES = ((0, 32), (32, 32), (64, 32), (96, 32))
 SPLITS = len(PIECES)
 EARLY = 128
 X_KV = len(X_UNITS)
@@ -435,7 +435,9 @@
 
     piece_grad(0)
     use_grad(2)
-    for r in range(1, SPLITS):
+    piece_dh(0)
+    piece_grad(1)
+    for r in range(2, SPLITS):
         piece_grad(r)
         piece_dh(r - 1)
     piece_dh(SPLITS - 1)
@@ -517,7 +519,7 @@
         k, j = 1 + t // 2, t % 2
         ring[t] = mm_at(md[k, 0, :, j * BLK:(j + 1) * BLK], dy_v[...])
         put(ring.at[t], dwd_hbm.at[k * CHUNK + j * BLK:k * CHUNK + (j + 1) * BLK, :], t)
-    n_row = 128
+    n_row = 256
     for i, (out, at) in enumerate(((dwg_hbm, 6), (dwu_hbm, 10))):
         for k in range(4):
             for j in range(2):

time: 106 us -> 107 us (level)
  no operation moved by 1% of the time
where the time goes in v14:
time: 107 us
  Pallas kernels  106 us (99%)
    pallas_call x1, Pallas kernels, local_layer(): pl.pallas_call(functools.partial(layer_kernel, d_model), out_shape=[vm(to...  95.4 us
    pallas_call x1, Pallas kernels, local_layer(): pl.pallas_call(grad_kernel, out_shape=[jax.ShapeDtypeStruct(tok, BF16), j...  10.4 us

profile of v14, /device:TPU:0, one launch (start us, length us, event | category | flops | bytes accessed | tf_op | source)
XLA Modules:
  0.0 106.6 jit_solution(10842459843033460428)
XLA Ops:
  0.6 95.4 %layer.1 = (bf16[256,512]{1,0:T(8,128)(2,1)S(1)}, bf16[256,512]{1,0:T(8,128)(2,1)S(1)}, f32[1,512]{1,0:T(1,128)S(1)}, bf16[512,256]{1,0:T(8,128)(2,1)S(1)}, bf16...) custom-call(bf16[256,512]{1,0:T(8,128)(2,1)} %bitcast.6, ...), custom_call_target="tpu_custom_call" | custom-call | tf_op jit(solution)/shard_map/layer/pallas_call | solution.py:555
  96.0 10.4 %weight_grads.1 = (bf16[256,512]{1,0:T(8,128)(2,1)}, bf16[256,512]{1,0:T(8,128)(2,1)}, f32[1,512]{1,0:T(1,128)}, f32[512,1024]{1,0:T(8,128)}, f32[512,4096]{1,0:...) custom-call(bf16[256,512]{1,0:T(8,128)(2,1)S(1)} %get-tuple-element., ...), custom_call_target="tpu_custom_call" | custom-call | tf_op jit(solution)/shard_map/weight_grads/pallas_call | solution.py:579

commit v15 on v13

--- a/solution.py
+++ b/solution.py
@@ -393,21 +393,21 @@
     use_grad(1)
     x_copy(9).wait_recv()
 
-    def scaled(k, rows):
+    def scaled(k, rows, which=(0, 1)):
         for j in range(2):
             cols = slice(j * BLK, (j + 1) * BLK)
             b = dact_block(k, j)
             d_act = (chip[b, rows].astype(F32) + rx[b, rows].astype(F32)).astype(BF16).astype(F32)
-            for i in range(2):
+            for i in which:
                 md[k, 1 + i, rows, cols] = (d_act * factors[k - 2, i, rows, cols]).astype(BF16)
 
-    def scaled_step(r, carry):
-        scaled(2, pl.ds(pl.multiple_of(r * 32, 32), 32))
-        return carry
-
-    lax.fori_loop(0, half // 32, scaled_step, 0)
-    for i in (1, 2):
-        gather_copy(2, i).start()
+    for i in range(2):
+        def scaled_step(r, carry, i=i):
+            scaled(2, pl.ds(pl.multiple_of(r * 32, 32), 32), (i,))
+            return carry
+
+        lax.fori_loop(0, half // 32, scaled_step, 0)
+        gather_copy(2, 1 + i).start()
 
     def dh_copy(r):
         at = pl.ds(2 * PIECES[r][0], 2 * PIECES[r][1])
@@ -434,7 +434,9 @@
         sums.append((jnp.sum(d_hat, axis=1, keepdims=True), jnp.sum(d_hat * both(xhat_v, r), axis=1, keepdims=True)))
 
     piece_grad(0)
-    use_grad(2)
+    for i, weight in ((1, wg_v), (2, wu_v)):
+        gather_copy(2, i).wait_recv()
+        dh_v[...] += mm_bt(md[2, i], weight[:, 2 * CHUNK:3 * CHUNK])
     for r in range(1, SPLITS):
         piece_grad(r)
         piece_dh(r - 1)

time: 106 us -> 106 us (level)
  no operation moved by 1% of the time
where the time goes in v15:
time: 106 us
  Pallas kernels  106 us (100%)
    pallas_call x1, Pallas kernels, local_layer(): pl.pallas_call(functools.partial(layer_kernel, d_model), out_shape=[vm(to...  95.1 us
    pallas_call x1, Pallas kernels, local_layer(): pl.pallas_call(grad_kernel, out_shape=[jax.ShapeDtypeStruct(tok, BF16), j...  10.4 us

profile of v15, /device:TPU:0, one launch (start us, length us, event | category | flops | bytes accessed | tf_op | source)
XLA Modules:
  0.0 106.3 jit_solution(8990216330671838004)
XLA Ops:
  0.6 95.1 %layer.1 = (bf16[256,512]{1,0:T(8,128)(2,1)S(1)}, bf16[256,512]{1,0:T(8,128)(2,1)S(1)}, f32[1,512]{1,0:T(1,128)S(1)}, bf16[512,256]{1,0:T(8,128)(2,1)S(1)}, bf16...) custom-call(bf16[256,512]{1,0:T(8,128)(2,1)} %bitcast.6, ...), custom_call_target="tpu_custom_call" | custom-call | tf_op jit(solution)/shard_map/layer/pallas_call | solution.py:555
  95.8 10.4 %weight_grads.1 = (bf16[256,512]{1,0:T(8,128)(2,1)}, bf16[256,512]{1,0:T(8,128)(2,1)}, f32[1,512]{1,0:T(1,128)}, f32[512,1024]{1,0:T(8,128)}, f32[512,4096]{1,0:...) custom-call(bf16[256,512]{1,0:T(8,128)(2,1)S(1)} %get-tuple-element., ...), custom_call_target="tpu_custom_call" | custom-call | tf_op jit(solution)/shard_map/weight_grads/pallas_call | solution.py:579
